TPU v7x, 32 devices: a whole 2x2x4 slice. The times are simulated.
32 devices in a mesh: fsdp: 4 (over z), seq: 8 (over y, x, core).
Axes of the slice: x: 2, y: 2, z: 4, core: 2. Of those that a mesh axis runs over, the one named last changes fastest.
Arguments:
- tokens: bfloat16 [8, 1024, 2048], P('fsdp', 'seq'), may hold values from -6 to 6
- cotangent: bfloat16 [8, 1024, 2048], P('fsdp', 'seq'), may hold values from -6 to 6
- gain_first: bfloat16 [2048], P('fsdp'), may hold values from 0.5 to 1.5
- w_inputs: bfloat16 [3, 2048, 2048], P(None, 'fsdp'), may hold values from -0.125 to 0.125
- w_conv: bfloat16 [3, 4, 2048], P(None, None, 'fsdp'), may hold values from -3 to 3
- w_beta: bfloat16 [2048, 16], P('fsdp'), may hold values from -0.125 to 0.125
- gain_heads: bfloat16 [128], P('fsdp'), may hold values from 0.5 to 1.5
- w_output: bfloat16 [2048, 2048], P('fsdp'), may hold values from -0.125 to 0.125
- gain_second: bfloat16 [2048], P('fsdp'), may hold values from 0.5 to 1.5
- w_gate_up: bfloat16 [2, 2048, 5632], P(None, 'fsdp'), may hold values from -0.125 to 0.125
- w_down: bfloat16 [5632, 2048], P('fsdp'), may hold values from -0.078125 to 0.078125
Outputs:
- output: bfloat16 [8, 1024, 2048], P('fsdp', 'seq')
- input_grad: float32 [8, 1024, 2048], P('fsdp', 'seq')
- grad_gain_first: float32 [2048], P('fsdp')
- grad_w_inputs: float32 [3, 2048, 2048], P(None, 'fsdp')
- grad_w_conv: float32 [3, 4, 2048], P(None, None, 'fsdp')
- grad_w_beta: float32 [2048, 16], P('fsdp')
- grad_gain_heads: float32 [128], P('fsdp')
- grad_w_output: float32 [2048, 2048], P('fsdp')
- grad_gain_second: float32 [2048], P('fsdp')
- grad_w_gate_up: float32 [2, 2048, 5632], P(None, 'fsdp')
- grad_w_down: float32 [5632, 2048], P('fsdp')
All inputs are finite; a program needn't handle non-finite values.
Results may differ from a plain program's by a relative error of at most 0.024.
Values may be sent and summed in bfloat16 or wider, within the bound.
No kernel may reach another device: no remote copies, remote signals or barrier semaphores. Data moves between devices by JAX's collectives and lax.ppermute only.
A program may use at most 704 MiB of HBM per device.

v0:
```python
import jax
import jax.numpy as jnp
from jax import lax
from jax.sharding import PartitionSpec as P

BLOCK = 64


highest = lax.Precision.HIGHEST


def from_behind(block, axis, distance):
    devices = range(lax.axis_size(axis))
    route = [(i - distance, i) for i in devices if i - distance in devices]
    return lax.ppermute(block, axis, route)


def carried_in(x, axis, join, neutral):
    place = lax.axis_index(axis)
    gathered = jax.tree.map(
        lambda a, kind: lax.all_gather(a.astype(kind), axis), x, (jnp.bfloat16, jnp.bfloat16)
    )
    state = jax.tree.map(lambda a, e: jnp.zeros_like(a) + jnp.asarray(e, a.dtype), x, neutral)

    def carried_one(step, state):
        return join(
            state,
            jax.tree.map(
                lambda a, own: lax.dynamic_index_in_dim(a, step, 0, False).astype(own.dtype),
                gathered,
                x,
            ),
        )

    return lax.fori_loop(0, place, carried_one, state)


def prefix(x, axis, join, neutral):
    count = lax.axis_size(axis)
    place = lax.axis_index(axis)
    ahead = count - 1 - place
    gathered = jax.tree.map(
        lambda a, kind: lax.all_gather(a.astype(kind), axis),
        x,
        jax.tree.map(lambda a: jnp.bfloat16 if a.dtype == jnp.float32 else a.dtype, x),
    )
    state = jax.tree.map(lambda a, e: jnp.zeros_like(a) + jnp.asarray(e, a.dtype), x, neutral)

    def prefix_one(step, state):
        source = count - 1 - step
        return join(
            state,
            jax.tree.map(
                lambda a, own: lax.dynamic_index_in_dim(a, source, 0, False).astype(own.dtype),
                gathered,
                x,
            ),
        )

    return lax.fori_loop(0, ahead, prefix_one, state)


def contract(pattern, left_op, right_op):
    return jnp.einsum(pattern, left_op, right_op, precision=highest)


def compose(earlier_map, later_map):
    return (
        contract("bhij,bhjk->bhik", later_map[0], earlier_map[0]),
        contract("bhij,bhjk->bhik", later_map[0], earlier_map[1]) + later_map[1],
    )


def block_step(carried, block_in):
    state, transit = carried
    queries, key_rows, value_rows, strength = block_in
    block_len = key_rows.shape[-2]
    gram_mat = contract("bhck,bhdk->bhcd", key_rows, key_rows)
    lower_mat = jnp.eye(block_len, dtype=jnp.float32) + jnp.tril(
        strength[..., :, None] * gram_mat, -1
    )
    w_rows = lax.linalg.triangular_solve(
        lower_mat, strength[..., None] * key_rows, left_side=True, lower=True, unit_diagonal=True
    )
    u_rows = lax.linalg.triangular_solve(
        lower_mat, strength[..., None] * value_rows, left_side=True, lower=True, unit_diagonal=True
    )
    fresh_values = u_rows - contract("bhck,bhkv->bhcv", w_rows, state)
    scores = jnp.tril(contract("bhck,bhdk->bhcd", queries, key_rows))
    mixed = contract("bhck,bhkv->bhcv", queries, state) + contract(
        "bhcd,bhdv->bhcv", scores, fresh_values
    )
    state = state + contract("bhck,bhcv->bhkv", key_rows, fresh_values)
    transit = transit - contract(
        "bhck,bhcj->bhkj", key_rows, contract("bhck,bhkj->bhcj", w_rows, transit)
    )
    return ((state, transit), mixed)


def local_pass(queries, key_rows, value_rows, strength, start_state):
    seq_count, length, head_count, head_dim = queries.shape

    def blocked(values):
        return values.reshape(seq_count, length // BLOCK, BLOCK, head_count, head_dim).transpose(
            1, 0, 3, 2, 4
        )

    strength_b = strength.reshape(seq_count, length // BLOCK, BLOCK, head_count).transpose(
        1, 0, 3, 2
    )
    identity = jnp.broadcast_to(jnp.eye(head_dim, dtype=jnp.float32), start_state.shape)
    carried, mixed_blocks = lax.scan(
        block_step,
        (start_state, identity),
        (blocked(queries), blocked(key_rows), blocked(value_rows), strength_b),
    )
    mixed = mixed_blocks.transpose(1, 0, 3, 2, 4).reshape(seq_count, length, head_count, head_dim)
    return (mixed, carried[0], carried[1])


def rule_only(queries, key_rows, value_rows, strength, start_state):
    mixed, end_state, transit = local_pass(queries, key_rows, value_rows, strength, start_state)
    return (mixed, end_state)


def norm_back(values, scale, grad_normed, gain):
    weighted = grad_normed * gain
    return scale * weighted - values * scale**3 * jnp.mean(
        values * weighted, axis=-1, keepdims=True
    )


def unit_back(values, grad_unit, factor):
    scaled = grad_unit * factor
    rho_scale = lax.rsqrt(jnp.sum(values * values, axis=-1, keepdims=True) + 1e-06)
    return rho_scale * scaled - values * rho_scale**3 * jnp.sum(
        values * scaled, axis=-1, keepdims=True
    )


def local(
    tokens,
    cotangent,
    gain_first,
    w_inputs,
    w_conv,
    w_beta,
    gain_heads,
    w_output,
    gain_second,
    w_gate_up,
    w_down,
):
    first_gain, input_mats, conv_taps, beta_mat, head_gain, output_mat = (
        lax.all_gather(gain_first, "fsdp", axis=0, tiled=True),
        lax.all_gather(w_inputs, "fsdp", axis=1, tiled=True),
        lax.all_gather(w_conv, "fsdp", axis=2, tiled=True),
        lax.all_gather(w_beta, "fsdp", axis=0, tiled=True),
        lax.all_gather(gain_heads, "fsdp", axis=0, tiled=True),
        lax.all_gather(w_output, "fsdp", axis=0, tiled=True),
    )
    seq_count, length, model_width = tokens.shape
    row_count = seq_count * length
    head_count = beta_mat.shape[1]
    head_dim = head_gain.shape[0]
    tap_count = conv_taps.shape[1]
    inputs = tokens.astype(jnp.float32)
    first_scale = lax.rsqrt(jnp.mean(inputs * inputs, axis=-1, keepdims=True) + 1e-05)
    first_weight = first_gain.astype(jnp.float32)
    normed = (inputs * first_scale * first_weight).astype(jnp.bfloat16)
    project = jnp.einsum(
        "bld,cde->cble", normed, input_mats, preferred_element_type=jnp.float32
    ).astype(jnp.bfloat16)
    before = from_behind(project[:, :, length - (tap_count - 1) :, :], "seq", 1)
    padded = jnp.concatenate([before, project], axis=2).astype(jnp.float32)
    tap_weights = conv_taps.astype(jnp.float32)
    conved = jnp.zeros(project.shape, jnp.float32)
    for offset in range(tap_count):
        conved = (
            conved
            + tap_weights[:, offset, None, None, :] * padded[:, :, offset : offset + length, :]
        )
    conv_sigmoid = jax.nn.sigmoid(conved)
    active = conved * conv_sigmoid
    pieces = active.reshape(3, seq_count, length, head_count, head_dim)
    query_factor = head_dim ** (-0.5)
    queries = (
        pieces[0]
        * lax.rsqrt(jnp.sum(pieces[0] * pieces[0], axis=-1, keepdims=True) + 1e-06)
        * query_factor
    ).astype(jnp.bfloat16)
    key_rows = (
        pieces[1] * lax.rsqrt(jnp.sum(pieces[1] * pieces[1], axis=-1, keepdims=True) + 1e-06)
    ).astype(jnp.bfloat16)
    value_rows = pieces[2].astype(jnp.bfloat16)
    strength = jax.nn.sigmoid(
        jnp.einsum("bld,dh->blh", normed, beta_mat, preferred_element_type=jnp.float32)
    )
    query_wide = queries.astype(jnp.float32)
    key_wide = key_rows.astype(jnp.float32)
    value_wide = value_rows.astype(jnp.float32)
    zeros_state = jnp.zeros((seq_count, head_count, head_dim, head_dim), jnp.float32)
    unused_mixed, end_states, transit = local_pass(
        query_wide, key_wide, value_wide, strength, zeros_state
    )
    identity = jnp.broadcast_to(jnp.eye(head_dim, dtype=jnp.float32), transit.shape)
    unused_map, start_state = carried_in(
        (transit, end_states), "seq", compose, (identity, zeros_state)
    )
    (mixed, unused_end), pull_rule = jax.vjp(
        rule_only, query_wide, key_wide, value_wide, strength, start_state
    )
    head_scale = lax.rsqrt(jnp.mean(mixed * mixed, axis=-1, keepdims=True) + 1e-05)
    head_weight = head_gain.astype(jnp.float32)
    normed_out = (
        (mixed * head_scale * head_weight)
        .reshape(seq_count, length, head_count * head_dim)
        .astype(jnp.bfloat16)
    )
    hidden = inputs + jnp.einsum(
        "ble,ed->bld", normed_out, output_mat, preferred_element_type=jnp.float32
    )
    second_gain, gate_up_mats, down_mat = (
        lax.all_gather(gain_second, "fsdp", axis=0, tiled=True),
        lax.all_gather(w_gate_up, "fsdp", axis=1, tiled=True),
        lax.all_gather(w_down, "fsdp", axis=0, tiled=True),
    )
    second_scale = lax.rsqrt(jnp.mean(hidden * hidden, axis=-1, keepdims=True) + 1e-05)
    second_weight = second_gain.astype(jnp.float32)
    normed_two = (hidden * second_scale * second_weight).astype(jnp.bfloat16)
    gate_up = jnp.einsum(
        "bld,cdf->cblf", normed_two, gate_up_mats, preferred_element_type=jnp.float32
    )
    sigmoid_gate = jax.nn.sigmoid(gate_up[0])
    swish_gate = gate_up[0] * sigmoid_gate
    inner_act = (swish_gate * gate_up[1]).astype(jnp.bfloat16)
    result = hidden + jnp.einsum(
        "blf,fd->bld", inner_act, down_mat, preferred_element_type=jnp.float32
    )
    output = result.astype(jnp.bfloat16)
    slice_two, slice_inner, slice_first, slice_out = (
        lax.all_to_all(
            normed_two.reshape(row_count, -1), "fsdp", split_axis=1, concat_axis=0, tiled=True
        ),
        lax.all_to_all(
            inner_act.reshape(row_count, -1), "fsdp", split_axis=1, concat_axis=0, tiled=True
        ),
        lax.all_to_all(
            normed.reshape(row_count, -1), "fsdp", split_axis=1, concat_axis=0, tiled=True
        ),
        lax.all_to_all(
            normed_out.reshape(row_count, -1), "fsdp", split_axis=1, concat_axis=0, tiled=True
        ),
    )
    grad_inner = jnp.einsum("bld,fd->blf", cotangent, down_mat, preferred_element_type=jnp.float32)
    slope_gate = sigmoid_gate * (1.0 + gate_up[0] * (1.0 - sigmoid_gate))
    grad_gate_up = jnp.stack(
        [grad_inner * gate_up[1] * slope_gate, grad_inner * swish_gate], axis=2
    ).astype(jnp.bfloat16)
    grad_normed_two = jnp.einsum(
        "blcf,cdf->bld", grad_gate_up, gate_up_mats, preferred_element_type=jnp.float32
    )
    grad_hidden = cotangent.astype(jnp.float32) + norm_back(
        hidden, second_scale, grad_normed_two, second_weight
    )
    grad_second = jnp.sum(grad_normed_two * hidden * second_scale, axis=(0, 1))
    pieces_in = (
        lax.all_gather(cotangent.reshape(row_count, -1), "fsdp", axis=0, tiled=True),
        lax.all_gather(grad_gate_up.reshape(row_count, -1), "fsdp", axis=0, tiled=True),
    )
    count = pieces_in[0].shape[0]
    down_part = jnp.einsum(
        "rf,rd->fd", slice_inner, pieces_in[0], preferred_element_type=jnp.float32
    )
    gu_part = jnp.einsum(
        "rd,rcf->cdf",
        slice_two,
        pieces_in[1].reshape(count, 2, -1),
        preferred_element_type=jnp.float32,
    )
    grad_branch = grad_hidden.astype(jnp.bfloat16)
    grad_normed_out = jnp.einsum(
        "bld,ed->ble", grad_branch, output_mat, preferred_element_type=jnp.float32
    )
    grad_normed_out = grad_normed_out.reshape(seq_count, length, head_count, head_dim)
    grad_head_gain = jnp.sum(grad_normed_out * mixed * head_scale, axis=(0, 1, 2))
    grad_mixed = norm_back(mixed, head_scale, grad_normed_out, head_weight)
    own_grads = pull_rule((grad_mixed, zeros_state))
    flipped = jnp.swapaxes(transit, -1, -2)
    unused_back, end_grad = prefix((flipped, own_grads[4]), "seq", compose, (identity, zeros_state))
    late_grads = pull_rule((jnp.zeros_like(grad_mixed), end_grad))
    grad_query = own_grads[0] + late_grads[0]
    grad_key = own_grads[1] + late_grads[1]
    grad_value = own_grads[2] + late_grads[2]
    grad_strength = own_grads[3] + late_grads[3]
    grad_logit = (grad_strength * strength * (1.0 - strength)).astype(jnp.bfloat16)
    grad_active = jnp.stack(
        [
            unit_back(pieces[0], grad_query, query_factor),
            unit_back(pieces[1], grad_key, 1.0),
            grad_value,
        ]
    ).reshape(project.shape)
    grad_conved = grad_active * conv_sigmoid * (1.0 + conved * (1.0 - conv_sigmoid))
    grad_taps = jnp.stack(
        [
            jnp.sum(grad_conved * padded[:, :, offset : offset + length, :], axis=(1, 2))
            for offset in range(tap_count)
        ],
        axis=1,
    )
    grad_padded = jnp.zeros(padded.shape, jnp.float32)
    for offset in range(tap_count):
        grad_padded = grad_padded + jnp.pad(
            tap_weights[:, offset, None, None, :] * grad_conved,
            ((0, 0), (0, 0), (offset, tap_count - 1 - offset), (0, 0)),
        )
    returned = from_behind(
        grad_padded[:, :, : tap_count - 1, :].astype(jnp.bfloat16), "seq", -1
    ).astype(jnp.float32)
    own_part = grad_padded[:, :, tap_count - 1 :, :]
    grad_project = jnp.concatenate(
        [
            own_part[:, :, : length - (tap_count - 1), :],
            own_part[:, :, length - (tap_count - 1) :, :] + returned,
        ],
        axis=2,
    ).astype(jnp.bfloat16)
    grad_normed = jnp.einsum(
        "cble,cde->bld", grad_project, input_mats, preferred_element_type=jnp.float32
    )
    grad_normed = grad_normed + jnp.einsum(
        "blh,dh->bld", grad_logit, beta_mat, preferred_element_type=jnp.float32
    )
    input_grad = grad_hidden + norm_back(inputs, first_scale, grad_normed, first_weight)
    grad_first = jnp.sum(grad_normed * inputs * first_scale, axis=(0, 1))
    project_rows = grad_project.transpose(1, 2, 0, 3).reshape(row_count, -1)
    pieces_in = (
        lax.all_gather(grad_branch.reshape(row_count, -1), "fsdp", axis=0, tiled=True),
        lax.all_gather(project_rows, "fsdp", axis=0, tiled=True),
        lax.all_gather(grad_logit.reshape(row_count, -1), "fsdp", axis=0, tiled=True),
    )
    count = pieces_in[0].shape[0]
    out_part = jnp.einsum("re,rd->ed", slice_out, pieces_in[0], preferred_element_type=jnp.float32)
    in_part = jnp.einsum(
        "rd,rce->cde",
        slice_first,
        pieces_in[1].reshape(count, 3, -1),
        preferred_element_type=jnp.float32,
    )
    beta_part = jnp.einsum(
        "rd,rh->dh", slice_first, pieces_in[2], preferred_element_type=jnp.float32
    )
    part_first, part_conv, part_heads, part_second = (
        lax.psum_scatter(
            grad_first.astype(jnp.bfloat16), "fsdp", scatter_dimension=0, tiled=True
        ).astype(jnp.float32),
        lax.psum_scatter(
            grad_taps.astype(jnp.bfloat16), "fsdp", scatter_dimension=2, tiled=True
        ).astype(jnp.float32),
        lax.psum_scatter(
            grad_head_gain.astype(jnp.bfloat16), "fsdp", scatter_dimension=0, tiled=True
        ).astype(jnp.float32),
        lax.psum_scatter(
            grad_second.astype(jnp.bfloat16), "fsdp", scatter_dimension=0, tiled=True
        ).astype(jnp.float32),
    )
    totals = (
        lax.psum(part_first.astype(jnp.bfloat16), "seq").astype(jnp.float32),
        lax.psum(in_part.astype(jnp.bfloat16), "seq").astype(jnp.float32),
        lax.psum(part_conv.astype(jnp.bfloat16), "seq").astype(jnp.float32),
        lax.psum(beta_part.astype(jnp.bfloat16), "seq").astype(jnp.float32),
        lax.psum(part_heads.astype(jnp.bfloat16), "seq").astype(jnp.float32),
        lax.psum(out_part.astype(jnp.bfloat16), "seq").astype(jnp.float32),
        lax.psum(part_second.astype(jnp.bfloat16), "seq").astype(jnp.float32),
        lax.psum(gu_part.astype(jnp.bfloat16), "seq").astype(jnp.float32),
        lax.psum(down_part.astype(jnp.bfloat16), "seq").astype(jnp.float32),
    )
    return (
        output,
        input_grad,
        totals[0],
        totals[1],
        totals[2],
        totals[3],
        totals[4],
        totals[5],
        totals[6],
        totals[7],
        totals[8],
    )


def solution(mesh):
    in_specs = (
        P("fsdp", "seq", None),
        P("fsdp", "seq", None),
        P("fsdp"),
        P(None, "fsdp", None),
        P(None, None, "fsdp"),
        P("fsdp", None),
        P("fsdp"),
        P("fsdp", None),
        P("fsdp"),
        P(None, "fsdp", None),
        P("fsdp", None),
    )
    out_specs = (
        P("fsdp", "seq", None),
        P("fsdp", "seq", None),
        P("fsdp"),
        P(None, "fsdp", None),
        P(None, None, "fsdp"),
        P("fsdp", None),
        P("fsdp"),
        P("fsdp", None),
        P("fsdp"),
        P(None, "fsdp", None),
        P("fsdp", None),
    )
    return jax.shard_map(local, mesh=mesh, in_specs=in_specs, out_specs=out_specs, check_vma=False)
```

profile of v0, /device:TPU:0, one launch (start us, length us, event | category | flops | bytes accessed | tf_op | source)
XLA Modules:
  0.0 4583.2 jit_solution(11209975152638770542)
XLA Ops:
  8.0 13.5 all-gather.4
  21.6 13.5 all_gather.69
  36.9 37.0 all_gather.66
  74.1 364.4 %all-gather.19.cloned.1.call-done = bf16[3,2048,2048]{2,1,0:T(8,128)(2,1)} async-done(((bf16[3,512,2048]{2,1,0:T(8,128)(2,1)}), bf16[3,2048,2048]{2,1,0:T(8,128)(2,1)}) %all-gather.19.cloned.1.call-update) | async-done | bytes 25165840 | tf_op jit(solution)/shard_map/all_gather | solution.py:156
  438.5 11.6 fusion.322
  472.4 381.4 %while.129 = (s32[]{:T(128)}, f32[2,16,128,128]{3,2,1,0:T(8,128)}, f32[2,16,128,128]{3,2,1,0:T(8,128)}, f32[2,2,16,64,128]{4,3,2,1,0:T(8,128)S(1)}, f32[2,2,16,6...) while((s32[]{:T(128)}, f32[2,16,128,128]{3,2,1,0:T(8,128)}, ...), condition=%wide.region_3.5_spmd.clone, body=%wide.region_2.4_spmd.clone.sunk | while | flops 2218151936 | bytes 64656136 | solution.py:112
  487.8 158.0 %custom-call.43 = f32[2,16,1,64,64]{3,4,2,1,0:T(8,128)S(1)} custom-call(f32[2,16,1,64,64]{4,3,2,1,0:T(8,128)} %fusion.644), custom_call_target="InvertDiagBlocksLowerTriangular" | custom-call | tf_op jit(solution)/shard_map/while/body/eval_jaxpr/triangular_solve/custom-call.1 | solution.py:85
  671.7 158.0 %custom-call.43 = f32[2,16,1,64,64]{3,4,2,1,0:T(8,128)S(1)} custom-call(f32[2,16,1,64,64]{4,3,2,1,0:T(8,128)} %fusion.644), custom_call_target="InvertDiagBlocksLowerTriangular" | custom-call | tf_op jit(solution)/shard_map/while/body/eval_jaxpr/triangular_solve/custom-call.1 | solution.py:85
  871.7 11.9 all-gather.5
  895.1 17.3 all-gather.35.cloned.1.call-done
  912.4 56.3 %all-gather.37.cloned.1.call-done = bf16[16,16,128,128]{3,2,1,0:T(8,128)(2,1)} async-done(((bf16[2,16,128,128]{3,2,1,0:T(8,128)(2,1)}), bf16[16,16,128,128]{3,2,1,0:T(8,128)(2,1)}) %all-gather.37.cloned.1.call-update) | async-done | bytes 8388624 | tf_op jit(solution)/shard_map/all_gather | solution.py:21
  976.8 386.8 %while.127 = (s32[]{:T(128)}, f32[2,16,128,128]{3,2,1,0:T(8,128)}, f32[2,2,16,64,128]{4,3,2,1,0:T(8,128)}, f32[2,2,16,64,64]{4,3,2,1,0:T(8,128)}, f32[2,2,16,64,...) while((s32[]{:T(128)}, f32[2,16,128,128]{3,2,1,0:T(8,128)}, ...), condition=%wide.region_8.10_spmd.clone, body=%wide.region_7.9_spmd.clone.sunk | while | flops 2217365504 | bytes 157516960 | solution.py:112
  989.6 158.0 %custom-call.41 = f32[2,16,1,64,64]{3,4,2,1,0:T(8,128)S(1)} custom-call(f32[2,16,1,64,64]{4,3,2,1,0:T(8,128)} %add_bitcast_fusion.5), custom_call_target="InvertDiagBlocksLowerTriangular" | custom-call | tf_op jit(solution)/shard_map/jvp()/while/body/eval_jaxpr/triangular_solve/custom-call.1 | solution.py:85
  1182.4 158.0 %custom-call.41 = f32[2,16,1,64,64]{3,4,2,1,0:T(8,128)S(1)} custom-call(f32[2,16,1,64,64]{4,3,2,1,0:T(8,128)} %add_bitcast_fusion.5), custom_call_target="InvertDiagBlocksLowerTriangular" | custom-call | tf_op jit(solution)/shard_map/jvp()/while/body/eval_jaxpr/triangular_solve/custom-call.1 | solution.py:85
  1384.9 503.5 %all-gather.23.cloned.1.call-done = bf16[2,2048,5632]{2,1,0:T(8,128)(2,1)} async-done(((bf16[2,512,5632]{2,1,0:T(8,128)(2,1)}), bf16[2,2048,5632]{2,1,0:T(8,128)(2,1)}) %all-gather.23.cloned.1.call-update) | async-done | bytes 46137360 | tf_op jit(solution)/shard_map/all_gather | solution.py:225
  1888.4 26.4 fusion.301
  1914.8 364.5 %all-gather.25.cloned.1.call-done = bf16[5632,2048]{1,0:T(8,128)(2,1)} async-done(((bf16[1408,2048]{1,0:T(8,128)(2,1)}), bf16[5632,2048]{1,0:T(8,128)(2,1)}) %all-gather.25.cloned.1.call-update) | async-done | bytes 23068688 | tf_op jit(solution)/shard_map/all_gather | solution.py:226
  2279.3 17.0 fusion.316
  2296.3 23.7 multiply_reduce_fusion.4
  2340.6 431.4 %while.130 = (s32[]{:T(128)}, f32[2,16,128,128]{3,2,1,0:T(8,128)}, f32[2,2,16,64,128]{4,2,3,0,1:T(8,128)}, f32[2,2,16,64,128]{4,2,3,0,1:T(8,128)}, f32[2,2,16,64...) while((s32[]{:T(128)}, f32[2,16,128,128]{3,2,1,0:T(8,128)}, ...), condition=%wide.region_17.21_spmd.clone.clone, body=%wide.region_13.20_spmd.clone.clone.sunk | while | flops 4638517248 | bytes 257136032 | solution.py:112
  2356.0 158.9 %custom-call.44 = f32[2,16,1,64,64]{3,4,2,1,0:T(8,128)} custom-call(f32[2,16,1,64,64]{4,3,2,1,0:T(8,128)} %fusion.688), custom_call_target="InvertDiagBlocksLowerTriangular" | custom-call | tf_op jit(solution)/shard_map/transpose(jvp())/while/body/eval_jaxpr/triangular_solve/custom-call.0 | solution.py:82
  2569.8 159.1 %custom-call.44 = f32[2,16,1,64,64]{3,4,2,1,0:T(8,128)} custom-call(f32[2,16,1,64,64]{4,3,2,1,0:T(8,128)} %fusion.688), custom_call_target="InvertDiagBlocksLowerTriangular" | custom-call | tf_op jit(solution)/shard_map/transpose(jvp())/while/body/eval_jaxpr/triangular_solve/custom-call.0 | solution.py:82
  2795.1 33.5 all-gather.41.cloned.1.call-done
  2830.2 56.1 %while.126 = (s32[]{:T(128)}, f32[2,16,128,128]{3,2,1,0:T(8,128)}, s32[]{:T(128)}, bf16[8,2,16,128,128]{4,3,2,1,0:T(8,128)(2,1)}, bf16[8,2,16,128,128]{4,3,2,1,0...) while((s32[]{:T(128)}, f32[2,16,128,128]{3,2,1,0:T(8,128)}, s32[]{:T(128)}, ...), condition=%wide.region_19.23_spmd, body=%wide.region_18.22_spmd.sunk | while | flops 806354944 | bytes 10486931 | solution.py:60
  2891.0 436.2 %while.128 = (s32[]{:T(128)}, f32[2,16,128,128]{3,2,1,0:T(8,128)}, f32[2,2,16,64,128]{4,2,3,0,1:T(8,128)}, f32[2,2,16,64,128]{4,2,3,0,1:T(8,128)}, f32[2,2,16,64...) while((s32[]{:T(128)}, f32[2,16,128,128]{3,2,1,0:T(8,128)}, ...), condition=%wide.region_24.28_spmd.clone.clone, body=%wide.region_20.27_spmd.clone.clone.sunk | while | flops 4636944384 | bytes 259229136 | solution.py:112
  2919.1 158.7 %custom-call.42 = f32[2,16,1,64,64]{3,4,2,1,0:T(8,128)} custom-call(f32[2,16,1,64,64]{4,3,2,1,0:T(8,128)} %fusion.621), custom_call_target="InvertDiagBlocksLowerTriangular" | custom-call | tf_op jit(solution)/shard_map/transpose(jvp())/while/body/eval_jaxpr/triangular_solve/custom-call.0 | solution.py:82
  3132.9 158.7 %custom-call.42 = f32[2,16,1,64,64]{3,4,2,1,0:T(8,128)} custom-call(f32[2,16,1,64,64]{4,3,2,1,0:T(8,128)} %fusion.621), custom_call_target="InvertDiagBlocksLowerTriangular" | custom-call | tf_op jit(solution)/shard_map/transpose(jvp())/while/body/eval_jaxpr/triangular_solve/custom-call.0 | solution.py:82
  3332.7 20.3 fusion.288
  3372.8 12.1 multiply_subtract_fusion.1
  3385.0 10.3 multiply_reduce_fusion.3
  3417.5 17.9 copy.310
  3441.6 32.3 copy.315
  3491.5 9.5 slice_bitcast_fusion
  3540.1 157.1 %all-to-all-done.3 = bf16[256,4,1408]{2,0,1:T(8,128)(2,1)} async-done(((bf16[256,4,1408]{2,0,1:T(8,128)(2,1)}), bf16[256,4,1408]{2,0,1:T(8,128)(2,1)}, u32[]{:S(2)}, u32[]{:S(2)}) %all-to-all-start.3) | async-done | bytes 2883616 | tf_op jit(solution)/shard_map/all_to_all | solution.py:245
  3700.8 10.6 convolution_convert_fusion
  3717.3 21.4 all-to-all-done
  3746.5 37.9 all-gather.27.cloned.1.call-done
  3784.4 13.6 convert_bitcast_fusion.2
  3798.0 376.7 %all-gather.31.cloned.1.call-done = bf16[1024,11264]{1,0:T(8,128)(2,1)} async-done(((bf16[256,11264]{1,0:T(8,128)(2,1)}), bf16[1024,11264]{1,0:T(8,128)(2,1)}) %all-gather.31.cloned.1.call-update) | async-done | bytes 23068688 | tf_op jit(solution)/shard_map/all_gather | solution.py:269
  4174.7 30.4 copy.316
  4205.1 19.4 convert_bitcast_fusion.1
  4226.1 18.4 fusion.342
  4244.7 13.3 all_gather.84
  4261.5 14.8 fusion.355
  4292.0 24.9 all-reduce.8
  4319.8 219.1 %all-reduce.13.cloned.1.call-done = (bf16[3,512,2048]{1,2,0:T(8,128)(2,1)}, bf16[2,512,5632]{1,2,0:T(8,128)(2,1)}, bf16[512,2048]{1,0:T(8,128)(2,1)}, bf16[1408,2048]{1,0:T(8,128)(2,1)}) async-done(((bf16[3,512,2048]{1,2,0:T(8,128)(2,1)}, bf16[2,512,5632]{1,2,0:T(8,128)(2,1)}, bf16[512,2048]{1,0:T(8,128)(2,1)}, bf16[1408,2048]{1,0:T(8,128)(2,1)}), (bf16[3,512,2048]{1,2,0:T(8,128)(2,1)}, ...) | async-done | bytes 25690128 | tf_op jit(solution)/shard_map/psum | solution.py:370
  4539.0 9.8 copy.321
  4551.3 16.6 copy.323
  (806 shorter events, 688.3 us)
Async XLA Ops:
  7.2 27.9 copy-start.70
  7.2 431.2 %all-gather.19.cloned.1.call-start = ((), (), s32[]{:S(2)}) async-start(), calls=%async_computation.5 | async-start | bytes 31457280 | tf_op jit(solution)/shard_map/all_gather | solution.py:156
  7.9 904.5 %all-gather.35.cloned.1.call-start = ((), (), s32[]{:S(2)}) async-start(), calls=%async_computation.13 | async-start | bytes 9437184 | tf_op jit(solution)/shard_map/all_gather | solution.py:21
  36.3 413.7 %copy-start.77 = (bf16[2,128,2048]{2,1,0:T(8,128)(2,1)}, bf16[2,128,2048]{2,1,0:T(8,128)(2,1)S(1)}, u32[]{:S(2)}) copy-start(bf16[2,128,2048]{2,1,0:T(8,128)(2,1)S(1)} %fusion.349) | copy-start | bytes 3145732
  36.7 37.2 copy-start.107
  74.0 380.1 %copy-start.102 = (f32[3,2048]{1,0:T(4,128)}, f32[3,2048]{1,0:T(4,128)S(1)}, u32[]{:S(2)}) copy-start(f32[3,2048]{1,0:T(4,128)S(1)} %get-tuple-element.2186) | copy-start | bytes 73732
  74.0 380.1 %copy-start.104 = (f32[3,2048]{1,0:T(4,128)}, f32[3,2048]{1,0:T(4,128)S(1)}, u32[]{:S(2)}) copy-start(f32[3,2048]{1,0:T(4,128)S(1)} %get-tuple-element.2187) | copy-start | bytes 73732
  74.0 380.0 %copy-start.105 = (f32[3,2048]{1,0:T(4,128)}, f32[3,2048]{1,0:T(4,128)S(1)}, u32[]{:S(2)}) copy-start(f32[3,2048]{1,0:T(4,128)S(1)} %get-tuple-element.2188) | copy-start | bytes 73732
  74.0 380.0 %copy-start.106 = (f32[3,2048]{1,0:T(4,128)}, f32[3,2048]{1,0:T(4,128)S(1)}, u32[]{:S(2)}) copy-start(f32[3,2048]{1,0:T(4,128)S(1)} %get-tuple-element.2189) | copy-start | bytes 73732
  450.1 2.9 collective-permute-start
  856.5 112.2 %all-gather.37.cloned.1.call-start = ((), (), s32[]{:S(2)}) async-start(), calls=%async_computation.14 | async-start | bytes 9437184 | tf_op jit(solution)/shard_map/all_gather | solution.py:21
  859.4 516.8 %all-gather.21.cloned.1.call-start = ((), (), s32[]{:S(2)}) async-start(), calls=%async_computation.6 | async-start | bytes 10485760 | tf_op jit(solution)/shard_map/all_gather | solution.py:160
  860.0 1028.4 %all-gather.23.cloned.1.call-start = ((), (), s32[]{:S(2)}) async-start(), calls=%async_computation.7 | async-start | bytes 57671680 | tf_op jit(solution)/shard_map/all_gather | solution.py:225
  860.6 1418.7 %all-gather.25.cloned.1.call-start = ((), (), s32[]{:S(2)}) async-start(), calls=%async_computation.8 | async-start | bytes 28835840 | tf_op jit(solution)/shard_map/all_gather | solution.py:226
  861.2 1933.9 %all-gather.39.cloned.1.call-start = ((), (), s32[]{:S(2)}) async-start(), calls=%async_computation.15 | async-start | bytes 9437184 | tf_op jit(solution)/shard_map/all_gather | solution.py:43
  883.6 1436.4 %copy-start.115 = (f32[4,1,512]{2,1,0:T(1,128)}, f32[4,1,512]{2,1,0:T(1,128)S(1)}, u32[]{:S(2)}) copy-start(f32[4,1,512]{2,1,0:T(1,128)S(1)} %convert_element_type.269) | copy-start | bytes 24580
  895.1 1933.5 %all-gather.41.cloned.1.call-start = ((), (), s32[]{:S(2)}) async-start(), calls=%async_computation.16 | async-start | bytes 9437184 | tf_op jit(solution)/shard_map/all_gather | solution.py:43
  1383.3 936.7 %copy-start.128 = (f32[2,128]{1,0:T(2,128)}, f32[2,128]{1,0:T(2,128)S(1)}, u32[]{:S(2)}) copy-start(f32[2,128]{1,0:T(2,128)S(1)} %get-tuple-element.2177) | copy-start | bytes 3076
  1383.4 936.6 %copy-start.133 = (f32[2,128]{1,0:T(2,128)}, f32[2,128]{1,0:T(2,128)S(1)}, u32[]{:S(2)}) copy-start(f32[2,128]{1,0:T(2,128)S(1)} %get-tuple-element.2176) | copy-start | bytes 3076
  1384.9 529.9 %copy-start.75 = (bf16[2,128,2048]{2,1,0:T(8,128)(2,1)}, bf16[2,128,2048]{2,1,0:T(8,128)(2,1)S(1)}, u32[]{:S(2)}) copy-start(bf16[2,128,2048]{2,1,0:T(8,128)(2,1)S(1)} %multiply_convert_fusion.1) | copy-start | bytes 3145732
  2296.3 23.7 copy-start.79
  2774.8 926.0 %all-gather.33.cloned.1.call-start = ((), (), s32[]{:S(2)}) async-start(), calls=%async_computation.12 | async-start | bytes 5242880 | tf_op jit(solution)/shard_map/all_gather | solution.py:268
  2775.5 935.9 %all-gather.29.cloned.1.call-start = ((), (), s32[]{:S(2)}) async-start(), calls=%async_computation.10 | async-start | bytes 5242880 | tf_op jit(solution)/shard_map/all_gather | solution.py:339
  2795.1 989.3 %all-gather.27.cloned.1.call-start = ((), (), s32[]{:S(2)}) async-start(), calls=%async_computation.9 | async-start | bytes 15728640 | tf_op jit(solution)/shard_map/all_gather | solution.py:340
  3409.8 4.1 collective-permute-start.1
  3437.4 737.3 %all-gather.31.cloned.1.call-start = ((), (), s32[]{:S(2)}) async-start(), calls=%async_computation.11 | async-start | bytes 28835840 | tf_op jit(solution)/shard_map/all_gather | solution.py:269
  3486.8 43.7 all-to-all-start.1
  3531.5 165.7 %all-to-all-start.3 = ((bf16[256,4,1408]{2,0,1:T(8,128)(2,1)}), bf16[256,4,1408]{2,0,1:T(8,128)(2,1)}, u32[]{:S(2)}, u32[]{:S(2)}) async-start(bf16[256,4,1408]{2,0,1:T(8,128)(2,1)} %fusion.318), calls=%async_computation.3 | async-start | bytes 5767168 | tf_op jit(solution)/shard_map/all_to_all | solution.py:245
  3697.2 41.5 all-to-all-start
  3717.3 25.8 copy-start.119
  3717.3 25.8 copy-start.120
  3717.3 25.8 copy-start.121
  3717.3 25.8 copy-start.122
  3738.8 45.6 copy-start.95
  3738.8 466.4 %all-to-all-start.2 = ((bf16[256,4,512]{2,0,1:T(8,128)(2,1)}), bf16[256,4,512]{2,0,1:T(8,128)(2,1)}, u32[]{:S(2)}, u32[]{:S(2)}) async-start(bf16[256,4,512]{2,0,1:T(8,128)(2,1)} %copy.317), calls=%async_computation.2 | async-start | bytes 2097152 | tf_op jit(solution)/shard_map/all_to_all | solution.py:242
  3743.0 547.5 %reduce-scatter.4.cloned.1.call-start = ((), (), s32[]{:S(2)}) async-start(), calls=%async_computation.17 | async-start | bytes 655360
  3746.4 792.5 %all-reduce.13.cloned.1.call-start = ((), (), s32[]{:S(2)}) async-start(), calls=%async_computation.18 | async-start | bytes 51380224 | tf_op jit(solution)/shard_map/psum | solution.py:370
  4226.1 18.4 copy-start.112
  4226.1 18.4 copy-start.114
  4226.1 18.6 copy-start.108
  4226.1 33.5 copy-start.101
  4244.5 16.9 copy-start.118
  4244.5 16.9 copy-start.132
  4261.4 24.0 copy-start.116
  4261.4 24.0 copy-start.129
  4261.4 24.0 copy-start.134
  4261.4 24.0 copy-start.136
  4261.5 24.0 copy-start.141
  (187 other events, 651.9 us)
Sparse Core Ops, SparseCore 0:
  9.6 428.7 all-gather.18
  856.7 55.7 all-gather.34
  914.3 54.3 all-gather.36
  970.2 149.7 all-gather.20
  1121.4 766.9 all-gather.22
  1889.8 389.3 all-gather.24
  2281.2 52.6 all-gather.38
  2774.9 53.6 all-gather.40
  2830.2 80.7 all-gather.32
  2912.4 79.5 all-gather.28
  3437.5 346.7 all-gather.26
  3786.4 388.2 all-gather.30
  4177.0 19.9 reduce-scatter.3
  4224.7 314.2 all-reduce.12
where the time goes:
time: 4600 us; the launch traced here: 4580 us
  waiting for transfers between devices  2160 us (47%)
  other arithmetic  1410 us (31%)
  matrix products  496 us (11%)
  local copies, waits for them, and re-layouts  314 us (7%)
  blocking collectives  132 us (3%)
    another operation x20, other arithmetic, block_step(): lax.linalg.triangular_solve(lower_mat, strength[..., None] * key_rows, le...  640 us
    another operation x16, other arithmetic, block_step(): lax.linalg.triangular_solve(lower_mat, strength[..., None] * value_rows,...  635 us
    all_gather x1, waiting for transfers between devices, local(): lax.all_gather(w_gate_up, 'fsdp', axis=1, tiled=True)  504 us
    all_gather x1, waiting for transfers between devices, local(): lax.all_gather(grad_gate_up.reshape(row_count, -1), 'fsdp', axis=0, tiled...  377 us
    all_gather x1, waiting for transfers between devices, local(): lax.all_gather(w_down, 'fsdp', axis=0, tiled=True)  364 us
    all_gather x1, waiting for transfers between devices, local(): lax.all_gather(w_inputs, 'fsdp', axis=1, tiled=True)  364 us
    dot_general x77, matrix products, contract(): return jnp.einsum(pattern, left_op, right_op, precision=highest)  239 us
    psum x1, waiting for transfers between devices, local(): lax.psum(in_part.astype(jnp.bfloat16), 'seq').astype(jnp.float32)  219 us
  transfers between devices with their start and end apart: 20, of which 13 were waited for; matrix products, arithmetic and copies ran while one was open for 38% of the time, Pallas kernels for 0%

commit v1 on v0

v1 whole, which is shorter than its diff:
```python
import functools

import jax
import jax.numpy as jnp
from jax import lax
from jax.experimental import pallas as pl
from jax.experimental.pallas import tpu as pltpu
from jax.sharding import PartitionSpec as P

LOW = jnp.bfloat16
WIDE = jnp.float32


def swap(x, bits):
    count = lax.axis_size("seq")
    return lax.ppermute(x, "seq", [(i, i ^ bits) for i in range(count)])


def gather_start(x):
    if lax.axis_size("seq") == 8:
        return [x, swap(x, 1), swap(x, 2), swap(x, 4)]
    return [x]


def gather_far(first):
    if lax.axis_size("seq") != 8:
        return []
    x, _, side, back = first
    half = x.shape[0] // 2
    if x.shape[0] % 32 == 0:
        return [swap(back[:half], 2), swap(side[half:], 4)]
    return [swap(back, 2)]


def gather_rest(first, far):
    count, x = lax.axis_size("seq"), first[0]
    if count == 8:
        _, twin, side, back = first
        side_twin, back_twin = swap(side, 1), swap(back, 1)
        return [[x], [twin], [side], [side_twin], [back], [back_twin], far, [swap(f, 1) for f in far]]
    held, bits = x[None], 1
    while bits < count:
        held = jnp.concatenate([held, swap(held, bits)])
        bits *= 2
    return [[held[b]] for b in range(count)]


def gather_xor(x):
    first = gather_start(x)
    return gather_rest(first, gather_far(first))


def add(first, second):
    return (first.astype(WIDE) + second.astype(WIDE)).astype(LOW)


def reduce_start(odd):
    return swap(odd, 1) if lax.axis_size("seq") == 8 else odd


def reduce_far(even, twin):
    count = lax.axis_size("seq")
    if count == 8:
        half = even.shape[1] // 2
        far, side, back = (add(even[b], twin[b]) for b in (3, 1, 2))
        far_top, far_low = swap(far[:half], 2), swap(far[half:], 4)
        side_top, back_low = swap(side[:half], 2), swap(back[half:], 4)
        return [even[0], twin[0], side[half:], back[:half], side_top, back_low, far_top, far_low]
    parts = jnp.stack([even, twin], axis=1).reshape((count,) + even.shape[1:])
    bits = count // 2
    while bits:
        parts = add(parts[:bits], swap(parts[bits:], bits))
        bits //= 2
    return [parts[0]]


def reduce_last(state):
    if len(state) == 1:
        return [state]
    own, twin, side, back, side_top, back_low, far_top, far_low = state
    side_low = swap(add(side, far_low), 2)
    back_top = swap(add(back, far_top), 4)
    return [[own], [twin], [side_top, side_low], [back_top, back_low]]


def exchange_xor(parts):
    count = lax.axis_size("seq")
    if count == 8:
        twin = swap(parts[1], 1)
        out = [parts[0, :1], twin[:1]]
        for n in (1, 2, 3):
            out.append(swap(jnp.concatenate([parts[0, n : n + 1], twin[n : n + 1]]), 2 * n))
        return out
    return [parts[0, :1]] + [swap(parts[b % 2, b // 2][None], b) for b in range(1, count)]


def sum_over(axis, x):
    count, bits = lax.axis_size(axis), 1
    while bits < count:
        x = x + lax.ppermute(x, axis, [(i, i ^ bits) for i in range(count)])
        bits *= 2
    return x


def after(x, *others):
    return lax.optimization_barrier((x,) + others)[0]


def dot(a, b, left=1, right=0):
    return lax.dot_general(
        a.astype(LOW), b.astype(LOW), (((left,), (right,)), ((), ())), preferred_element_type=WIDE
    )


def iota(shape, dim):
    return lax.broadcasted_iota(jnp.int32, shape, dim)


def shifted(x, by):
    rows = x.shape[0]
    turned = pltpu.roll(x, by % rows, 0)
    row = iota(x.shape, 0)
    return jnp.where(row >= by if by > 0 else row < rows + by, turned, 0.0)


def conv_silu(x, taps):
    count = taps.shape[0]
    moved = [shifted(x, count - 1 - j) if j < count - 1 else x for j in range(count)]
    conved = sum(taps[j : j + 1] * moved[j] for j in range(count))
    gate = jax.nn.sigmoid(conved)
    return moved, conved, gate, conved * gate


def unit_scale(values):
    return lax.rsqrt(jnp.sum(values * values, axis=-1, keepdims=True) + 1e-06)


def pick_lane(block, lane):
    return jnp.sum(jnp.where(iota(block.shape, 1) == lane, block, 0.0), axis=-1, keepdims=True)


def invert_unit_lower(mats):
    size = mats[0].shape[0]
    row, col = iota((size, size), 0), iota((size, size), 1)
    invs = [jnp.where(row == col, 1.0, jnp.where(row // 2 == col // 2, -a, 0.0)) for a in mats]
    width = 2
    while width < size:
        mask = (row // (2 * width) == col // (2 * width)) & (row // width != col // width)
        part = [dot(t, jnp.where(mask, a, 0.0)) for t, a in zip(invs, mats)]
        invs = [t - dot(p, t) for t, p in zip(invs, part)]
        width *= 2
    return invs


def mixer_forward(
    place_ref, proj_ref, taps_ref, logit_ref, gain_ref, out_ref, mixed_ref, state_ref, inv_ref, w_ref, fresh_ref
):
    place, head = place_ref[0], pl.program_id(0)
    count, _, length, _ = proj_ref.shape
    dim = mixed_ref.shape[-1]
    spot = [jnp.bitwise_xor(place, i) for i in range(count)]
    whole = jnp.concatenate([proj_ref[j, 0] for j in spot]).astype(WIDE)
    acts = [conv_silu(whole[:, c * dim : (c + 1) * dim], taps_ref[0, c])[3] for c in range(3)]
    queries = (acts[0] * (unit_scale(acts[0]) * dim ** (-0.5))).astype(LOW)
    key_rows = (acts[1] * unit_scale(acts[1])).astype(LOW)
    value_rows = acts[2].astype(LOW)

    def cut(x):
        return [x[i * length : (i + 1) * length] for i in range(count)]

    q, k, v = cut(queries), cut(key_rows), cut(value_rows)
    beta = [jax.nn.sigmoid(pick_lane(logit_ref[j, 0], head)) for j in spot]
    row, col = iota((length, length), 0), iota((length, length), 1)
    lower = [jnp.where(row > col, b * dot(x, x, 1, 1), 0.0) for b, x in zip(beta, k)]
    invs = [t.astype(LOW) for t in invert_unit_lower(lower)]
    w = [dot(t, b * x.astype(WIDE)).astype(LOW) for t, b, x in zip(invs, beta, k)]
    u = [dot(t, b * x.astype(WIDE)) for t, b, x in zip(invs, beta, v)]
    scores = [jnp.where(row >= col, dot(a, b, 1, 1), 0.0).astype(LOW) for a, b in zip(q, k)]
    turn = [dot(a, b, 0, 0).astype(LOW) for a, b in zip(k, w)]
    push = [dot(a, b, 0, 0) for a, b in zip(k, u)]
    state = jnp.zeros((dim, dim), WIDE)
    states = []
    for i in range(count):
        states.append(state.astype(LOW))
        state = state + (push[i] - dot(turn[i], states[i]))
    fresh = [(a - dot(b, c)).astype(LOW) for a, b, c in zip(u, w, states)]
    gain = gain_ref[...]
    for i in range(count):
        mixed = dot(q[i], states[i]) + dot(scores[i], fresh[i])
        scale = lax.rsqrt(jnp.mean(mixed * mixed, axis=-1, keepdims=True) + 1e-05)
        mixed_ref[0, 0, i] = mixed
        out_ref[spot[i] & 1, spot[i] >> 1] = (mixed * scale * gain).astype(LOW)
        state_ref[0, 0, i] = states[i]
        inv_ref[0, 0, i] = invs[i]
        w_ref[0, 0, i] = w[i]
        fresh_ref[0, 0, i] = fresh[i]


def mixer_backward(stacks, place_ref, proj_ref, taps_ref, logit_ref, gain_ref, *refs):
    gout_refs, refs = refs[: len(stacks)], refs[len(stacks) :]
    mixed_ref, state_ref, inv_ref, w_ref, fresh_ref = refs[:5]
    gproj_ref, glogit_ref, gtaps_ref, ggain_ref, gout_ref = refs[-5:]
    at = 0
    for ref, size in zip(gout_refs, stacks):
        gout_ref[at : at + size] = ref[...]
        at += size
    place, head = place_ref[0], pl.program_id(0)
    count, _, length, _ = proj_ref.shape
    dim = mixed_ref.shape[-1]
    spot = [jnp.bitwise_xor(place, i) for i in range(count)]
    whole = jnp.concatenate([proj_ref[j, 0] for j in spot]).astype(WIDE)
    convs = [conv_silu(whole[:, c * dim : (c + 1) * dim], taps_ref[0, c]) for c in range(3)]
    acts = [c[3] for c in convs]
    q_scale, k_scale = unit_scale(acts[0]), unit_scale(acts[1])
    factor = dim ** (-0.5)

    def cut(x):
        return [x[i * length : (i + 1) * length] for i in range(count)]

    q = cut((acts[0] * (q_scale * factor)).astype(LOW))
    k = cut((acts[1] * k_scale).astype(LOW))
    v = cut(acts[2].astype(LOW))
    beta = [jax.nn.sigmoid(pick_lane(logit_ref[j, 0], head)) for j in spot]
    row, col = iota((length, length), 0), iota((length, length), 1)
    gain = gain_ref[...]
    gain_sum = jnp.zeros((1, dim), WIDE)
    gm = []
    for i in range(count):
        mixed = mixed_ref[0, 0, i]
        scale = lax.rsqrt(jnp.mean(mixed * mixed, axis=-1, keepdims=True) + 1e-05)
        grad = gout_ref[spot[i]].astype(WIDE)
        gain_sum = gain_sum + jnp.sum(grad * mixed * scale, axis=0, keepdims=True)
        weighted = grad * gain
        back = scale * weighted - mixed * (
            scale * scale * scale * jnp.mean(mixed * weighted, axis=-1, keepdims=True)
        )
        gm.append(back.astype(LOW))
    ggain_ref[0] = gain_sum
    inv, w, fresh, states = ([r[0, 0, i] for i in range(count)] for r in (inv_ref, w_ref, fresh_ref, state_ref))
    gram = [dot(x, x, 1, 1) for x in k]
    scores = [jnp.where(row >= col, dot(a, b, 1, 1), 0.0).astype(LOW) for a, b in zip(q, k)]
    turn = [dot(a, b, 0, 0).astype(LOW) for a, b in zip(k, w)]
    direct = [dot(a, b, 0, 0) for a, b in zip(scores, gm)]
    enter = [dot(a, b, 0, 0) - dot(c, d, 0, 0) for a, b, c, d in zip(q, gm, w, direct)]
    gstate = jnp.zeros((dim, dim), WIDE)
    late = [None] * count
    for i in reversed(range(count)):
        late[i] = gstate.astype(LOW)
        gstate = gstate + (enter[i] - dot(turn[i], late[i], 0, 0))
    gfresh = [a + dot(b, c) for a, b, c in zip(direct, k, late)]
    g = [dot(a, b, 0, 0) for a, b in zip(inv, gfresh)]
    g_low = [x.astype(LOW) for x in g]
    gs = [dot(a, b, 1, 1) for a, b in zip(g_low, states)]
    ga = [jnp.where(row > col, -dot(a, b, 1, 1), 0.0) for a, b in zip(g_low, fresh)]
    gscore = [jnp.where(row >= col, dot(a, b, 1, 1), 0.0).astype(LOW) for a, b in zip(gm, fresh)]
    gq = [dot(a, b, 1, 1) + dot(c, d) for a, b, c, d in zip(gm, states, gscore, k)]
    weighted_a = [b * a for b, a in zip(beta, ga)]
    gk = [
        dot(f, d, 1, 1) + dot(sc, qq, 0, 0) - b * s + dot(wa, kk) + dot(wa, kk, 0, 0)
        for f, d, sc, qq, b, s, wa, kk in zip(fresh, late, gscore, q, beta, gs, weighted_a, k)
    ]
    gv = [b * x for b, x in zip(beta, g)]
    lane = iota((length, glogit_ref.shape[-1]), 1)
    for i in range(count):
        gbeta = jnp.sum(
            g[i] * v[i].astype(WIDE) - gs[i] * k[i].astype(WIDE) + ga[i] * gram[i], axis=-1, keepdims=True
        )
        glogit = gbeta * beta[i] * (1.0 - beta[i])
        before = glogit_ref[spot[i], 0]
        keep = jnp.where(lane < head, before.astype(WIDE), 0.0)
        glogit_ref[spot[i], 0] = jnp.where(lane == head, glogit, keep).astype(LOW)

    def unit_back(values, scale, grad):
        return scale * grad - values * (
            scale * scale * scale * jnp.sum(values * grad, axis=-1, keepdims=True)
        )

    gacts = [
        unit_back(acts[0], q_scale, jnp.concatenate(gq) * factor),
        unit_back(acts[1], k_scale, jnp.concatenate(gk)),
        jnp.concatenate(gv),
    ]
    for c in range(3):
        moved, conved, gate, _ = convs[c]
        gconv = gacts[c] * gate * (1.0 + conved * (1.0 - gate))
        taps = taps_ref[0, c]
        gtaps_ref[0, c] = jnp.concatenate([jnp.sum(gconv * m, axis=0, keepdims=True) for m in moved])
        last = len(moved) - 1
        gp = taps[last : last + 1] * gconv
        for j in range(last):
            gp = gp + taps[j : j + 1] * shifted(gconv, j - last)
        gp = gp.astype(LOW)
        for i in range(count):
            gproj_ref[spot[i], 0, :, c * dim : (c + 1) * dim] = gp[i * length : (i + 1) * length]


def mixer_specs(b, count, length, dim, lanes, taps):
    small = [
        pl.BlockSpec((count, 1, length, 3 * dim), lambda h, p: (0, b, 0, h)),
        pl.BlockSpec((1, 3, taps, dim), lambda h, p: (h, 0, 0, 0)),
        pl.BlockSpec((count, 1, length, lanes), lambda h, p: (0, b, 0, 0)),
        pl.BlockSpec((1, dim), lambda h, p: (0, 0)),
    ]
    saved = pl.BlockSpec((1, 1, count, length, dim), lambda h, p: (0, h, 0, 0, 0))
    square = pl.BlockSpec((1, 1, count, dim, dim), lambda h, p: (0, h, 0, 0, 0))
    inverse = pl.BlockSpec((1, 1, count, length, length), lambda h, p: (0, h, 0, 0, 0))
    return small, [saved, square, inverse, saved, saved]


def run_mixer_forward(b, place, proj, taps, logits, gain):
    count, _, length, width = proj.shape
    heads, _, tap_count, dim = taps.shape
    small, saved = mixer_specs(b, count, length, dim, logits.shape[-1], tap_count)
    shapes = [
        jax.ShapeDtypeStruct((2, count // 2, length, heads * dim), LOW),
        jax.ShapeDtypeStruct((1, heads, count, length, dim), WIDE),
        jax.ShapeDtypeStruct((1, heads, count, dim, dim), LOW),
        jax.ShapeDtypeStruct((1, heads, count, length, length), LOW),
        jax.ShapeDtypeStruct((1, heads, count, length, dim), LOW),
        jax.ShapeDtypeStruct((1, heads, count, length, dim), LOW),
    ]
    out = pl.BlockSpec((2, count // 2, length, dim), lambda h, p: (0, 0, 0, h))
    return pl.pallas_call(
        mixer_forward,
        out_shape=shapes,
        grid_spec=pltpu.PrefetchScalarGridSpec(
            num_scalar_prefetch=1, grid=(heads,), in_specs=small, out_specs=[out] + saved
        ),
        compiler_params=pltpu.CompilerParams(vmem_limit_bytes=56 * 2**20),
        cost_estimate=cost(10),
        name="mixer_forward",
    )(place, proj, taps, logits, gain)


def run_mixer_backward(b, place, proj, taps, logits, gain, gout, saved_values, held):
    count, _, length, width = proj.shape
    heads, _, tap_count, dim = taps.shape
    small, saved = mixer_specs(b, count, length, dim, logits.shape[-1], tap_count)
    shapes = [
        jax.ShapeDtypeStruct(proj.shape, LOW),
        jax.ShapeDtypeStruct(logits.shape, LOW),
        jax.ShapeDtypeStruct((heads, 3, tap_count, dim), WIDE),
        jax.ShapeDtypeStruct((heads, 1, dim), WIDE),
    ]
    outs = [
        small[0],
        small[2],
        pl.BlockSpec((1, 3, tap_count, dim), lambda h, p: (h, 0, 0, 0)),
        pl.BlockSpec((1, 1, dim), lambda h, p: (h, 0, 0)),
    ]
    sizes = [g.shape[0] for g in gout]
    gouts = [pl.BlockSpec((n, length, dim), lambda h, p: (0, 0, h)) for n in sizes]
    held = list(held or [])
    first = 1 + len(small) + len(gouts) + len(saved)
    return pl.pallas_call(
        functools.partial(mixer_backward, sizes),
        out_shape=shapes,
        grid_spec=pltpu.PrefetchScalarGridSpec(
            num_scalar_prefetch=1,
            grid=(heads,),
            in_specs=small + gouts + saved + [ANY] * len(held),
            out_specs=outs,
            scratch_shapes=[pltpu.VMEM((count, length, dim), LOW)],
        ),
        input_output_aliases={first + n: n for n in range(len(held))},
        compiler_params=pltpu.CompilerParams(vmem_limit_bytes=56 * 2**20),
        cost_estimate=cost(13),
        name="mixer_backward",
    )(place, proj, taps, logits, gain, *gout, *saved_values, *held)


ANY = pl.BlockSpec(memory_space=pl.ANY)
FULL = pltpu.VMEM
PARAMS = pltpu.CompilerParams(vmem_limit_bytes=60 * 2**20)


def cost(micros):
    return pl.CostEstimate(flops=int(micros * 0.5e9), transcendentals=0, bytes_accessed=0)


def fetch(entries, refs, buf, sems):
    copies, n = [], 0
    for b, entry in enumerate(entries):
        row, mine = 0, []
        for size in entry:
            copy = pltpu.make_async_copy(refs[n], buf.at[b, pl.ds(row, size)], sems.at[n])
            copy.start()
            mine.append(copy)
            row, n = row + size, n + 1
        copies.append(mine)
    return copies


def heights(entries):
    return [[a.shape[0] for a in entry] for entry in entries]


def flat(entries):
    return [a for entry in entries for a in entry]


def project_kernel(entries, *refs):
    n = sum(len(e) for e in entries)
    w_ref, beta_ref, proj_ref, logit_ref, all_ref, buf, sems, out_sems = refs[n:]
    copies = fetch(entries, refs[:n], buf, sems)
    outs = []
    for b, mine in enumerate(copies):
        for c in mine:
            c.wait()
        out = pltpu.make_async_copy(buf.at[b], all_ref.at[b], out_sems.at[b])
        out.start()
        outs.append(out)
        x = buf[b]
        proj_ref[b] = dot(x, w_ref[...]).astype(LOW)
        logit_ref[b] = dot(x, beta_ref[...], 1, 1)
    for out in outs:
        out.wait()


def run_project(entries, w, beta, cols):
    sizes = heights(entries)
    count, rows = len(sizes), sum(sizes[0])
    pieces = flat(entries)
    width = pieces[0].shape[1]
    return pl.pallas_call(
        functools.partial(project_kernel, sizes),
        grid=(1,),
        in_specs=[ANY] * len(pieces)
        + [pl.BlockSpec((width, cols), lambda g: (0, 0)), pl.BlockSpec(beta.shape, lambda g: (0, 0))],
        out_specs=[
            pl.BlockSpec((count, rows, cols), lambda g: (0, 0, 0)),
            pl.BlockSpec((count, rows, beta.shape[0]), lambda g: (0, 0, 0)),
            ANY,
        ],
        out_shape=[
            jax.ShapeDtypeStruct((count, rows, cols), LOW),
            jax.ShapeDtypeStruct((count, rows, beta.shape[0]), WIDE),
            jax.ShapeDtypeStruct((count, rows, width), LOW),
        ],
        scratch_shapes=[
            pltpu.VMEM((count, rows, width), LOW),
            pltpu.SemaphoreType.DMA((len(pieces),)),
            pltpu.SemaphoreType.DMA((count,)),
        ],
        compiler_params=PARAMS,
        cost_estimate=cost(16),
        name="project",
    )(*pieces, w, beta)


def gate_kernel(entries, others, *refs):
    n = sum(len(e) for e in entries)
    m = n + sum(len(e) for e in others)
    w_ref, inner_ref, up_ref, gate_ref, all_ref, side_ref = refs[m : m + 6]
    buf, side, sems, out_sems, side_sems, back_sems = refs[m + 6 :]
    copies = fetch(entries, refs[:n], buf, sems)
    beside = fetch(others, refs[n:m], side, side_sems)
    ff = inner_ref.shape[-1]
    outs = []
    for b, mine in enumerate(copies):
        for c in mine:
            c.wait()
        out = pltpu.make_async_copy(buf.at[b], all_ref.at[b], out_sems.at[b])
        out.start()
        outs.append(out)
        both = dot(buf[b], w_ref[...])
        gate, up = both[:, :ff], both[:, ff:]
        sig = jax.nn.sigmoid(gate)
        swish = gate * sig
        inner_ref[b] = (swish * up).astype(LOW)
        gate_ref[b] = (up * sig * (1.0 + gate * (1.0 - sig))).astype(LOW)
        up_ref[b] = swish.astype(LOW)
        for c in beside[b]:
            c.wait()
        out = pltpu.make_async_copy(side.at[b], side_ref.at[b], back_sems.at[b])
        out.start()
        outs.append(out)
    for out in outs:
        out.wait()


def run_gate(entries, others, w):
    sizes = heights(entries)
    beside = flat(others)
    count, rows = len(sizes), sum(sizes[0])
    pieces = flat(entries)
    width, ff = pieces[0].shape[1], w.shape[1] // 2
    return pl.pallas_call(
        functools.partial(gate_kernel, sizes, heights(others)),
        in_specs=[ANY] * (len(pieces) + len(beside)) + [pl.BlockSpec(memory_space=FULL)],
        out_specs=[pl.BlockSpec(memory_space=FULL)] * 3 + [ANY] * 2,
        out_shape=[jax.ShapeDtypeStruct((count, rows, ff), LOW)] * 3
        + [jax.ShapeDtypeStruct((count, rows, width), LOW)] * 2,
        scratch_shapes=[
            pltpu.VMEM((count, rows, width), LOW),
            pltpu.VMEM((count, rows, width), LOW),
            pltpu.SemaphoreType.DMA((len(pieces),)),
            pltpu.SemaphoreType.DMA((count,)),
            pltpu.SemaphoreType.DMA((len(beside),)),
            pltpu.SemaphoreType.DMA((count,)),
        ],
        compiler_params=PARAMS,
        cost_estimate=cost(25),
        name="gate",
    )(*pieces, *beside, w)


def gate_back_kernel(cot_ref, up_ref, gate_ref, down_ref, w_ref, grad_ref, even_ref, odd_ref):
    _, rows, width = cot_ref.shape
    grad = dot(cot_ref[...].reshape(2 * rows, width), down_ref[...], 1, 1)
    gate, up = (r[...].reshape(2 * rows, r.shape[-1]).astype(WIDE) for r in (gate_ref, up_ref))
    both = jnp.concatenate([grad * gate, grad * up], axis=1).astype(LOW)
    grad_ref[...] = both.reshape(grad_ref.shape)
    two = dot(both, w_ref[...], 1, 1).astype(LOW)
    even_ref[0] = two[:rows]
    odd_ref[0] = two[rows:]


def run_gate_back(cot, up, gate, down, w):
    count, rows, width = cot.shape
    ff = up.shape[-1]

    def block(cols, depth=2):
        return pl.BlockSpec((depth, rows, cols), lambda b: (b, 0, 0))

    def once(x):
        return pl.BlockSpec(x.shape, lambda b: (0, 0), pipeline_mode=pl.Buffered(1))

    half = jax.ShapeDtypeStruct((count // 2, rows, width), LOW)
    return pl.pallas_call(
        gate_back_kernel,
        grid=(count // 2,),
        in_specs=[block(width), block(ff), block(ff), once(down), once(w)],
        out_specs=[block(2 * ff), block(width, 1), block(width, 1)],
        out_shape=[jax.ShapeDtypeStruct((count, rows, 2 * ff), LOW), half, half],
        compiler_params=PARAMS,
        cost_estimate=cost(32),
        name="gate_back",
    )(cot, up, gate, down, w)


def pairs_kernel(count, right, *refs):
    even_ref, odd_ref = refs[2 * count :]
    rows = even_ref.shape[1]
    total = 0.0
    for n in range(count):
        x, w = refs[n], refs[count + n]
        total = total + dot(x[...].reshape(2 * rows, x.shape[-1]), w[...], 1, right[n])
    total = total.astype(LOW)
    even_ref[0] = total[:rows]
    odd_ref[0] = total[rows:]


def run_pairs(terms, width, name):
    count, rows, _ = terms[0][0].shape
    half = jax.ShapeDtypeStruct((count // 2, rows, width), LOW)
    weight_specs = []
    for x, w, right in terms:
        shape = (x.shape[-1], width) if right == 0 else (width, x.shape[-1])
        weight_specs.append(pl.BlockSpec(shape, lambda b: (0, 0), pipeline_mode=pl.Buffered(1)))
    return pl.pallas_call(
        functools.partial(pairs_kernel, len(terms), [t[2] for t in terms]),
        grid=(count // 2,),
        in_specs=[pl.BlockSpec((2, rows, t[0].shape[-1]), lambda b: (b, 0, 0)) for t in terms] + weight_specs,
        out_specs=[pl.BlockSpec((1, rows, width), lambda b: (b, 0, 0))] * 2,
        out_shape=[half, half],
        compiler_params=PARAMS,
        cost_estimate=cost(12),
        name=name,
    )(*[t[0] for t in terms], *[t[1] for t in terms])


def branch_kernel(entries, place_ref, *refs):
    n = sum(len(e) for e in entries)
    count = len(entries)
    parts, (token_ref, gain_ref, hidden_ref, two_ref, rows_ref, buf, sems) = refs[n:-7], refs[-7:]
    copies = fetch(entries, refs[:n], buf, sems)
    place = place_ref[0]
    wide = parts[0].shape[-1]

    def spot(b):
        return pl.ds(pl.multiple_of(jnp.bitwise_xor(place, b) * wide, wide), wide)

    row, at = 0, 0
    for ref in parts:
        size, length, _ = ref.shape
        for i in range(size):
            rows_ref[row : row + length, spot(at + i)] = ref[i]
        at += size
        if at == count:
            row, at = row + length, 0
    rows = rows_ref[...]
    for b, mine in enumerate(copies):
        for c in mine:
            c.wait()
        hidden_ref[:, spot(b)] = dot(rows, buf[b])
    hidden = hidden_ref[...] + token_ref[...].astype(WIDE)
    hidden_ref[...] = hidden
    scale = lax.rsqrt(jnp.mean(hidden * hidden, axis=-1, keepdims=True) + 1e-05)
    two_ref[...] = (hidden * scale * gain_ref[...]).astype(LOW)


def run_branch(place, entries, parts, tokens, gain):
    sizes = heights(entries)
    pieces = flat(entries)
    depth, wide = sum(sizes[0]), parts[0].shape[-1]
    vmem = pl.BlockSpec(memory_space=FULL)
    return pl.pallas_call(
        functools.partial(branch_kernel, sizes),
        in_specs=[pl.BlockSpec(memory_space=pltpu.SMEM)] + [ANY] * len(pieces) + [vmem] * (len(parts) + 2),
        out_specs=[vmem] * 3,
        out_shape=[
            jax.ShapeDtypeStruct(tokens.shape, WIDE),
            jax.ShapeDtypeStruct(tokens.shape, LOW),
            jax.ShapeDtypeStruct((tokens.shape[0], depth), LOW),
        ],
        scratch_shapes=[
            pltpu.VMEM((len(sizes), depth, wide), LOW),
            pltpu.SemaphoreType.DMA((len(pieces),)),
        ],
        compiler_params=PARAMS,
        cost_estimate=cost(10),
        name="branch",
    )(place, *pieces, *parts, tokens, gain)


def branch_back_kernel(entries, grads, place_ref, *refs):
    n = sum(len(e) for e in entries)
    m = sum(len(e) for e in grads)
    count = len(entries)
    adds, (hidden_ref, cot_ref, gain_ref) = refs[n : n + m], refs[n + m : n + m + 3]
    ghidden_ref, gsum_ref, gbranch_ref, *gout_refs, buf, gout_all, sems = refs[n + m + 3 :]
    copies = fetch(entries, refs[:n], buf, sems)
    place = place_ref[0]
    wide = gbranch_ref.shape[-1]
    total, at = 0.0, 0
    for entry in grads:
        here = [adds[at + i][...].astype(WIDE) for i in range(len(entry))]
        at += len(entry)
        total = total + (jnp.concatenate(here) if len(here) > 1 else here[0])
    hidden = hidden_ref[...]
    scale = lax.rsqrt(jnp.mean(hidden * hidden, axis=-1, keepdims=True) + 1e-05)
    gsum_ref[...] = jnp.sum(total * hidden * scale, axis=0, keepdims=True)
    weighted = total * gain_ref[...]
    back = scale * weighted - hidden * (
        scale * scale * scale * jnp.mean(hidden * weighted, axis=-1, keepdims=True)
    )
    ghidden_ref[...] = cot_ref[...].astype(WIDE) + back

    def spot(b):
        return pl.ds(pl.multiple_of(jnp.bitwise_xor(place, b) * wide, wide), wide)

    for b, mine in enumerate(copies):
        for c in mine:
            c.wait()
        gbranch = ghidden_ref[:, spot(b)].astype(LOW)
        gbranch_ref[b % 2, b // 2] = gbranch
        part = dot(gbranch, buf[b], 1, 1)
        if b == 0:
            gout_all[...] = part
        else:
            gout_all[...] += part
    for b in range(count):
        for i, ref in enumerate(gout_refs):
            length = ref.shape[2]
            ref[b % 2, b // 2] = gout_all[i * length : (i + 1) * length, spot(b)].astype(LOW)


def run_branch_back(place, entries, grads, hidden, cot, gain, seqs):
    sizes, grad_sizes = heights(entries), heights(grads)
    pieces, adds = flat(entries), flat(grads)
    count, depth, wide = len(sizes), sum(sizes[0]), pieces[0].shape[1]
    rows = hidden.shape[0]
    vmem = pl.BlockSpec(memory_space=FULL)
    return pl.pallas_call(
        functools.partial(branch_back_kernel, sizes, grad_sizes),
        in_specs=[pl.BlockSpec(memory_space=pltpu.SMEM)] + [ANY] * len(pieces) + [vmem] * (len(adds) + 3),
        out_specs=[vmem] * (3 + seqs),
        out_shape=[
            jax.ShapeDtypeStruct(hidden.shape, WIDE),
            jax.ShapeDtypeStruct((1, hidden.shape[1]), WIDE),
            jax.ShapeDtypeStruct((2, count // 2, rows, wide), LOW),
        ]
        + [jax.ShapeDtypeStruct((2, count // 2, rows // seqs, wide), LOW)] * seqs,
        scratch_shapes=[
            pltpu.VMEM((count, depth, wide), LOW),
            pltpu.VMEM((rows, depth), WIDE),
            pltpu.SemaphoreType.DMA((len(pieces),)),
        ],
        compiler_params=PARAMS,
        cost_estimate=cost(10),
        name="branch_back",
    )(place, *pieces, *adds, hidden, cot, gain)


def outer_kernel(entries, stacks, *refs):
    n = sum(len(e) for e in entries)
    cols, out_ref, total_ref = refs[n : n + len(stacks)], refs[-2], refs[-1]
    spots = [(ref, i) for ref, size in zip(cols, stacks) for i in range(size)]
    at = 0
    for (ref, i), entry in zip(spots, entries):
        row = 0
        for size in entry:
            part = dot(refs[at][...], ref[i, row : row + size], 0, 0)
            total_ref[...] = part if at == 0 else total_ref[...] + part
            row, at = row + size, at + 1
    out_ref[...] = total_ref[...].astype(LOW)


def run_outer(entries, cols, name):
    pieces = flat(entries)
    shape = (pieces[0].shape[1], cols[0].shape[-1])
    vmem = pl.BlockSpec(memory_space=FULL)
    return pl.pallas_call(
        functools.partial(outer_kernel, heights(entries), [c.shape[0] for c in cols]),
        in_specs=[vmem] * (len(pieces) + len(cols)),
        out_specs=vmem,
        out_shape=jax.ShapeDtypeStruct(shape, LOW),
        scratch_shapes=[pltpu.VMEM(shape, WIDE)],
        compiler_params=PARAMS,
        cost_estimate=cost(8),
        name=name,
    )(*pieces, *cols)


def spread_kernel(entries, layout, place_ref, *refs):
    n = sum(len(e) for e in entries)
    out_ref, held = refs[n:]
    step, steps, at = pl.program_id(0), pl.num_programs(0), 0
    for b, entry in enumerate(entries):
        value = refs[at][...]
        if len(entry) > 1:
            value = jnp.where(step < steps // 2, value, refs[at + 1][...])
        held[jnp.bitwise_xor(place_ref[0], b)] = value
        at += len(entry)
    for i in range(len(entries)):
        for src, width, index in layout(i):
            out_ref[index] = held[i, :, src : src + width].astype(WIDE)


def run_spread(place, entries, piece_block, steps, layout, shape, block, index, name):
    specs = []
    for entry in entries:
        if len(entry) > 1:
            specs.append(pl.BlockSpec(piece_block, lambda g: (jnp.minimum(g, steps // 2 - 1), 0)))
            specs.append(pl.BlockSpec(piece_block, lambda g: (jnp.maximum(g - steps // 2, 0), 0)))
        elif piece_block[0] == entry[0].shape[0]:
            specs.append(pl.BlockSpec(piece_block, lambda g: (0, g)))
        else:
            specs.append(pl.BlockSpec(piece_block, lambda g: (g, 0)))
    return pl.pallas_call(
        functools.partial(spread_kernel, heights(entries), layout),
        grid=(steps,),
        in_specs=[pl.BlockSpec(memory_space=pltpu.SMEM)] + specs,
        out_specs=pl.BlockSpec(block, index),
        out_shape=jax.ShapeDtypeStruct(shape, WIDE),
        scratch_shapes=[pltpu.VMEM((len(entries),) + piece_block, LOW)],
        compiler_params=PARAMS,
        cost_estimate=cost(10),
        name=name,
    )(place, *flat(entries))


def norm_back(values, scale, grad, gain):
    weighted = grad * gain
    return scale * weighted - values * scale**3 * jnp.mean(values * weighted, axis=-1, keepdims=True)


def local(
    tokens,
    cotangent,
    gain_first,
    w_inputs,
    w_conv,
    w_beta,
    gain_heads,
    w_output,
    gain_second,
    w_gate_up,
    w_down,
):
    shards, count, place = lax.axis_size("fsdp"), lax.axis_size("seq"), lax.axis_index("seq")
    shard = lax.axis_index("fsdp")
    seqs, length, width = tokens.shape
    rows = seqs * length
    part = width // shards
    all_heads = w_beta.shape[1]
    heads = all_heads // count
    wide = heads * (w_output.shape[0] * shards // all_heads)
    dim = wide // heads
    hidden_part = w_down.shape[0]
    piece = hidden_part // count
    taps = w_conv.shape[1]
    place_arr = jnp.reshape(place, (1,)).astype(jnp.int32)

    def over_shards(x, axis=0):
        return lax.all_gather(x, "fsdp", axis=axis, tiled=True)

    packed = jnp.concatenate(
        [
            gain_first[None],
            gain_second[None],
            jnp.pad(gain_heads[None], ((0, 0), (0, part - gain_heads.shape[0]))),
            w_conv.reshape(3 * taps, part),
            w_beta.T,
        ]
    )
    packed = lax.all_gather(packed, "fsdp", axis=0)
    first_weight = packed[:, 0].reshape(width).astype(WIDE)
    second_weight = packed[:, 1].reshape(width).astype(WIDE)
    head_weight = packed[:, 2, : gain_heads.shape[0]].reshape(1, dim).astype(WIDE)
    conv_all = packed[:, 3 : 3 + 3 * taps].transpose(1, 0, 2).reshape(3, taps, width)
    conv_own = lax.dynamic_slice_in_dim(conv_all, place * wide, wide, 2).astype(WIDE)
    conv_own = conv_own.reshape(3, taps, heads, dim).transpose(2, 0, 1, 3)
    beta_all = packed[:, 3 + 3 * taps :].transpose(1, 0, 2).reshape(all_heads, width)
    beta_own = lax.dynamic_slice_in_dim(beta_all, place * heads, heads, 0)
    beta_own = jnp.pad(beta_own, ((0, 128 - heads), (0, 0)))

    ff = piece * shards
    win = lax.dynamic_slice_in_dim(w_inputs, place * wide, wide, 2)
    win = win.reshape(3, part, heads, dim).transpose(1, 2, 0, 3).reshape(part, 3 * wide)
    wio = jnp.concatenate([win, lax.dynamic_slice_in_dim(w_output, place * wide, wide, 1)], axis=1)
    later = after(place, wio)
    pieces = [
        lax.dynamic_slice(w_gate_up, (0, 0, f * hidden_part + later * piece), (2, part, piece)) for f in range(shards)
    ]
    wgu_own = jnp.concatenate([p[c] for c in range(2) for p in pieces], axis=1)
    later = after(later, wgu_own)
    wdown_own = lax.dynamic_slice_in_dim(w_down, later * piece, piece, 0)
    wio = over_shards(wio)
    wgu = over_shards(wgu_own)
    wdown = over_shards(wdown_own)

    inputs = tokens.reshape(rows, width).astype(WIDE)
    first_scale = lax.rsqrt(jnp.mean(inputs * inputs, axis=-1, keepdims=True) + 1e-05)
    normed = (inputs * first_scale * first_weight).astype(LOW)
    cot_own = cotangent.reshape(rows, width)
    cot_first = gather_start(cot_own)
    normed_first = gather_start(after(normed, wgu_own, wdown_own, *cot_first))
    normed_far = gather_far(normed_first)
    normed_parts = gather_rest(normed_first, normed_far)
    cot_far = gather_far([after(c, *normed_far) for c in cot_first])
    cot_parts = gather_rest(cot_first, cot_far)

    wio_late = after(wio, *cot_far)
    proj, logits, normed_all = run_project(normed_parts, wio_late, beta_own, 3 * wide)
    wout_first = gather_start(wio[:, 3 * wide :])
    proj = proj.reshape(count, seqs, length, 3 * wide)
    logits = logits.reshape(count, seqs, length, 128)
    wout_far, out_parts, saved = [], [], []
    for b in range(seqs):
        late = [after(proj, *wout_first), after(proj, *wout_far)][min(b - 1, 1)] if b else proj
        mixed_out, *kept = run_mixer_forward(b, place_arr, late, conv_own, logits, head_weight)
        saved.append(kept)
        if b == 0:
            wout_far = gather_far(wout_first)
        if b == seqs - 1:
            mixed_out = after(mixed_out, *wout_far)
        out_parts += exchange_xor(mixed_out)
    wout_parts = gather_rest(wout_first, wout_far)
    hidden, normed_two, out_rows = run_branch(
        place_arr, wout_parts, out_parts, tokens.reshape(rows, width), second_weight[None]
    )
    two_parts = gather_xor(normed_two)
    inner, up_slope, gate_slope, two_all, cot_all = run_gate(two_parts, cot_parts, wgu)

    def to_owner(partial):
        return lax.psum_scatter(partial, "fsdp", scatter_dimension=0, tiled=True)

    out_first = gather_start(after(out_rows, inner))
    inner_late = after(inner, wdown)
    gwdown = jnp.einsum("brf,brd->fd", inner_late, cot_all, preferred_element_type=WIDE).astype(LOW)
    up_slope, gwdown = lax.optimization_barrier((up_slope, gwdown, *out_first))[:2]
    gwdown = to_owner(gwdown)

    ggu, gtwo_even, gtwo_odd = run_gate_back(cot_all, up_slope, gate_slope, wdown, wgu)
    gtwo_twin = reduce_start(gtwo_odd)
    out_far = gather_far(out_first)
    ggu = after(ggu, *out_far)
    gwgu = jnp.einsum("brd,brf->df", two_all, ggu, preferred_element_type=WIDE).astype(LOW)
    gtwo_even, gwgu = lax.optimization_barrier((gtwo_even, gwgu))
    gtwo_state = reduce_far(gtwo_even, gtwo_twin)
    down_even, down_odd = run_pairs([(after(inner, gwgu), wdown, 0)], width, "down")
    gwgu = to_owner(after(gwgu, gwdown))
    gtwo_parts = reduce_last(gtwo_state)
    hidden_late = after(hidden, down_odd)

    ghidden, gsecond, gbranch, *gouts = run_branch_back(
        place_arr, wout_parts, gtwo_parts, hidden_late, cot_own, second_weight[None], seqs
    )
    gouts = [exchange_xor(g) for g in gouts]
    gwdown_first = gather_start(after(gwdown, ghidden))
    gwdown_far = gather_far(gwdown_first)
    down_twin = reduce_start(after(down_odd, ghidden))
    held, gtaps, ggain = None, [], []
    for b in range(seqs):
        gout = gouts[b]
        if b == seqs - 1:
            gout[0] = after(gout[0], *gwdown_first)
        *held, gtap, ghead = run_mixer_backward(
            b, place_arr, proj, conv_own, logits, head_weight, gout, saved[b], held
        )
        gtaps.append(gtap)
        ggain.append(ghead)
    gproj, glogit = held
    gproj = after(gproj, *gwdown_far, gwgu, down_twin)
    gproj = gproj.reshape(count, rows, 3 * wide)
    glogit = glogit.reshape(count, rows, 128)
    gwin = jnp.einsum("brd,bre->de", normed_all, gproj, preferred_element_type=WIDE).astype(LOW)
    down_state = reduce_far(down_even, down_twin)
    gbranch_cols = exchange_xor(after(gbranch, gouts[-1][-1]))
    gproj, gwin = lax.optimization_barrier((gproj, gwin, *down_state, *gbranch_cols))[:2]
    gwin = to_owner(gwin)
    gnormed_even, gnormed_odd = run_pairs([(gproj, wio, 1), (glogit, beta_own, 0)], width, "input_back")
    gnormed_twin = reduce_start(gnormed_odd)
    down = reduce_last(down_state)
    output = (hidden + sum(jnp.concatenate(e).astype(WIDE) for e in down)).astype(LOW)
    gnormed_state = reduce_far(gnormed_even, after(gnormed_twin, output))
    out_all_parts = gather_rest(out_first, out_far)
    gwout = run_outer(out_all_parts, [after(gbranch_cols[0], *gnormed_twin)] + gbranch_cols[1:], "output_weights")
    gnormed_state[0], gwout = lax.optimization_barrier((gnormed_state[0], gwout))
    gnormed = reduce_last(gnormed_state)
    gwgu_first = gather_start(after(gwgu, *gnormed_state[4:]))
    gwdown_parts = gather_rest(gwdown_first, gwdown_far)
    gnormed[0][0], gwin, *_ = lax.optimization_barrier((gnormed[0][0], gwin, *gwgu_first))
    gwout = to_owner(after(gwout, gwin))

    gnormed = sum(jnp.concatenate(e).astype(WIDE) for e in gnormed)
    input_grad = ghidden + norm_back(inputs, first_scale, gnormed, first_weight)
    gfirst = jnp.sum(gnormed * inputs * first_scale, axis=0)
    gtaps, ggain = sum(gtaps), sum(ggain)

    lanes = min(256, width)
    gwdown = run_spread(
        place_arr,
        gwdown_parts,
        (piece, lanes),
        width // lanes,
        lambda i: [(0, lanes, (slice(i * piece, (i + 1) * piece), slice(None)))],
        (hidden_part, width),
        (hidden_part, lanes),
        lambda g: (0, g),
        "spread_down",
    )
    tall = min(64, part)
    gwgu_far = gather_far([after(g, gwdown) for g in gwgu_first])
    gwgu_parts = gather_rest(gwgu_first, gwgu_far)
    gwin_first = gather_start(after(gwin, *gwgu_far))
    gwgu = run_spread(
        place_arr,
        gwgu_parts,
        (tall, 2 * ff),
        part // tall,
        lambda i: [
            (
                c * ff + f * piece,
                piece,
                (c, slice(None), slice(f * hidden_part + i * piece, f * hidden_part + (i + 1) * piece)),
            )
            for c in range(2)
            for f in range(shards)
        ],
        (2, part, hidden_part * shards),
        (2, tall, hidden_part * shards),
        lambda g: (0, g, 0),
        "spread_gate_up",
    )
    gwin_far = gather_far([after(g, gwgu) for g in gwin_first])
    gwin_parts = gather_rest(gwin_first, gwin_far)
    gwout_parts = gather_xor(after(gwout, *gwin_far))
    gwin = run_spread(
        place_arr,
        gwin_parts,
        (tall, 3 * wide),
        part // tall,
        lambda i: [
            (
                (h * 3 + c) * dim,
                dim,
                (c, slice(None), slice((i * heads + h) * dim, (i * heads + h + 1) * dim)),
            )
            for c in range(3)
            for h in range(heads)
        ],
        (3, part, width),
        (3, tall, width),
        lambda g: (0, g, 0),
        "spread_inputs",
    )
    gwout = run_spread(
        after(place_arr, gwin),
        gwout_parts,
        (tall, wide),
        part // tall,
        lambda i: [(0, wide, (slice(None), slice(i * wide, (i + 1) * wide)))],
        (part, width),
        (tall, width),
        lambda g: (g, 0),
        "spread_output",
    )

    gbeta = jnp.einsum("brh,brd->hd", glogit, normed_all, preferred_element_type=WIDE)[:heads]
    gtaps = gtaps.transpose(1, 2, 0, 3).reshape(3 * taps, wide)
    ggain = jnp.pad(jnp.sum(ggain, axis=0), ((0, 0), (0, width - dim)))
    small = sum_over("fsdp", jnp.concatenate([gsecond, ggain, gbeta]))
    gbeta = lax.dynamic_update_slice(
        jnp.zeros((all_heads, width), WIDE), small[2:], (place * heads, 0)
    )
    gtaps = lax.dynamic_update_slice(
        jnp.zeros((3 * taps, width), WIDE), sum_over("fsdp", gtaps), (0, place * wide)
    )
    small = sum_over("seq", jnp.concatenate([small[:2], gtaps, gbeta]))
    own = lax.dynamic_slice_in_dim(small, shard * part, part, 1)
    gfirst = lax.dynamic_slice_in_dim(sum_over("fsdp", sum_over("seq", gfirst[None])), shard * part, part, 1)
    ggain = lax.dynamic_slice_in_dim(small[1], shard * (dim // shards), dim // shards, 0)
    return (
        output.reshape(tokens.shape),
        input_grad.reshape(tokens.shape),
        gfirst[0],
        gwin,
        own[2 : 2 + 3 * taps].reshape(3, taps, part),
        own[2 + 3 * taps :].T,
        ggain,
        gwout,
        own[0],
        gwgu,
        gwdown,
    )


def solution(mesh):
    in_specs = (
        P("fsdp", "seq", None),
        P("fsdp", "seq", None),
        P("fsdp"),
        P(None, "fsdp", None),
        P(None, None, "fsdp"),
        P("fsdp", None),
        P("fsdp"),
        P("fsdp", None),
        P("fsdp"),
        P(None, "fsdp", None),
        P("fsdp", None),
    )
    out_specs = (
        P("fsdp", "seq", None),
        P("fsdp", "seq", None),
        P("fsdp"),
        P(None, "fsdp", None),
        P(None, None, "fsdp"),
        P("fsdp", None),
        P("fsdp"),
        P("fsdp", None),
        P("fsdp"),
        P(None, "fsdp", None),
        P("fsdp", None),
    )
    return jax.shard_map(local, mesh=mesh, in_specs=in_specs, out_specs=out_specs, check_vma=False)
```

time: 4600 us -> 765 us (0.17)
  waiting for transfers between devices: 2160 us -> 257 us
  other arithmetic: 1410 us -> 40.8 us
  matrix products: 496 us -> 46 us
  local copies, waits for them, and re-layouts: 314 us -> 67.4 us
  Pallas kernels: 0 us -> 217 us
  blocking collectives: 132 us -> 15 us
  starting transfers between devices: 20.9 us -> 98.4 us
    all_gather x12 -> x3, waiting for transfers between devices: 1750 us -> 0.02 us  [over_shards(): return lax.all_gather(x, 'fsdp', axis=axis, tiled=True)]
    another operation x43 -> x0, other arithmetic: 1280 us -> none  [the longest x20 640 us: block_step(): lax.linalg.triangular_solve(lower_mat, strength[..., None] * key_rows, le...]
    dot_general x100 -> x4, matrix products: 435 us -> 46 us  [the longest x1 19.3 us: local(): jnp.einsum('brd,brf->df', two_all, ggu, preferred_element_type=WIDE)]
    ppermute x2 -> x132, waiting for transfers between devices: 0.91 us -> 257 us  [the longest x120 254 us: swap(): return lax.ppermute(x, 'seq', [(i, i ^ bits) for i in range(count)])]
    psum x1 -> x0, waiting for transfers between devices: 219 us -> none  [local(): lax.psum(in_part.astype(jnp.bfloat16), 'seq').astype(jnp.float32)]
    pallas_call x0 -> x16, Pallas kernels: none -> 217 us  [the longest x4 39.6 us: run_spread(): pl.pallas_call(functools.partial(spread_kernel, heights(entries), layout)...]
    all_to_all x4 -> x0, waiting for transfers between devices: 184 us -> none  [the longest x1 157 us: local(): lax.all_to_all(inner_act.reshape(row_count, -1), 'fsdp', split_axis=1, co...]
    ppermute x2 -> x132, starting transfers between devices: 3.26 us -> 96.8 us  [the longest x120 84.2 us: swap(): return lax.ppermute(x, 'seq', [(i, i ^ bits) for i in range(count)])]
  transfers between devices with their start and end apart: 20 -> 139, of which waited for: 13 -> 52; matrix products, arithmetic and copies ran while one was open for 38% -> 19% of each run, Pallas kernels for 0% -> 26%
where the time goes in v1:
time: 765 us; the launch traced here: 758 us
  waiting for transfers between devices  257 us (34%)
  Pallas kernels  217 us (28%)
  starting transfers between devices  98.4 us (13%)
  local copies, waits for them, and re-layouts  67.4 us (9%)
  matrix products  46 us (6%)
  other arithmetic  40.8 us (5%)
  between operations  16.2 us (2%)
  blocking collectives  15 us (2%)
    ppermute x120, waiting for transfers between devices, swap(): return lax.ppermute(x, 'seq', [(i, i ^ bits) for i in range(count)])  254 us
    ppermute x120, starting transfers between devices, swap(): return lax.ppermute(x, 'seq', [(i, i ^ bits) for i in range(count)])  84.2 us
    pallas_call x4, Pallas kernels, run_spread(): pl.pallas_call(functools.partial(spread_kernel, heights(entries), layout)...  39.6 us
    pallas_call x1, Pallas kernels, run_gate_back(): pl.pallas_call(gate_back_kernel, grid=(count // 2,), in_specs=[block(widt...  32.2 us
    pallas_call x2, Pallas kernels, run_mixer_backward(): pl.pallas_call(functools.partial(mixer_backward, sizes), out_shape=shapes...  29.8 us
    pallas_call x1, Pallas kernels, run_gate(): pl.pallas_call(functools.partial(gate_kernel, sizes, heights(others)), in...  26.4 us
    pallas_call x2, Pallas kernels, run_pairs(): pl.pallas_call(functools.partial(pairs_kernel, len(terms), [t[2] for t in...  23.5 us
    pallas_call x2, Pallas kernels, run_mixer_forward(): pl.pallas_call(mixer_forward, out_shape=shapes, grid_spec=pltpu.PrefetchS...  22.1 us
  transfers between devices with their start and end apart: 139, of which 52 were waited for; matrix products, arithmetic and copies ran while one was open for 19% of the time, Pallas kernels for 26%

profile of v1, /device:TPU:0, one launch (start us, length us, event | category | flops | bytes accessed | tf_op | source)
XLA Modules:
  0.0 758.3 jit_solution(10682010407084869969)
XLA Ops:
  22.7 15.0 %all-gather.1 = bf16[4,31,512]{2,1,0:T(8,128)(2,1)S(1)} all-gather(bf16[1,31,512]{2,1,0:T(8,128)(2,1)S(1)} %bitcast.220), channel_id=2, replica_groups=mesh['fsdp'=4,'seq'=8] {'fsdp'}, dimensions={0}, use_global_device_ids=true | all-gather | bytes 158720 | tf_op jit(solution)/shard_map/all_gather | solution.py:808
  40.2 4.1 collective-permute-done.10.refs_12_
  47.9 22.4 %collective-permute-done.15.refs_4_ = bf16[256,2048]{1,0:T(8,128)(2,1)} collective-permute-done((bf16[256,2048]{1,0:T(8,128)(2,1)S(1)}, bf16[256,2048]{1,0:T(8,128)(2,1)}, u32[]{:S(2)}, u32[]{:S(2)}) %collective-permute-start.15) | collective-permute-done | bytes 1048608 | tf_op jit(solution)/shard_map/ppermute | solution.py:16
  74.8 9.0 %collective-permute-done.17.refs_6_ = bf16[128,2048]{1,0:T(8,128)(2,1)S(1)} collective-permute-done((bf16[128,2048]{1,0:T(8,128)(2,1)S(1)}, bf16[128,2048]{1,0:T(8,128)(2,1)S(1)}, u32[]{:S(2)}, u32[]{:S(2)}) %collective-permute-start.17) | collective-permute-done | bytes 524320 | tf_op jit(solution)/shard_map/ppermute | solution.py:16
  90.1 8.1 %collective-permute-done.21.refs_16_ = bf16[128,2048]{1,0:T(8,128)(2,1)} collective-permute-done((bf16[128,2048]{1,0:T(8,128)(2,1)S(1)}, bf16[128,2048]{1,0:T(8,128)(2,1)}, u32[]{:S(2)}, u32[]{:S(2)}) %collective-permute-start.21) | collective-permute-done | bytes 524320 | tf_op jit(solution)/shard_map/ppermute | solution.py:16
  106.1 15.7 %project.1 = (bf16[8,256,768]{2,1,0:T(8,128)(2,1)}, f32[8,256,128]{2,1,0:T(8,128)}, bf16[8,256,2048]{2,1,0:T(8,128)(2,1)}) custom-call(bf16[256,2048]{1,0:T(8,128)(2,1)} %copy-done.12, bf16[256,2048]{1,0:T(8,128)(2,1)} %collective-permute-done.12.refs_1_, bf16[256,2048]{1,0:T(8,128)(2,1)} %collective-permute-done.13.refs_2_, ...), custom_call_target="tpu_custom_call" | custom-call | flops 8000000000 | tf_op jit(solution)/shard_map/project/pallas_call | solution.py:425
  121.9 11.2 %mixer_forward.2 = (bf16[2,4,128,256]{3,2,1,0:T(8,128)(2,1)}, f32[1,2,8,128,128]{4,3,2,1,0:T(8,128)}, bf16[1,2,8,128,128]{4,3,2,1,0:T(8,128)(2,1)}, bf16[1,2,8,1...) custom-call(s32[1]{0:T(128)} %bitcast.place_ref, ...), custom_call_target="tpu_custom_call" | custom-call | flops 5000000000 | tf_op jit(solution)/shard_map/mixer_forward/pallas_call | solution.py:323
  141.8 10.9 %mixer_forward.3 = (bf16[2,4,128,256]{3,2,1,0:T(8,128)(2,1)}, f32[1,2,8,128,128]{4,3,2,1,0:T(8,128)}, bf16[1,2,8,128,128]{4,3,2,1,0:T(8,128)(2,1)}, bf16[1,2,8,1...) custom-call(s32[1]{0:T(128)} %bitcast.place_ref, ...), custom_call_target="tpu_custom_call" | custom-call | flops 5000000000 | tf_op jit(solution)/shard_map/mixer_forward/pallas_call | solution.py:323
  159.9 4.2 collective-permute-done.26.refs_14_
  165.5 3.7 collective-permute-done.28.refs_17_
  170.5 3.7 collective-permute-done.29.refs_18_
  181.1 10.9 %branch.1 = (f32[256,2048]{1,0:T(8,128)}, bf16[256,2048]{1,0:T(8,128)(2,1)}, bf16[256,2048]{1,0:T(8,128)(2,1)}) custom-call(s32[1]{0:T(128)} %bitcast.place_ref, bf16[2048,256]{1,0:T(8,128)(2,1)} %copy-done.10, bf16[2048,256]{1,0:T(8,128)(2,1)} %collective-permute-done.refs_1_, bf16[2048,256]{1,0:T(8,128)(2,1)} %copy-done.26, bf16[2048,256]{1,0:T(8,128)(2,1)} %copy-done.47, ...), custom_call_target="tpu_custom_call" | custom-call | flops 5000000000 | tf_op jit(solution)/shard_map/branch/pallas_call | solution.py:608
  194.6 20.3 %collective-permute-done.34.refs_4_ = bf16[256,2048]{1,0:T(8,128)(2,1)S(1)} collective-permute-done((bf16[256,2048]{1,0:T(8,128)(2,1)}, bf16[256,2048]{1,0:T(8,128)(2,1)S(1)}, u32[]{:S(2)}, u32[]{:S(2)}) %collective-permute-start.34) | collective-permute-done | bytes 1048608 | tf_op jit(solution)/shard_map/ppermute | solution.py:16
  219.9 11.6 %collective-permute-done.36.refs_6_ = bf16[128,2048]{1,0:T(8,128)(2,1)} collective-permute-done((bf16[128,2048]{1,0:T(8,128)(2,1)S(1)}, bf16[128,2048]{1,0:T(8,128)(2,1)}, u32[]{:S(2)}, u32[]{:S(2)}) %collective-permute-start.36) | collective-permute-done | bytes 524320 | tf_op jit(solution)/shard_map/ppermute | solution.py:16
  235.7 26.4 %gate.1 = (bf16[8,256,704]{2,1,0:T(8,128)(2,1)}, bf16[8,256,704]{2,1,0:T(8,128)(2,1)}, bf16[8,256,704]{2,1,0:T(8,128)(2,1)}, bf16[8,256,2048]{2,1,0:T(8,128)(2,1)}, bf16[8,256,2048]{2,1,0:T(8,128)(2,1)}) custom-call(bf16[256,2048]{1,0:T(8,128)(2,1)} %get-tuple-element.106.refs_0_, bf16[256,2048]{1,0:T(8,128)(2,1)} %collective-permute-done.31.refs_1_, ...), custom_call_target="tpu_custom_call" | custom-call | flops 12499999744 | tf_op jit(solution)/shard_map/gate/pallas_call | solution.py:488
  264.3 10.7 %bitcast_convert_fusion.2 = bf16[704,2048]{1,0:T(8,128)(2,1)} fusion(bf16[8,256,704]{2,1,0:T(8,128)(2,1)} %get-tuple-element.120.refs_0_, bf16[8,256,2048]{2,1,0:T(8,128)(2,1)} %get-tuple-element.108.cot_ref), kind=kOutput, calls=%fused_computation.2 | convolution fusion | flops 5907021824 | bytes 14155776 | tf_op jit(solution)/shard_map/brf,brd->fd/dot_general | solution.py:872
  275.0 13.0 %collective-permute-done.45.refs_2_ = bf16[256,2048]{1,0:T(8,128)(2,1)S(1)} collective-permute-done((bf16[256,2048]{1,0:T(8,128)(2,1)}, bf16[256,2048]{1,0:T(8,128)(2,1)S(1)}, u32[]{:S(2)}, u32[]{:S(2)}) %collective-permute-start.45) | collective-permute-done | bytes 1048608 | tf_op jit(solution)/shard_map/ppermute | solution.py:16
  289.2 32.2 %gate_back.1 = (bf16[8,256,1408]{2,1,0:T(8,128)(2,1)}, bf16[4,256,2048]{2,1,0:T(8,128)(2,1)}, bf16[4,256,2048]{2,1,0:T(8,128)(2,1)}) custom-call(bf16[8,256,2048]{2,1,0:T(8,128)(2,1)} %get-tuple-element.108.cot_ref, bf16[8,256,704]{2,1,0:T(8,128)(2,1)} %get-tuple-element.113.up_ref, bf16[8,256,704]{2,1,0:T(8,128)(2,1)} %get-tuple-element.114.gate_ref, ...), custom_call_target="tpu_custom_call" | custom-call | flops 16000000000 | tf_op jit(solution)/shard_map/gate_back/pallas_call | solution.py:530
  323.9 11.9 %collective-permute-done.47.refs_6_ = bf16[128,2048]{1,0:T(8,128)(2,1)S(1)} collective-permute-done((bf16[128,2048]{1,0:T(8,128)(2,1)S(1)}, bf16[128,2048]{1,0:T(8,128)(2,1)S(1)}, u32[]{:S(2)}, u32[]{:S(2)}) %collective-permute-start.47) | collective-permute-done | bytes 524320 | tf_op jit(solution)/shard_map/ppermute | solution.py:16
  336.6 19.3 %bitcast_convert_fusion = bf16[2048,1408]{1,0:T(8,128)(2,1)} fusion(bf16[8,256,2048]{2,1,0:T(8,128)(2,1)} %get-tuple-element.116, bf16[8,256,1408]{2,1,0:T(8,128)(2,1)} %get-tuple-element.118), kind=kOutput, calls=%fused_computation | convolution fusion | flops 11814043648 | bytes 19922944 | tf_op jit(solution)/shard_map/brd,brf->df/dot_general | solution.py:880
  356.4 10.6 %down.1 = (bf16[4,256,2048]{2,1,0:T(8,128)(2,1)}, bf16[4,256,2048]{2,1,0:T(8,128)(2,1)}) custom-call(bf16[8,256,704]{2,1,0:T(8,128)(2,1)} %get-tuple-element.120.refs_0_, bf16[704,2048]{1,0:T(8,128)(2,1)} %all-gather.10.cloned.1.call-done.down_ref.refs_1_), custom_call_target="tpu_custom_call" | custom-call | flops 6000000000 | tf_op jit(solution)/shard_map/down/pallas_call | solution.py:561
  366.9 4.3 add_convert_fusion.7
  375.6 10.6 %collective-permute-done.51 = bf16[128,2048]{1,0:T(8,128)(2,1)S(1)} collective-permute-done((bf16[128,2048]{1,0:T(8,128)(2,1)S(1)}, bf16[128,2048]{1,0:T(8,128)(2,1)S(1)}, u32[]{:S(2)}, u32[]{:S(2)}) %collective-permute-start.51) | collective-permute-done | bytes 524320 | tf_op jit(solution)/shard_map/ppermute | solution.py:16
  387.4 11.4 %collective-permute-done.53 = bf16[128,2048]{1,0:T(8,128)(2,1)S(1)} collective-permute-done((bf16[128,2048]{1,0:T(8,128)(2,1)S(1)}, bf16[128,2048]{1,0:T(8,128)(2,1)S(1)}, u32[]{:S(2)}, u32[]{:S(2)}) %collective-permute-start.53) | collective-permute-done | bytes 524320 | tf_op jit(solution)/shard_map/ppermute | solution.py:16
  404.4 3.9 collective-permute-done.52.refs_13_
  410.3 9.7 %branch_back.1 = (f32[256,2048]{1,0:T(8,128)}, f32[1,2048]{1,0:T(1,128)}, bf16[2,4,256,256]{3,2,1,0:T(8,128)(2,1)}, bf16[2,4,128,256]{3,2,1,0:T(8,128)(2,1)}, bf16[2,4,128,256]{3,2,1,0:T(8,128)(2,1)}) custom-call(s32[1]{0:T(128)} %bitcast.place_ref, bf16[2048,256]{1,0:T(8,128)(2,1)} %copy-done.10, bf16[2048,256]{1,0:T(8,128)(2,1)} %collective-permute-done.refs_1_, ...), custom_call_target="tpu_custom_call" | custom-call | flops 5000000000 | tf_op jit(solution)/shard_map/branch_back/pallas_call | solution.py:675
  441.0 14.8 %mixer_backward.2 = (bf16[8,2,128,768]{3,2,1,0:T(8,128)(2,1)}, bf16[8,2,128,128]{3,2,1,0:T(8,128)(2,1)}, f32[2,3,4,128]{3,2,1,0:T(4,128)}, f32[2,1,128]{2,1,0:T(1,128)}) custom-call(s32[1]{0:T(128)} %bitcast.place_ref, bf16[8,2,128,768]{3,2,1,0:T(8,128)(2,1)} %bitcast.242, f32[2,3,4,128]{3,2,1,0:T(4,128)} %copy_bitcast_fusion.taps_ref, ...), custom_call_target="tpu_custom_call" | custom-call | flops 6499999744 | tf_op jit(solution)/shard_map/mixer_backward/pallas_call | solution.py:355
  462.2 12.8 %collective-permute-done.64.refs_2_ = bf16[176,2048]{1,0:T(8,128)(2,1)} collective-permute-done((bf16[176,2048]{1,0:T(8,128)(2,1)S(1)}, bf16[176,2048]{1,0:T(8,128)(2,1)}, u32[]{:S(2)}, u32[]{:S(2)}) %collective-permute-start.64) | collective-permute-done | bytes 720928 | tf_op jit(solution)/shard_map/ppermute | solution.py:16
  480.6 15.0 %mixer_backward.3 = (bf16[8,2,128,768]{3,2,1,0:T(8,128)(2,1)}, bf16[8,2,128,128]{3,2,1,0:T(8,128)(2,1)}, f32[2,3,4,128]{3,2,1,0:T(4,128)}, f32[2,1,128]{2,1,0:T(1,128)}) custom-call(s32[1]{0:T(128)} %bitcast.place_ref, bf16[8,2,128,768]{3,2,1,0:T(8,128)(2,1)} %bitcast.243, ...), custom_call_target="tpu_custom_call", output_to_operand_aliasing={{0}: (15, {}), {1}: (16, {})} | custom-call | flops 6499999744 | tf_op jit(solution)/shard_map/mixer_backward/pallas_call | solution.py:355
  506.4 11.4 %bitcast_convert_fusion.1 = bf16[2048,768]{1,0:T(8,128)(2,1)} fusion(bf16[8,256,2048]{2,1,0:T(8,128)(2,1)} %get-tuple-element.148, bf16[8,256,768]{2,1,0:T(8,128)(2,1)} %bitcast.244), kind=kOutput, calls=%fused_computation.1 | convolution fusion | flops 6444023808 | bytes 14680064 | tf_op jit(solution)/shard_map/brd,bre->de/dot_general | solution.py:909
  518.1 3.6 collective-permute-done.62
  521.8 4.4 collective-permute-done.60
  526.2 12.9 %input_back.1 = (bf16[4,256,2048]{2,1,0:T(8,128)(2,1)}, bf16[4,256,2048]{2,1,0:T(8,128)(2,1)}) custom-call(bf16[8,256,768]{2,1,0:T(8,128)(2,1)} %bitcast.245, bf16[8,256,128]{2,1,0:T(8,128)(2,1)} %bitcast.215, bf16[2048,1024]{1,0:T(8,128)(2,1)} %all-gather.6.cloned.1.call-done.refs_10_.refs_2_, bf16[128,2048]{1,0:T(8,128)(2,1)} %pad.13.refs_11_.refs_3_), custom_call_target="tpu_custom_call" | custom-call | flops 6000000000 | tf_op jit(solution)/shard_map/input_back/pallas_call | solution.py:561
  539.8 4.7 convolution_bitcast_fusion
  551.0 10.1 %collective-permute-done.59 = bf16[128,2048]{1,0:T(8,128)(2,1)} collective-permute-done((bf16[128,2048]{1,0:T(8,128)(2,1)}, bf16[128,2048]{1,0:T(8,128)(2,1)}, u32[]{:S(2)}, u32[]{:S(2)}) %collective-permute-start.59) | collective-permute-done | bytes 524320 | tf_op jit(solution)/shard_map/ppermute | solution.py:16
  564.6 4.5 add_convert_fusion.3
  575.3 12.2 %collective-permute-done.85 = bf16[128,2048]{1,0:T(8,128)(2,1)} collective-permute-done((bf16[128,2048]{1,0:T(8,128)(2,1)S(1)}, bf16[128,2048]{1,0:T(8,128)(2,1)}, u32[]{:S(2)}, u32[]{:S(2)}) %collective-permute-start.85) | collective-permute-done | bytes 524320 | tf_op jit(solution)/shard_map/ppermute | solution.py:16
  588.1 8.5 %collective-permute-done.87 = bf16[128,2048]{1,0:T(8,128)(2,1)S(1)} collective-permute-done((bf16[128,2048]{1,0:T(8,128)(2,1)S(1)}, bf16[128,2048]{1,0:T(8,128)(2,1)S(1)}, u32[]{:S(2)}, u32[]{:S(2)}) %collective-permute-start.87) | collective-permute-done | bytes 524320 | tf_op jit(solution)/shard_map/ppermute | solution.py:16
  603.6 7.6 output_weights.1
  614.9 9.2 %spread_down.1 = f32[1408,2048]{1,0:T(8,128)} custom-call(s32[1]{0:T(128)} %bitcast.place_ref, bf16[176,2048]{1,0:T(8,128)(2,1)} %reduce-scatter.5.cloned.1.call-done.refs_0_, bf16[176,2048]{1,0:T(8,128)(2,1)} %copy-done.52, bf16[176,2048]{1,0:T(8,128)(2,1)} %collective-permute-done.64.refs_2_, bf16[176,2048]{1,0:T(8,128)(2,1)} %collective-permute-done.98.refs_3_, ...), custom_call_target="tpu_custom_call" | custom-call | flops 5000000000 | tf_op jit(solution)/shard_map/spread_down/pallas_call | solution.py:751
  624.0 12.6 %collective-permute-done.90.refs_4_ = bf16[512,1408]{1,0:T(8,128)(2,1)} collective-permute-done((bf16[512,1408]{1,0:T(8,128)(2,1)}, bf16[512,1408]{1,0:T(8,128)(2,1)}, u32[]{:S(2)}, u32[]{:S(2)}) %collective-permute-start.90) | collective-permute-done | bytes 1441824 | tf_op jit(solution)/shard_map/ppermute | solution.py:16
  645.7 12.3 %collective-permute-done.101.refs_6_ = bf16[256,1408]{1,0:T(8,128)(2,1)} collective-permute-done((bf16[256,1408]{1,0:T(8,128)(2,1)}, bf16[256,1408]{1,0:T(8,128)(2,1)}, u32[]{:S(2)}, u32[]{:S(2)}) %collective-permute-start.101) | collective-permute-done | bytes 720928 | tf_op jit(solution)/shard_map/ppermute | solution.py:16
  670.9 14.9 %spread_gate_up.1 = f32[2,512,5632]{2,1,0:T(8,128)} custom-call(s32[1]{0:T(128)} %bitcast.place_ref, bf16[512,1408]{1,0:T(8,128)(2,1)} %reduce-scatter.7.cloned.1.call-done.refs_0_, bf16[512,1408]{1,0:T(8,128)(2,1)} %collective-permute-done.88.refs_1_, bf16[512,1408]{1,0:T(8,128)(2,1)} %collective-permute-done.89.refs_2_, ...), custom_call_target="tpu_custom_call" | custom-call | flops 5000000000 | tf_op jit(solution)/shard_map/spread_gate_up/pallas_call | solution.py:751
  694.6 3.5 fusion.7
  703.4 4.0 collective-permute-done.113.refs_7_
  727.7 4.5 fusion.4
  733.9 9.4 %spread_inputs.1 = f32[3,512,2048]{2,1,0:T(8,128)} custom-call(s32[1]{0:T(128)} %bitcast.place_ref, bf16[512,768]{1,0:T(8,128)(2,1)} %reduce-scatter.9.cloned.1.call-done.refs_0_, bf16[512,768]{1,0:T(8,128)(2,1)} %collective-permute-done.103.refs_1_, bf16[512,768]{1,0:T(8,128)(2,1)} %collective-permute-done.104.refs_2_, ...), custom_call_target="tpu_custom_call" | custom-call | flops 5000000000 | tf_op jit(solution)/shard_map/spread_inputs/pallas_call | solution.py:751
  744.9 6.1 spread_output.1
  (565 shorter events, 228.4 us)
Async XLA Ops:
  7.2 94.0 %all-gather.6.cloned.1.call-start = ((), (), s32[]{:S(2)}) async-start(), calls=%async_computation.4 | async-start | bytes 5242880 | tf_op jit(solution)/shard_map/all_gather | solution.py:797
  11.8 221.0 %all-gather.8.cloned.1.call-start = ((), (), s32[]{:S(2)}) async-start(), calls=%async_computation.5 | async-start | bytes 7208960 | tf_op jit(solution)/shard_map/all_gather | solution.py:797
  17.2 247.1 %all-gather.10.cloned.1.call-start = ((), (), s32[]{:S(2)}) async-start(), calls=%async_computation.6 | async-start | bytes 3604480 | tf_op jit(solution)/shard_map/all_gather | solution.py:797
  17.2 22.9 %collective-permute-start.9 = (bf16[256,2048]{1,0:T(8,128)(2,1)}, bf16[256,2048]{1,0:T(8,128)(2,1)}, u32[]{:S(2)}, u32[]{:S(2)}) collective-permute-start(bf16[256,2048]{1,0:T(8,128)(2,1)} %bitcast.235), channel_id=1, source_target_pairs={{0,1},{1,0},{2,3},{3,2},{4,5},{5,4},{6,7},{7,6},{8,9},{9,8},{10,11... | collective-permute-start | bytes 3145736 | tf_op jit(solution)/shard_map/ppermute | solution.py:16
  17.7 26.5 %collective-permute-start.10 = (bf16[256,2048]{1,0:T(8,128)(2,1)}, bf16[256,2048]{1,0:T(8,128)(2,1)S(1)}, u32[]{:S(2)}, u32[]{:S(2)}) collective-permute-start(bf16[256,2048]{1,0:T(8,128)(2,1)} %bitcast.236), channel_id=1, source_target_pairs={{0,2},{1,3},{2,0},{3,1},{4,6},{5,7},{6,4},{7,5},{8,10},{9,11},{10,... | collective-permute-start | bytes 3145736 | tf_op jit(solution)/shard_map/ppermute | solution.py:16
  20.3 25.5 %collective-permute-start.11 = (bf16[256,2048]{1,0:T(8,128)(2,1)}, bf16[256,2048]{1,0:T(8,128)(2,1)}, u32[]{:S(2)}, u32[]{:S(2)}) collective-permute-start(bf16[256,2048]{1,0:T(8,128)(2,1)} %bitcast.237), channel_id=1, source_target_pairs={{0,4},{1,5},{2,6},{3,7},{4,0},{5,1},{6,2},{7,3},{8,12},{9,13},{10,... | collective-permute-start | bytes 3145736 | tf_op jit(solution)/shard_map/ppermute | solution.py:16
  45.9 24.5 %collective-permute-start.15 = (bf16[256,2048]{1,0:T(8,128)(2,1)S(1)}, bf16[256,2048]{1,0:T(8,128)(2,1)}, u32[]{:S(2)}, u32[]{:S(2)}) collective-permute-start(bf16[256,2048]{1,0:T(8,128)(2,1)S(1)} %fusion.1.refs_0_), channel_id=1, source_target_pairs={{0,4},{1,5},{2,6},{3,7},{4,0},{5,1},{6,2},{7,3},{8,12},{9,13},{10,... | collective-permute-start | bytes 3145736 | tf_op jit(solution)/shard_map/ppermute | solution.py:16
  47.4 24.8 %collective-permute-start.13 = (bf16[256,2048]{1,0:T(8,128)(2,1)S(1)}, bf16[256,2048]{1,0:T(8,128)(2,1)}, u32[]{:S(2)}, u32[]{:S(2)}) collective-permute-start(bf16[256,2048]{1,0:T(8,128)(2,1)S(1)} %fusion.1.refs_0_), channel_id=1, source_target_pairs={{0,2},{1,3},{2,0},{3,1},{4,6},{5,7},{6,4},{7,5},{8,10},{9,11},{10,... | collective-permute-start | bytes 3145736 | tf_op jit(solution)/shard_map/ppermute | solution.py:16
  102.5 39.3 %collective-permute-start = (bf16[2048,256]{1,0:T(8,128)(2,1)S(1)}, bf16[2048,256]{1,0:T(8,128)(2,1)}, u32[]{:S(2)}, u32[]{:S(2)}) collective-permute-start(bf16[2048,256]{1,0:T(8,128)(2,1)S(1)} %slice.556.refs_0_), channel_id=1, source_target_pairs={{0,1},{1,0},{2,3},{3,2},{4,5},{5,4},{6,7},{7,6},{8,9},{9,8},{10,11... | collective-permute-start | bytes 3145736 | tf_op jit(solution)/shard_map/ppermute | solution.py:16
  103.1 36.5 %collective-permute-start.1 = (bf16[2048,256]{1,0:T(8,128)(2,1)S(1)}, bf16[2048,256]{1,0:T(8,128)(2,1)S(1)}, u32[]{:S(2)}, u32[]{:S(2)}) collective-permute-start(bf16[2048,256]{1,0:T(8,128)(2,1)S(1)} %slice.556.refs_0_), channel_id=1, source_target_pairs={{0,2},{1,3},{2,0},{3,1},{4,6},{5,7},{6,4},{7,5},{8,10},{9,11},{10,... | collective-permute-start | bytes 3145736 | tf_op jit(solution)/shard_map/ppermute | solution.py:16
  104.3 33.6 %collective-permute-start.3 = (bf16[2048,256]{1,0:T(8,128)(2,1)S(1)}, bf16[2048,256]{1,0:T(8,128)(2,1)}, u32[]{:S(2)}, u32[]{:S(2)}) collective-permute-start(bf16[2048,256]{1,0:T(8,128)(2,1)S(1)} %slice.556.refs_0_), channel_id=1, source_target_pairs={{0,4},{1,5},{2,6},{3,7},{4,0},{5,1},{6,2},{7,3},{8,12},{9,13},{10,... | collective-permute-start | bytes 3145736 | tf_op jit(solution)/shard_map/ppermute | solution.py:16
  141.8 38.3 %collective-permute-start.2 = (bf16[2048,256]{1,0:T(8,128)(2,1)S(1)}, bf16[2048,256]{1,0:T(8,128)(2,1)S(1)}, u32[]{:S(2)}, u32[]{:S(2)}) collective-permute-start(bf16[2048,256]{1,0:T(8,128)(2,1)S(1)} %collective-permute-done.1.refs_2_), channel_id=1, source_target_pairs={{0,1},{1,0},{2,3},{3,2},{4,5},{5,4},{6,7},{7,6},{8,9},{9,8},{10,11... | collective-permute-start | bytes 3145736 | tf_op jit(solution)/shard_map/ppermute | solution.py:16
  153.6 26.5 %collective-permute-start.4 = (bf16[2048,256]{1,0:T(8,128)(2,1)}, bf16[2048,256]{1,0:T(8,128)(2,1)}, u32[]{:S(2)}, u32[]{:S(2)}) collective-permute-start(bf16[2048,256]{1,0:T(8,128)(2,1)} %collective-permute-done.3.refs_4_), channel_id=1, source_target_pairs={{0,1},{1,0},{2,3},{3,2},{4,5},{5,4},{6,7},{7,6},{8,9},{9,8},{10,11... | collective-permute-start | bytes 3145736 | tf_op jit(solution)/shard_map/ppermute | solution.py:16
  175.7 180.2 %reduce-scatter.5.cloned.1.call-start = ((), (), s32[]{:S(2)}) async-start(), calls=%async_computation.7 | async-start | bytes 3604480 | tf_op jit(solution)/shard_map/reduce_scatter | solution.py:868
  192.0 22.9 %collective-permute-start.34 = (bf16[256,2048]{1,0:T(8,128)(2,1)}, bf16[256,2048]{1,0:T(8,128)(2,1)S(1)}, u32[]{:S(2)}, u32[]{:S(2)}) collective-permute-start(bf16[256,2048]{1,0:T(8,128)(2,1)} %get-tuple-element.106.refs_0_), channel_id=1, source_target_pairs={{0,4},{1,5},{2,6},{3,7},{4,0},{5,1},{6,2},{7,3},{8,12},{9,13},{10,... | collective-permute-start | bytes 3145736 | tf_op jit(solution)/shard_map/ppermute | solution.py:16
  193.3 22.6 %collective-permute-start.32 = (bf16[256,2048]{1,0:T(8,128)(2,1)}, bf16[256,2048]{1,0:T(8,128)(2,1)}, u32[]{:S(2)}, u32[]{:S(2)}) collective-permute-start(bf16[256,2048]{1,0:T(8,128)(2,1)} %get-tuple-element.106.refs_0_), channel_id=1, source_target_pairs={{0,2},{1,3},{2,0},{3,1},{4,6},{5,7},{6,4},{7,5},{8,10},{9,11},{10,... | collective-permute-start | bytes 3145736 | tf_op jit(solution)/shard_map/ppermute | solution.py:16
  194.1 22.9 %collective-permute-start.40 = (bf16[256,2048]{1,0:T(8,128)(2,1)S(1)}, bf16[256,2048]{1,0:T(8,128)(2,1)S(1)}, u32[]{:S(2)}, u32[]{:S(2)}) collective-permute-start(bf16[256,2048]{1,0:T(8,128)(2,1)S(1)} %copy-done.28), channel_id=1, source_target_pairs={{0,1},{1,0},{2,3},{3,2},{4,5},{5,4},{6,7},{7,6},{8,9},{9,8},{10,11... | collective-permute-start | bytes 3145736 | tf_op jit(solution)/shard_map/ppermute | solution.py:16
  194.1 24.1 %collective-permute-start.41 = (bf16[256,2048]{1,0:T(8,128)(2,1)}, bf16[256,2048]{1,0:T(8,128)(2,1)S(1)}, u32[]{:S(2)}, u32[]{:S(2)}) collective-permute-start(bf16[256,2048]{1,0:T(8,128)(2,1)} %collective-permute-done.11.refs_14_), channel_id=1, source_target_pairs={{0,1},{1,0},{2,3},{3,2},{4,5},{5,4},{6,7},{7,6},{8,9},{9,8},{10,11... | collective-permute-start | bytes 3145736 | tf_op jit(solution)/shard_map/ppermute | solution.py:16
  194.6 23.6 %collective-permute-start.42 = (bf16[128,2048]{1,0:T(8,128)(2,1)}, bf16[128,2048]{1,0:T(8,128)(2,1)S(1)}, u32[]{:S(2)}, u32[]{:S(2)}) collective-permute-start(bf16[128,2048]{1,0:T(8,128)(2,1)} %collective-permute-done.21.refs_16_), channel_id=1, source_target_pairs={{0,1},{1,0},{2,3},{3,2},{4,5},{5,4},{6,7},{7,6},{8,9},{9,8},{10,11... | collective-permute-start | bytes 1572872 | tf_op jit(solution)/shard_map/ppermute | solution.py:16
  262.4 25.6 %collective-permute-start.45 = (bf16[256,2048]{1,0:T(8,128)(2,1)}, bf16[256,2048]{1,0:T(8,128)(2,1)S(1)}, u32[]{:S(2)}, u32[]{:S(2)}) collective-permute-start(bf16[256,2048]{1,0:T(8,128)(2,1)} %get-tuple-element.112.refs_0_), channel_id=1, source_target_pairs={{0,2},{1,3},{2,0},{3,1},{4,6},{5,7},{6,4},{7,5},{8,10},{9,11},{10,... | collective-permute-start | bytes 3145736 | tf_op jit(solution)/shard_map/ppermute | solution.py:16
  263.5 25.4 %collective-permute-start.46 = (bf16[256,2048]{1,0:T(8,128)(2,1)}, bf16[256,2048]{1,0:T(8,128)(2,1)S(1)}, u32[]{:S(2)}, u32[]{:S(2)}) collective-permute-start(bf16[256,2048]{1,0:T(8,128)(2,1)} %get-tuple-element.112.refs_0_), channel_id=1, source_target_pairs={{0,4},{1,5},{2,6},{3,7},{4,0},{5,1},{6,2},{7,3},{8,12},{9,13},{10,... | collective-permute-start | bytes 3145736 | tf_op jit(solution)/shard_map/ppermute | solution.py:16
  288.9 215.7 %reduce-scatter.7.cloned.1.call-start = ((), (), s32[]{:S(2)}) async-start(), calls=%async_computation.8 | async-start | bytes 7208960 | tf_op jit(solution)/shard_map/reduce_scatter | solution.py:868
  321.3 45.6 %collective-permute-start.49 = (bf16[4,256,2048]{2,1,0:T(8,128)(2,1)}, bf16[4,256,2048]{2,1,0:T(8,128)(2,1)}, u32[]{:S(2)}, u32[]{:S(2)}) collective-permute-start(bf16[4,256,2048]{2,1,0:T(8,128)(2,1)} %get-tuple-element.124), channel_id=1, source_target_pairs={{0,1},{1,0},{2,3},{3,2},{4,5},{5,4},{6,7},{7,6},{8,9},{9,8},{10,11... | collective-permute-start | bytes 12582920 | tf_op jit(solution)/shard_map/ppermute | solution.py:16
  355.9 289.8 %reduce-scatter.9.cloned.1.call-start = ((), (), s32[]{:S(2)}) async-start(), calls=%async_computation.9 | async-start | bytes 3932160 | tf_op jit(solution)/shard_map/reduce_scatter | solution.py:868
  372.7 31.7 %collective-permute-start.50 = (bf16[128,2048]{1,0:T(8,128)(2,1)S(1)}, bf16[128,2048]{1,0:T(8,128)(2,1)S(1)}, u32[]{:S(2)}, u32[]{:S(2)}) collective-permute-start(bf16[128,2048]{1,0:T(8,128)(2,1)S(1)} %slice_bitcast_fusion.22), channel_id=1, source_target_pairs={{0,2},{1,3},{2,0},{3,1},{4,6},{5,7},{6,4},{7,5},{8,10},{9,11},{10,... | collective-permute-start | bytes 1572872 | tf_op jit(solution)/shard_map/ppermute | solution.py:16
  373.8 25.1 %collective-permute-start.53 = (bf16[128,2048]{1,0:T(8,128)(2,1)S(1)}, bf16[128,2048]{1,0:T(8,128)(2,1)S(1)}, u32[]{:S(2)}, u32[]{:S(2)}) collective-permute-start(bf16[128,2048]{1,0:T(8,128)(2,1)S(1)} %get-tuple-element.202), channel_id=1, source_target_pairs={{0,2},{1,3},{2,0},{3,1},{4,6},{5,7},{6,4},{7,5},{8,10},{9,11},{10,... | collective-permute-start | bytes 1572872 | tf_op jit(solution)/shard_map/ppermute | solution.py:16
  374.8 29.6 %collective-permute-start.55 = (bf16[128,2048]{1,0:T(8,128)(2,1)S(1)}, bf16[128,2048]{1,0:T(8,128)(2,1)S(1)}, u32[]{:S(2)}, u32[]{:S(2)}) collective-permute-start(bf16[128,2048]{1,0:T(8,128)(2,1)S(1)} %slice_bitcast_fusion.17), channel_id=1, source_target_pairs={{0,4},{1,5},{2,6},{3,7},{4,0},{5,1},{6,2},{7,3},{8,12},{9,13},{10,... | collective-permute-start | bytes 1572872 | tf_op jit(solution)/shard_map/ppermute | solution.py:16
  420.0 75.6 %collective-permute-start.56 = (bf16[4,256,2048]{2,1,0:T(8,128)(2,1)}, bf16[4,256,2048]{2,1,0:T(8,128)(2,1)}, u32[]{:S(2)}, u32[]{:S(2)}) collective-permute-start(bf16[4,256,2048]{2,1,0:T(8,128)(2,1)} %get-tuple-element.127), channel_id=1, source_target_pairs={{0,1},{1,0},{2,3},{3,2},{4,5},{5,4},{6,7},{7,6},{8,9},{9,8},{10,11... | collective-permute-start | bytes 12582920 | tf_op jit(solution)/shard_map/ppermute | solution.py:16
  435.5 23.5 %collective-permute-start.75 = (bf16[4,256,256]{2,1,0:T(8,128)(2,1)S(1)}, bf16[4,256,256]{2,1,0:T(8,128)(2,1)S(1)}, u32[]{:S(2)}, u32[]{:S(2)}) collective-permute-start(bf16[4,256,256]{2,1,0:T(8,128)(2,1)S(1)} %slice_bitcast_fusion.23), channel_id=1, source_target_pairs={{0,1},{1,0},{2,3},{3,2},{4,5},{5,4},{6,7},{7,6},{8,9},{9,8},{10,11... | collective-permute-start | bytes 1572872 | tf_op jit(solution)/shard_map/ppermute | solution.py:16
  475.0 29.5 %collective-permute-start.76 = (bf16[2,256,256]{2,1,0:T(8,128)(2,1)S(1)}, bf16[2,256,256]{2,1,0:T(8,128)(2,1)}, u32[]{:S(2)}, u32[]{:S(2)}) collective-permute-start(bf16[2,256,256]{2,1,0:T(8,128)(2,1)S(1)} %pad_maximum_fusion.1), channel_id=1, source_target_pairs={{0,2},{1,3},{2,0},{3,1},{4,6},{5,7},{6,4},{7,5},{8,10},{9,11},{10,... | collective-permute-start | bytes 786440 | tf_op jit(solution)/shard_map/ppermute | solution.py:16
  476.6 28.6 %collective-permute-start.77 = (bf16[2,256,256]{2,1,0:T(8,128)(2,1)}, bf16[2,256,256]{2,1,0:T(8,128)(2,1)}, u32[]{:S(2)}, u32[]{:S(2)}) collective-permute-start(bf16[2,256,256]{2,1,0:T(8,128)(2,1)} %pad_maximum_fusion.2), channel_id=1, source_target_pairs={{0,4},{1,5},{2,6},{3,7},{4,0},{5,1},{6,2},{7,3},{8,12},{9,13},{10,... | collective-permute-start | bytes 786440 | tf_op jit(solution)/shard_map/ppermute | solution.py:16
  477.8 40.0 %collective-permute-start.78 = (bf16[2,256,256]{2,1,0:T(8,128)(2,1)S(1)}, bf16[2,256,256]{2,1,0:T(8,128)(2,1)}, u32[]{:S(2)}, u32[]{:S(2)}) collective-permute-start(bf16[2,256,256]{2,1,0:T(8,128)(2,1)S(1)} %pad_maximum_fusion.3), channel_id=1, source_target_pairs={{0,6},{1,7},{2,4},{3,5},{4,2},{5,3},{6,0},{7,1},{8,14},{9,15},{10,... | collective-permute-start | bytes 786440 | tf_op jit(solution)/shard_map/ppermute | solution.py:16
  479.6 23.5 %collective-permute-start.74 = (bf16[176,2048]{1,0:T(8,128)(2,1)S(1)}, bf16[176,2048]{1,0:T(8,128)(2,1)}, u32[]{:S(2)}, u32[]{:S(2)}) collective-permute-start(bf16[176,2048]{1,0:T(8,128)(2,1)S(1)} %collective-permute-done.65.refs_4_), channel_id=1, source_target_pairs={{0,2},{1,3},{2,0},{3,1},{4,6},{5,7},{6,4},{7,5},{8,10},{9,11},{10,... | collective-permute-start | bytes 2162696 | tf_op jit(solution)/shard_map/ppermute | solution.py:16
  539.1 30.0 %collective-permute-start.83 = (bf16[4,256,2048]{2,1,0:T(8,128)(2,1)}, bf16[4,256,2048]{2,1,0:T(8,128)(2,1)}, u32[]{:S(2)}, u32[]{:S(2)}) collective-permute-start(bf16[4,256,2048]{2,1,0:T(8,128)(2,1)} %get-tuple-element.156), channel_id=1, source_target_pairs={{0,1},{1,0},{2,3},{3,2},{4,5},{5,4},{6,7},{7,6},{8,9},{9,8},{10,11... | collective-permute-start | bytes 12582920 | tf_op jit(solution)/shard_map/ppermute | solution.py:16
  539.2 58.3 %collective-permute-start.79 = (bf16[256,2048]{1,0:T(8,128)(2,1)}, bf16[256,2048]{1,0:T(8,128)(2,1)}, u32[]{:S(2)}, u32[]{:S(2)}) collective-permute-start(bf16[256,2048]{1,0:T(8,128)(2,1)} %copy-done.24), channel_id=1, source_target_pairs={{0,1},{1,0},{2,3},{3,2},{4,5},{5,4},{6,7},{7,6},{8,9},{9,8},{10,11... | collective-permute-start | bytes 3145736 | tf_op jit(solution)/shard_map/ppermute | solution.py:16
  539.7 61.3 %collective-permute-start.80 = (bf16[256,2048]{1,0:T(8,128)(2,1)}, bf16[256,2048]{1,0:T(8,128)(2,1)}, u32[]{:S(2)}, u32[]{:S(2)}) collective-permute-start(bf16[256,2048]{1,0:T(8,128)(2,1)} %copy-done.25), channel_id=1, source_target_pairs={{0,1},{1,0},{2,3},{3,2},{4,5},{5,4},{6,7},{7,6},{8,9},{9,8},{10,11... | collective-permute-start | bytes 3145736 | tf_op jit(solution)/shard_map/ppermute | solution.py:16
  550.5 156.9 %reduce-scatter.11.cloned.1.call-start = ((), (), s32[]{:S(2)}) async-start(), calls=%async_computation.10 | async-start | bytes 1310720 | tf_op jit(solution)/shard_map/reduce_scatter | solution.py:868
  601.1 38.5 %collective-permute-start.89 = (bf16[512,1408]{1,0:T(8,128)(2,1)}, bf16[512,1408]{1,0:T(8,128)(2,1)}, u32[]{:S(2)}, u32[]{:S(2)}) collective-permute-start(bf16[512,1408]{1,0:T(8,128)(2,1)} %reduce-scatter.7.cloned.1.call-done.refs_0_), channel_id=1, source_target_pairs={{0,2},{1,3},{2,0},{3,1},{4,6},{5,7},{6,4},{7,5},{8,10},{9,11},{10,... | collective-permute-start | bytes 4325384 | tf_op jit(solution)/shard_map/ppermute | solution.py:16
  602.7 34.0 %collective-permute-start.90 = (bf16[512,1408]{1,0:T(8,128)(2,1)}, bf16[512,1408]{1,0:T(8,128)(2,1)}, u32[]{:S(2)}, u32[]{:S(2)}) collective-permute-start(bf16[512,1408]{1,0:T(8,128)(2,1)} %reduce-scatter.7.cloned.1.call-done.refs_0_), channel_id=1, source_target_pairs={{0,4},{1,5},{2,6},{3,7},{4,0},{5,1},{6,2},{7,3},{8,12},{9,13},{10,... | collective-permute-start | bytes 4325384 | tf_op jit(solution)/shard_map/ppermute | solution.py:16
  611.9 32.7 %collective-permute-start.88 = (bf16[512,1408]{1,0:T(8,128)(2,1)}, bf16[512,1408]{1,0:T(8,128)(2,1)}, u32[]{:S(2)}, u32[]{:S(2)}) collective-permute-start(bf16[512,1408]{1,0:T(8,128)(2,1)} %reduce-scatter.7.cloned.1.call-done.refs_0_), channel_id=1, source_target_pairs={{0,1},{1,0},{2,3},{3,2},{4,5},{5,4},{6,7},{7,6},{8,9},{9,8},{10,11... | collective-permute-start | bytes 4325384 | tf_op jit(solution)/shard_map/ppermute | solution.py:16
  613.8 28.8 %collective-permute-start.120 = (f32[30,2048]{1,0:T(8,128)S(1)}, f32[30,2048]{1,0:T(8,128)S(1)}, u32[]{:S(2)}, u32[]{:S(2)}) collective-permute-start(f32[30,2048]{1,0:T(8,128)S(1)} %pad_maximum_fusion.4), channel_id=1, source_target_pairs={{0,1},{1,0},{2,3},{3,2},{4,5},{5,4},{6,7},{7,6},{8,9},{9,8},{10,11... | collective-permute-start | bytes 737288 | tf_op jit(solution)/shard_map/ppermute | solution.py:100
  642.7 22.9 %collective-permute-start.109 = (bf16[512,1408]{1,0:T(8,128)(2,1)}, bf16[512,1408]{1,0:T(8,128)(2,1)}, u32[]{:S(2)}, u32[]{:S(2)}) collective-permute-start(bf16[512,1408]{1,0:T(8,128)(2,1)} %collective-permute-done.90.refs_4_), channel_id=1, source_target_pairs={{0,1},{1,0},{2,3},{3,2},{4,5},{5,4},{6,7},{7,6},{8,9},{9,8},{10,11... | collective-permute-start | bytes 4325384 | tf_op jit(solution)/shard_map/ppermute | solution.py:16
  662.0 26.4 %collective-permute-start.104 = (bf16[512,768]{1,0:T(8,128)(2,1)}, bf16[512,768]{1,0:T(8,128)(2,1)}, u32[]{:S(2)}, u32[]{:S(2)}) collective-permute-start(bf16[512,768]{1,0:T(8,128)(2,1)} %reduce-scatter.9.cloned.1.call-done.refs_0_), channel_id=1, source_target_pairs={{0,2},{1,3},{2,0},{3,1},{4,6},{5,7},{6,4},{7,5},{8,10},{9,11},{10,... | collective-permute-start | bytes 2359304 | tf_op jit(solution)/shard_map/ppermute | solution.py:16
  662.6 23.2 %collective-permute-start.106 = (bf16[512,768]{1,0:T(8,128)(2,1)}, bf16[512,768]{1,0:T(8,128)(2,1)}, u32[]{:S(2)}, u32[]{:S(2)}) collective-permute-start(bf16[512,768]{1,0:T(8,128)(2,1)} %reduce-scatter.9.cloned.1.call-done.refs_0_), channel_id=1, source_target_pairs={{0,4},{1,5},{2,6},{3,7},{4,0},{5,1},{6,2},{7,3},{8,12},{9,13},{10,... | collective-permute-start | bytes 2359304 | tf_op jit(solution)/shard_map/ppermute | solution.py:16
  665.6 29.0 %collective-permute-start.92 = (bf16[128,2048]{1,0:T(8,128)(2,1)}, bf16[128,2048]{1,0:T(8,128)(2,1)S(1)}, u32[]{:S(2)}, u32[]{:S(2)}) collective-permute-start(bf16[128,2048]{1,0:T(8,128)(2,1)} %fusion.10), channel_id=1, source_target_pairs={{0,4},{1,5},{2,6},{3,7},{4,0},{5,1},{6,2},{7,3},{8,12},{9,13},{10,... | collective-permute-start | bytes 1572872 | tf_op jit(solution)/shard_map/ppermute | solution.py:16
  666.7 27.9 %collective-permute-start.91 = (bf16[128,2048]{1,0:T(8,128)(2,1)}, bf16[128,2048]{1,0:T(8,128)(2,1)S(1)}, u32[]{:S(2)}, u32[]{:S(2)}) collective-permute-start(bf16[128,2048]{1,0:T(8,128)(2,1)} %fusion.11), channel_id=1, source_target_pairs={{0,2},{1,3},{2,0},{3,1},{4,6},{5,7},{6,4},{7,5},{8,10},{9,11},{10,... | collective-permute-start | bytes 1572872 | tf_op jit(solution)/shard_map/ppermute | solution.py:16
  670.0 30.3 %collective-permute-start.122 = (f32[30,2048]{1,0:T(8,128)S(1)}, f32[30,2048]{1,0:T(8,128)}, u32[]{:S(2)}, u32[]{:S(2)}) collective-permute-start(f32[30,2048]{1,0:T(8,128)S(1)} %add.236), channel_id=1, source_target_pairs={{0,4},{1,5},{2,6},{3,7},{4,0},{5,1},{6,2},{7,3},{8,12},{9,13},{10,... | collective-permute-start | bytes 737288 | tf_op jit(solution)/shard_map/ppermute | solution.py:100
  698.1 27.2 %collective-permute-start.103 = (bf16[512,768]{1,0:T(8,128)(2,1)}, bf16[512,768]{1,0:T(8,128)(2,1)}, u32[]{:S(2)}, u32[]{:S(2)}) collective-permute-start(bf16[512,768]{1,0:T(8,128)(2,1)} %reduce-scatter.9.cloned.1.call-done.refs_0_), channel_id=1, source_target_pairs={{0,1},{1,0},{2,3},{3,2},{4,5},{5,4},{6,7},{7,6},{8,9},{9,8},{10,11... | collective-permute-start | bytes 2359304 | tf_op jit(solution)/shard_map/ppermute | solution.py:16
  (179 other events, 2101.0 us)
Sparse Core Ops, SparseCore 0:
  11.9 85.4 all-gather.5
  99.6 104.9 all-gather.7
  206.1 57.4 all-gather.9
  289.0 56.6 reduce-scatter.4
  356.0 102.7 reduce-scatter.6
  550.6 62.4 reduce-scatter.8
  645.9 26.5 reduce-scatter.10

commit v2 on v1

--- a/solution.py
+++ b/solution.py
@@ -16,18 +16,19 @@
     return lax.ppermute(x, "seq", [(i, i ^ bits) for i in range(count)])
 
 
-def gather_start(x):
+def gather_start(x, together=False):
     if lax.axis_size("seq") == 8:
-        return [x, swap(x, 1), swap(x, 2), swap(x, 4)]
+        got = [swap(x, 1), swap(x, 2), swap(x, 4)]
+        return [x] + list(lax.optimization_barrier(got) if together else got)
     return [x]
 
 
-def gather_far(first):
+def gather_far(first, split=True):
     if lax.axis_size("seq") != 8:
         return []
     x, _, side, back = first
     half = x.shape[0] // 2
-    if x.shape[0] % 32 == 0:
+    if split and x.shape[0] % 32 == 0:
         return [swap(back[:half], 2), swap(side[half:], 4)]
     return [swap(back, 2)]
 
@@ -58,48 +59,57 @@
     return swap(odd, 1) if lax.axis_size("seq") == 8 else odd
 
 
-def reduce_far(even, twin):
+def reduce_add(even, twin):
     count = lax.axis_size("seq")
     if count == 8:
         half = even.shape[1] // 2
-        far, side, back = (add(even[b], twin[b]) for b in (3, 1, 2))
-        far_top, far_low = swap(far[:half], 2), swap(far[half:], 4)
-        side_top, back_low = swap(side[:half], 2), swap(back[half:], 4)
-        return [even[0], twin[0], side[half:], back[:half], side_top, back_low, far_top, far_low]
+        top, low = slice(None, half), slice(half, None)
+        return [
+            even,
+            twin,
+            add(even[1, low], twin[1, low]),
+            add(even[2, top], twin[2, top]),
+            add(even[1::2, top], twin[1::2, top]),
+            add(even[2:, low], twin[2:, low]),
+        ]
     parts = jnp.stack([even, twin], axis=1).reshape((count,) + even.shape[1:])
     bits = count // 2
     while bits:
         parts = add(parts[:bits], swap(parts[bits:], bits))
         bits //= 2
-    return [parts[0]]
+    return [parts]
+
+
+def reduce_far(state):
+    if len(state) == 1:
+        return state
+    sends = lax.optimization_barrier(state[4:])
+    return state[:4] + list(lax.optimization_barrier([swap(sends[0], 2), swap(sends[1], 4)]))
+
+
+def reduce_more(state):
+    if len(state) == 1:
+        return state
+    even, twin, side, back, from_side, from_back = state
+    return [even, twin, add(side, from_back[1]), add(back, from_side[1]), from_side, from_back]
 
 
 def reduce_last(state):
     if len(state) == 1:
         return [state]
-    own, twin, side, back, side_top, back_low, far_top, far_low = state
-    side_low = swap(add(side, far_low), 2)
-    back_top = swap(add(back, far_top), 4)
-    return [[own], [twin], [side_top, side_low], [back_top, back_low]]
-
-
-def exchange_xor(parts):
-    count = lax.axis_size("seq")
-    if count == 8:
-        twin = swap(parts[1], 1)
-        out = [parts[0, :1], twin[:1]]
-        for n in (1, 2, 3):
-            out.append(swap(jnp.concatenate([parts[0, n : n + 1], twin[n : n + 1]]), 2 * n))
-        return out
-    return [parts[0, :1]] + [swap(parts[b % 2, b // 2][None], b) for b in range(1, count)]
-
-
-def sum_over(axis, x):
-    count, bits = lax.axis_size(axis), 1
-    while bits < count:
-        x = x + lax.ppermute(x, axis, [(i, i ^ bits) for i in range(count)])
-        bits *= 2
-    return x
+    even, twin, side, back, from_side, from_back = state
+    side, back = lax.optimization_barrier([swap(side, 2), swap(back, 4)])
+    return [[even], [twin], [from_side, side], [back, from_back]]
+
+
+def total_of(parts):
+    width = parts[0][0].shape[-1]
+    rows = [jnp.concatenate([a[0] if a.ndim == 3 else a for a in e]) for e in parts]
+    return sum(r.reshape(-1, width).astype(WIDE) for r in rows)
+
+
+def exchange(parts):
+    return lax.all_to_all(parts, "seq", split_axis=0, concat_axis=0, tiled=True)
 
 
 def after(x, *others):
@@ -153,8 +163,9 @@
 
 
 def mixer_forward(
-    place_ref, proj_ref, taps_ref, logit_ref, gain_ref, out_ref, mixed_ref, state_ref, inv_ref, w_ref, fresh_ref
+    place_ref, proj_ref, taps_ref, logit_ref, gain_ref, *refs
 ):
+    out_ref, mixed_ref, state_ref, inv_ref, w_ref, fresh_ref = refs[-6:]
     place, head = place_ref[0], pl.program_id(0)
     count, _, length, _ = proj_ref.shape
     dim = mixed_ref.shape[-1]
@@ -189,22 +200,17 @@
         mixed = dot(q[i], states[i]) + dot(scores[i], fresh[i])
         scale = lax.rsqrt(jnp.mean(mixed * mixed, axis=-1, keepdims=True) + 1e-05)
         mixed_ref[0, 0, i] = mixed
-        out_ref[spot[i] & 1, spot[i] >> 1] = (mixed * scale * gain).astype(LOW)
+        out_ref[i] = (mixed * scale * gain).astype(LOW)
         state_ref[0, 0, i] = states[i]
         inv_ref[0, 0, i] = invs[i]
         w_ref[0, 0, i] = w[i]
         fresh_ref[0, 0, i] = fresh[i]
 
 
-def mixer_backward(stacks, place_ref, proj_ref, taps_ref, logit_ref, gain_ref, *refs):
-    gout_refs, refs = refs[: len(stacks)], refs[len(stacks) :]
+def mixer_backward(place_ref, proj_ref, taps_ref, logit_ref, gain_ref, gout_ref, *refs):
     mixed_ref, state_ref, inv_ref, w_ref, fresh_ref = refs[:5]
-    gproj_ref, glogit_ref, gtaps_ref, ggain_ref, gout_ref = refs[-5:]
-    at = 0
-    for ref, size in zip(gout_refs, stacks):
-        gout_ref[at : at + size] = ref[...]
-        at += size
-    place, head = place_ref[0], pl.program_id(0)
+    gproj_ref, glogit_ref, gtaps_ref, ggain_ref = refs[-4:]
+    place, head = place_ref[0], pl.program_id(1)
     count, _, length, _ = proj_ref.shape
     dim = mixed_ref.shape[-1]
     spot = [jnp.bitwise_xor(place, i) for i in range(count)]
@@ -228,14 +234,14 @@
     for i in range(count):
         mixed = mixed_ref[0, 0, i]
         scale = lax.rsqrt(jnp.mean(mixed * mixed, axis=-1, keepdims=True) + 1e-05)
-        grad = gout_ref[spot[i]].astype(WIDE)
+        grad = gout_ref[i].astype(WIDE)
         gain_sum = gain_sum + jnp.sum(grad * mixed * scale, axis=0, keepdims=True)
         weighted = grad * gain
         back = scale * weighted - mixed * (
             scale * scale * scale * jnp.mean(mixed * weighted, axis=-1, keepdims=True)
         )
         gm.append(back.astype(LOW))
-    ggain_ref[0] = gain_sum
+    ggain_ref[0, 0] = gain_sum
     inv, w, fresh, states = ([r[0, 0, i] for i in range(count)] for r in (inv_ref, w_ref, fresh_ref, state_ref))
     gram = [dot(x, x, 1, 1) for x in k]
     scores = [jnp.where(row >= col, dot(a, b, 1, 1), 0.0).astype(LOW) for a, b in zip(q, k)]
@@ -284,7 +290,7 @@
         moved, conved, gate, _ = convs[c]
         gconv = gacts[c] * gate * (1.0 + conved * (1.0 - gate))
         taps = taps_ref[0, c]
-        gtaps_ref[0, c] = jnp.concatenate([jnp.sum(gconv * m, axis=0, keepdims=True) for m in moved])
+        gtaps_ref[0, 0, c] = jnp.concatenate([jnp.sum(gconv * m, axis=0, keepdims=True) for m in moved])
         last = len(moved) - 1
         gp = taps[last : last + 1] * gconv
         for j in range(last):
@@ -294,79 +300,80 @@
             gproj_ref[spot[i], 0, :, c * dim : (c + 1) * dim] = gp[i * length : (i + 1) * length]
 
 
-def mixer_specs(b, count, length, dim, lanes, taps):
+def mixer_specs(at, count, length, dim, lanes, taps):
+    def spec(shape, place):
+        return pl.BlockSpec(shape, lambda *g: place(*at(*g)))
+
     small = [
-        pl.BlockSpec((count, 1, length, 3 * dim), lambda h, p: (0, b, 0, h)),
-        pl.BlockSpec((1, 3, taps, dim), lambda h, p: (h, 0, 0, 0)),
-        pl.BlockSpec((count, 1, length, lanes), lambda h, p: (0, b, 0, 0)),
-        pl.BlockSpec((1, dim), lambda h, p: (0, 0)),
+        spec((count, 1, length, 3 * dim), lambda b, h: (0, b, 0, h)),
+        spec((1, 3, taps, dim), lambda b, h: (h, 0, 0, 0)),
+        spec((count, 1, length, lanes), lambda b, h: (0, b, 0, 0)),
+        spec((1, dim), lambda b, h: (0, 0)),
     ]
-    saved = pl.BlockSpec((1, 1, count, length, dim), lambda h, p: (0, h, 0, 0, 0))
-    square = pl.BlockSpec((1, 1, count, dim, dim), lambda h, p: (0, h, 0, 0, 0))
-    inverse = pl.BlockSpec((1, 1, count, length, length), lambda h, p: (0, h, 0, 0, 0))
-    return small, [saved, square, inverse, saved, saved]
-
-
-def run_mixer_forward(b, place, proj, taps, logits, gain):
-    count, _, length, width = proj.shape
+    saved = spec((1, 1, count, length, dim), lambda b, h: (b, h, 0, 0, 0))
+    square = spec((1, 1, count, dim, dim), lambda b, h: (b, h, 0, 0, 0))
+    inverse = spec((1, 1, count, length, length), lambda b, h: (b, h, 0, 0, 0))
+    return small, [saved, square, inverse, saved, saved], spec
+
+
+def run_mixer_forward(b, place, proj, taps, logits, gain, held):
+    count, seqs, length, width = proj.shape
     heads, _, tap_count, dim = taps.shape
-    small, saved = mixer_specs(b, count, length, dim, logits.shape[-1], tap_count)
+    small, saved, spec = mixer_specs(lambda h, p: (b, h), count, length, dim, logits.shape[-1], tap_count)
     shapes = [
-        jax.ShapeDtypeStruct((2, count // 2, length, heads * dim), LOW),
-        jax.ShapeDtypeStruct((1, heads, count, length, dim), WIDE),
-        jax.ShapeDtypeStruct((1, heads, count, dim, dim), LOW),
-        jax.ShapeDtypeStruct((1, heads, count, length, length), LOW),
-        jax.ShapeDtypeStruct((1, heads, count, length, dim), LOW),
-        jax.ShapeDtypeStruct((1, heads, count, length, dim), LOW),
+        jax.ShapeDtypeStruct((count, length, heads * dim), LOW),
+        jax.ShapeDtypeStruct((seqs, heads, count, length, dim), WIDE),
+        jax.ShapeDtypeStruct((seqs, heads, count, dim, dim), LOW),
+        jax.ShapeDtypeStruct((seqs, heads, count, length, length), LOW),
+        jax.ShapeDtypeStruct((seqs, heads, count, length, dim), LOW),
+        jax.ShapeDtypeStruct((seqs, heads, count, length, dim), LOW),
     ]
-    out = pl.BlockSpec((2, count // 2, length, dim), lambda h, p: (0, 0, 0, h))
+    held = list(held or [])
     return pl.pallas_call(
         mixer_forward,
         out_shape=shapes,
         grid_spec=pltpu.PrefetchScalarGridSpec(
-            num_scalar_prefetch=1, grid=(heads,), in_specs=small, out_specs=[out] + saved
+            num_scalar_prefetch=1,
+            grid=(heads,),
+            in_specs=small + [ANY] * len(held),
+            out_specs=[spec((count, length, dim), lambda b, h: (0, 0, h))] + saved,
         ),
+        input_output_aliases={1 + len(small) + n: 1 + n for n in range(len(held))},
         compiler_params=pltpu.CompilerParams(vmem_limit_bytes=56 * 2**20),
         cost_estimate=cost(10),
         name="mixer_forward",
-    )(place, proj, taps, logits, gain)
-
-
-def run_mixer_backward(b, place, proj, taps, logits, gain, gout, saved_values, held):
-    count, _, length, width = proj.shape
+    )(place, proj, taps, logits, gain, *held)
+
+
+def run_mixer_backward(place, proj, taps, logits, gain, gout, saved_values):
+    count, seqs, length, width = proj.shape
     heads, _, tap_count, dim = taps.shape
-    small, saved = mixer_specs(b, count, length, dim, logits.shape[-1], tap_count)
+    small, saved, spec = mixer_specs(lambda b, h, p: (b, h), count, length, dim, logits.shape[-1], tap_count)
     shapes = [
         jax.ShapeDtypeStruct(proj.shape, LOW),
         jax.ShapeDtypeStruct(logits.shape, LOW),
-        jax.ShapeDtypeStruct((heads, 3, tap_count, dim), WIDE),
-        jax.ShapeDtypeStruct((heads, 1, dim), WIDE),
+        jax.ShapeDtypeStruct((seqs, heads, 3, tap_count, dim), WIDE),
+        jax.ShapeDtypeStruct((seqs, heads, 1, dim), WIDE),
     ]
     outs = [
         small[0],
         small[2],
-        pl.BlockSpec((1, 3, tap_count, dim), lambda h, p: (h, 0, 0, 0)),
-        pl.BlockSpec((1, 1, dim), lambda h, p: (h, 0, 0)),
+        spec((1, 1, 3, tap_count, dim), lambda b, h: (b, h, 0, 0, 0)),
+        spec((1, 1, 1, dim), lambda b, h: (b, h, 0, 0)),
     ]
-    sizes = [g.shape[0] for g in gout]
-    gouts = [pl.BlockSpec((n, length, dim), lambda h, p: (0, 0, h)) for n in sizes]
-    held = list(held or [])
-    first = 1 + len(small) + len(gouts) + len(saved)
     return pl.pallas_call(
-        functools.partial(mixer_backward, sizes),
+        mixer_backward,
         out_shape=shapes,
         grid_spec=pltpu.PrefetchScalarGridSpec(
             num_scalar_prefetch=1,
-            grid=(heads,),
-            in_specs=small + gouts + saved + [ANY] * len(held),
+            grid=(seqs, heads),
+            in_specs=small + [spec((count, length, dim), lambda b, h: (0, b, h))] + saved,
             out_specs=outs,
-            scratch_shapes=[pltpu.VMEM((count, length, dim), LOW)],
         ),
-        input_output_aliases={first + n: n for n in range(len(held))},
         compiler_params=pltpu.CompilerParams(vmem_limit_bytes=56 * 2**20),
-        cost_estimate=cost(13),
+        cost_estimate=cost(26),
         name="mixer_backward",
-    )(place, proj, taps, logits, gain, *gout, *saved_values, *held)
+    )(place, proj, taps, logits, gain, gout, *saved_values)
 
 
 ANY = pl.BlockSpec(memory_space=pl.ANY)
@@ -375,7 +382,7 @@
 
 
 def cost(micros):
-    return pl.CostEstimate(flops=int(micros * 0.5e9), transcendentals=0, bytes_accessed=0)
+    return pl.CostEstimate(flops=int(micros * 1.15e9), transcendentals=0, bytes_accessed=int(micros * 3.5e6))
 
 
 def fetch(entries, refs, buf, sems):
@@ -383,14 +390,43 @@
     for b, entry in enumerate(entries):
         row, mine = 0, []
         for size in entry:
-            copy = pltpu.make_async_copy(refs[n], buf.at[b, pl.ds(row, size)], sems.at[n])
-            copy.start()
-            mine.append(copy)
+            mine.append(pltpu.make_async_copy(refs[n], buf.at[b, pl.ds(row, size)], sems.at[n]))
             row, n = row + size, n + 1
         copies.append(mine)
     return copies
 
 
+def start_all(copies):
+    for mine in copies:
+        for c in mine:
+            c.start()
+
+
+def stream(copies, outs):
+    step, last = pl.program_id(0), len(copies) // 2 - 1
+
+    @pl.when(step == 0)
+    def _():
+        start_all(copies)
+
+    for i in range(last + 1):
+
+        @pl.when(step == i)
+        def _(i=i):
+            for b in (2 * i, 2 * i + 1):
+                for c in copies[b]:
+                    c.wait()
+                outs[b].start()
+
+    def finish():
+        @pl.when(step == last)
+        def _():
+            for out in outs:
+                out.wait()
+
+    return finish
+
+
 def heights(entries):
     return [[a.shape[0] for a in entry] for entry in entries]
 
@@ -402,19 +438,13 @@
 def project_kernel(entries, *refs):
     n = sum(len(e) for e in entries)
     w_ref, beta_ref, proj_ref, logit_ref, all_ref, buf, sems, out_sems = refs[n:]
-    copies = fetch(entries, refs[:n], buf, sems)
-    outs = []
-    for b, mine in enumerate(copies):
-        for c in mine:
-            c.wait()
-        out = pltpu.make_async_copy(buf.at[b], all_ref.at[b], out_sems.at[b])
-        out.start()
-        outs.append(out)
-        x = buf[b]
-        proj_ref[b] = dot(x, w_ref[...]).astype(LOW)
-        logit_ref[b] = dot(x, beta_ref[...], 1, 1)
-    for out in outs:
-        out.wait()
+    count, rows, width = buf.shape
+    outs = [pltpu.make_async_copy(buf.at[b], all_ref.at[b], out_sems.at[b]) for b in range(count)]
+    finish = stream(fetch(entries, refs[:n], buf, sems), outs)
+    x = buf[pl.ds(2 * pl.program_id(0), 2)].reshape(2 * rows, width)
+    proj_ref[...] = dot(x, w_ref[...]).astype(LOW).reshape(proj_ref.shape)
+    logit_ref[...] = dot(x, beta_ref[...], 1, 1).reshape(logit_ref.shape)
+    finish()
 
 
 def run_project(entries, w, beta, cols):
@@ -422,19 +452,23 @@
     count, rows = len(sizes), sum(sizes[0])
     pieces = flat(entries)
     width = pieces[0].shape[1]
+    lanes = beta.shape[0]
     return pl.pallas_call(
         functools.partial(project_kernel, sizes),
-        grid=(1,),
+        grid=(count // 2,),
         in_specs=[ANY] * len(pieces)
-        + [pl.BlockSpec((width, cols), lambda g: (0, 0)), pl.BlockSpec(beta.shape, lambda g: (0, 0))],
+        + [
+            pl.BlockSpec((width, cols), lambda g: (0, 0), pipeline_mode=pl.Buffered(1)),
+            pl.BlockSpec(beta.shape, lambda g: (0, 0), pipeline_mode=pl.Buffered(1)),
+        ],
         out_specs=[
-            pl.BlockSpec((count, rows, cols), lambda g: (0, 0, 0)),
-            pl.BlockSpec((count, rows, beta.shape[0]), lambda g: (0, 0, 0)),
+            pl.BlockSpec((2, rows, cols), lambda g: (g, 0, 0)),
+            pl.BlockSpec((2, rows, lanes), lambda g: (g, 0, 0)),
             ANY,
         ],
         out_shape=[
             jax.ShapeDtypeStruct((count, rows, cols), LOW),
-            jax.ShapeDtypeStruct((count, rows, beta.shape[0]), WIDE),
+            jax.ShapeDtypeStruct((count, rows, lanes), WIDE),
             jax.ShapeDtypeStruct((count, rows, width), LOW),
         ],
         scratch_shapes=[
@@ -453,30 +487,21 @@
     m = n + sum(len(e) for e in others)
     w_ref, inner_ref, up_ref, gate_ref, all_ref, side_ref = refs[m : m + 6]
     buf, side, sems, out_sems, side_sems, back_sems = refs[m + 6 :]
-    copies = fetch(entries, refs[:n], buf, sems)
-    beside = fetch(others, refs[n:m], side, side_sems)
+    count, rows, width = buf.shape
+    outs = [pltpu.make_async_copy(buf.at[b], all_ref.at[b], out_sems.at[b]) for b in range(count)]
+    backs = [pltpu.make_async_copy(side.at[b], side_ref.at[b], back_sems.at[b]) for b in range(count)]
+    finish = stream(fetch(entries, refs[:n], buf, sems), outs)
+    finish_side = stream(fetch(others, refs[n:m], side, side_sems), backs)
     ff = inner_ref.shape[-1]
-    outs = []
-    for b, mine in enumerate(copies):
-        for c in mine:
-            c.wait()
-        out = pltpu.make_async_copy(buf.at[b], all_ref.at[b], out_sems.at[b])
-        out.start()
-        outs.append(out)
-        both = dot(buf[b], w_ref[...])
-        gate, up = both[:, :ff], both[:, ff:]
-        sig = jax.nn.sigmoid(gate)
-        swish = gate * sig
-        inner_ref[b] = (swish * up).astype(LOW)
-        gate_ref[b] = (up * sig * (1.0 + gate * (1.0 - sig))).astype(LOW)
-        up_ref[b] = swish.astype(LOW)
-        for c in beside[b]:
-            c.wait()
-        out = pltpu.make_async_copy(side.at[b], side_ref.at[b], back_sems.at[b])
-        out.start()
-        outs.append(out)
-    for out in outs:
-        out.wait()
+    both = dot(buf[pl.ds(2 * pl.program_id(0), 2)].reshape(2 * rows, width), w_ref[...])
+    gate, up = both[:, :ff], both[:, ff:]
+    sig = jax.nn.sigmoid(gate)
+    swish = gate * sig
+    inner_ref[...] = (swish * up).astype(LOW).reshape(inner_ref.shape)
+    gate_ref[...] = (up * sig * (1.0 + gate * (1.0 - sig))).astype(LOW).reshape(gate_ref.shape)
+    up_ref[...] = swish.astype(LOW).reshape(up_ref.shape)
+    finish()
+    finish_side()
 
 
 def run_gate(entries, others, w):
@@ -487,8 +512,10 @@
     width, ff = pieces[0].shape[1], w.shape[1] // 2
     return pl.pallas_call(
         functools.partial(gate_kernel, sizes, heights(others)),
-        in_specs=[ANY] * (len(pieces) + len(beside)) + [pl.BlockSpec(memory_space=FULL)],
-        out_specs=[pl.BlockSpec(memory_space=FULL)] * 3 + [ANY] * 2,
+        grid=(count // 2,),
+        in_specs=[ANY] * (len(pieces) + len(beside))
+        + [pl.BlockSpec(w.shape, lambda g: (0, 0), pipeline_mode=pl.Buffered(1))],
+        out_specs=[pl.BlockSpec((2, rows, ff), lambda g: (g, 0, 0))] * 3 + [ANY] * 2,
         out_shape=[jax.ShapeDtypeStruct((count, rows, ff), LOW)] * 3
         + [jax.ShapeDtypeStruct((count, rows, width), LOW)] * 2,
         scratch_shapes=[
@@ -551,7 +578,7 @@
     odd_ref[0] = total[rows:]
 
 
-def run_pairs(terms, width, name):
+def run_pairs(terms, width, name, micros):
     count, rows, _ = terms[0][0].shape
     half = jax.ShapeDtypeStruct((count // 2, rows, width), LOW)
     weight_specs = []
@@ -565,7 +592,7 @@
         out_specs=[pl.BlockSpec((1, rows, width), lambda b: (b, 0, 0))] * 2,
         out_shape=[half, half],
         compiler_params=PARAMS,
-        cost_estimate=cost(12),
+        cost_estimate=cost(micros),
         name=name,
     )(*[t[0] for t in terms], *[t[1] for t in terms])
 
@@ -575,20 +602,17 @@
     count = len(entries)
     parts, (token_ref, gain_ref, hidden_ref, two_ref, rows_ref, buf, sems) = refs[n:-7], refs[-7:]
     copies = fetch(entries, refs[:n], buf, sems)
+    start_all(copies)
     place = place_ref[0]
     wide = parts[0].shape[-1]
 
     def spot(b):
         return pl.ds(pl.multiple_of(jnp.bitwise_xor(place, b) * wide, wide), wide)
 
-    row, at = 0, 0
-    for ref in parts:
-        size, length, _ = ref.shape
-        for i in range(size):
-            rows_ref[row : row + length, spot(at + i)] = ref[i]
-        at += size
-        if at == count:
-            row, at = row + length, 0
+    for n, ref in enumerate(parts):
+        length = ref.shape[1]
+        for i in range(count):
+            rows_ref[n * length : (n + 1) * length, i * wide : (i + 1) * wide] = ref[i]
     rows = rows_ref[...]
     for b, mine in enumerate(copies):
         for c in mine:
@@ -629,13 +653,14 @@
     m = sum(len(e) for e in grads)
     count = len(entries)
     adds, (hidden_ref, cot_ref, gain_ref) = refs[n : n + m], refs[n + m : n + m + 3]
-    ghidden_ref, gsum_ref, gbranch_ref, *gout_refs, buf, gout_all, sems = refs[n + m + 3 :]
+    ghidden_ref, gsum_ref, gbranch_ref, gout_ref, buf, gout_all, sems = refs[n + m + 3 :]
     copies = fetch(entries, refs[:n], buf, sems)
+    start_all(copies)
     place = place_ref[0]
     wide = gbranch_ref.shape[-1]
     total, at = 0.0, 0
     for entry in grads:
-        here = [adds[at + i][...].astype(WIDE) for i in range(len(entry))]
+        here = [adds[at + i][...].astype(WIDE).reshape(-1, hidden_ref.shape[-1]) for i in range(len(entry))]
         at += len(entry)
         total = total + (jnp.concatenate(here) if len(here) > 1 else here[0])
     hidden = hidden_ref[...]
@@ -653,35 +678,48 @@
     for b, mine in enumerate(copies):
         for c in mine:
             c.wait()
-        gbranch = ghidden_ref[:, spot(b)].astype(LOW)
-        gbranch_ref[b % 2, b // 2] = gbranch
-        part = dot(gbranch, buf[b], 1, 1)
+        gbranch_ref[b] = ghidden_ref[:, b * wide : (b + 1) * wide].astype(LOW)
+        part = dot(ghidden_ref[:, spot(b)], buf[b], 1, 1)
         if b == 0:
             gout_all[...] = part
         else:
             gout_all[...] += part
     for b in range(count):
-        for i, ref in enumerate(gout_refs):
-            length = ref.shape[2]
-            ref[b % 2, b // 2] = gout_all[i * length : (i + 1) * length, spot(b)].astype(LOW)
-
-
-def run_branch_back(place, entries, grads, hidden, cot, gain, seqs):
+        gout_ref[b] = gout_all[:, b * wide : (b + 1) * wide].astype(LOW)
+
+
+def run_branch_back(place, entries, grads, hidden, cot, gain):
     sizes, grad_sizes = heights(entries), heights(grads)
     pieces, adds = flat(entries), flat(grads)
     count, depth, wide = len(sizes), sum(sizes[0]), pieces[0].shape[1]
     rows = hidden.shape[0]
-    vmem = pl.BlockSpec(memory_space=FULL)
+
+    def first(x):
+        shape = x.shape if len(x.shape) == 2 else (1,) + x.shape[1:]
+        return pl.BlockSpec(shape, lambda g: (0,) * len(shape))
+
+    def whole(shape):
+        return pl.BlockSpec(shape, lambda g: (0,) * len(shape))
+
     return pl.pallas_call(
         functools.partial(branch_back_kernel, sizes, grad_sizes),
-        in_specs=[pl.BlockSpec(memory_space=pltpu.SMEM)] + [ANY] * len(pieces) + [vmem] * (len(adds) + 3),
-        out_specs=[vmem] * (3 + seqs),
+        grid=(1,),
+        in_specs=[pl.BlockSpec(memory_space=pltpu.SMEM)]
+        + [ANY] * len(pieces)
+        + [first(x) for x in adds]
+        + [whole(x.shape) for x in (hidden, cot, gain)],
+        out_specs=[
+            whole(hidden.shape),
+            whole((1, hidden.shape[1])),
+            whole((count, rows, wide)),
+            whole((count, rows, wide)),
+        ],
         out_shape=[
             jax.ShapeDtypeStruct(hidden.shape, WIDE),
             jax.ShapeDtypeStruct((1, hidden.shape[1]), WIDE),
-            jax.ShapeDtypeStruct((2, count // 2, rows, wide), LOW),
-        ]
-        + [jax.ShapeDtypeStruct((2, count // 2, rows // seqs, wide), LOW)] * seqs,
+            jax.ShapeDtypeStruct((count, rows, wide), LOW),
+            jax.ShapeDtypeStruct((count, rows, wide), LOW),
+        ],
         scratch_shapes=[
             pltpu.VMEM((count, depth, wide), LOW),
             pltpu.VMEM((rows, depth), WIDE),
@@ -693,34 +731,33 @@
     )(place, *pieces, *adds, hidden, cot, gain)
 
 
-def outer_kernel(entries, stacks, *refs):
-    n = sum(len(e) for e in entries)
-    cols, out_ref, total_ref = refs[n : n + len(stacks)], refs[-2], refs[-1]
-    spots = [(ref, i) for ref, size in zip(cols, stacks) for i in range(size)]
+def outer_kernel(entries, place_ref, cols_ref, *refs):
+    out_ref, total_ref = refs[-2:]
     at = 0
-    for (ref, i), entry in zip(spots, entries):
+    for b, entry in enumerate(entries):
+        cols = cols_ref[jnp.bitwise_xor(place_ref[0], b)]
         row = 0
         for size in entry:
-            part = dot(refs[at][...], ref[i, row : row + size], 0, 0)
+            part = dot(refs[at][...], cols[row : row + size], 0, 0)
             total_ref[...] = part if at == 0 else total_ref[...] + part
             row, at = row + size, at + 1
     out_ref[...] = total_ref[...].astype(LOW)
 
 
-def run_outer(entries, cols, name):
+def run_outer(place, entries, cols, name):
     pieces = flat(entries)
-    shape = (pieces[0].shape[1], cols[0].shape[-1])
+    shape = (pieces[0].shape[1], cols.shape[-1])
     vmem = pl.BlockSpec(memory_space=FULL)
     return pl.pallas_call(
-        functools.partial(outer_kernel, heights(entries), [c.shape[0] for c in cols]),
-        in_specs=[vmem] * (len(pieces) + len(cols)),
+        functools.partial(outer_kernel, heights(entries)),
+        in_specs=[pl.BlockSpec(memory_space=pltpu.SMEM)] + [vmem] * (len(pieces) + 1),
         out_specs=vmem,
         out_shape=jax.ShapeDtypeStruct(shape, LOW),
         scratch_shapes=[pltpu.VMEM(shape, WIDE)],
         compiler_params=PARAMS,
         cost_estimate=cost(8),
         name=name,
-    )(*pieces, *cols)
+    )(place, cols, *pieces)
 
 
 def spread_kernel(entries, layout, place_ref, *refs):
@@ -842,22 +879,21 @@
     cot_far = gather_far([after(c, *normed_far) for c in cot_first])
     cot_parts = gather_rest(cot_first, cot_far)
 
-    wio_late = after(wio, *cot_far)
+    wio_late = after(wio, *normed_far, *cot_far)
     proj, logits, normed_all = run_project(normed_parts, wio_late, beta_own, 3 * wide)
-    wout_first = gather_start(wio[:, 3 * wide :])
+    wout_first = gather_start(wio_late[:, 3 * wide :])
     proj = proj.reshape(count, seqs, length, 3 * wide)
     logits = logits.reshape(count, seqs, length, 128)
-    wout_far, out_parts, saved = [], [], []
+    wout_far, out_parts, saved = [], [], None
     for b in range(seqs):
         late = [after(proj, *wout_first), after(proj, *wout_far)][min(b - 1, 1)] if b else proj
-        mixed_out, *kept = run_mixer_forward(b, place_arr, late, conv_own, logits, head_weight)
-        saved.append(kept)
+        mixed_out, *saved = run_mixer_forward(b, place_arr, late, conv_own, logits, head_weight, saved)
         if b == 0:
             wout_far = gather_far(wout_first)
+            wout_parts = gather_rest(wout_first, wout_far)
         if b == seqs - 1:
-            mixed_out = after(mixed_out, *wout_far)
-        out_parts += exchange_xor(mixed_out)
-    wout_parts = gather_rest(wout_first, wout_far)
+            mixed_out = after(mixed_out, *wout_far, *out_parts)
+        out_parts.append(exchange(mixed_out))
     hidden, normed_two, out_rows = run_branch(
         place_arr, wout_parts, out_parts, tokens.reshape(rows, width), second_weight[None]
     )
@@ -867,69 +903,53 @@
     def to_owner(partial):
         return lax.psum_scatter(partial, "fsdp", scatter_dimension=0, tiled=True)
 
-    out_first = gather_start(after(out_rows, inner))
-    inner_late = after(inner, wdown)
-    gwdown = jnp.einsum("brf,brd->fd", inner_late, cot_all, preferred_element_type=WIDE).astype(LOW)
-    up_slope, gwdown = lax.optimization_barrier((up_slope, gwdown, *out_first))[:2]
-    gwdown = to_owner(gwdown)
-
+    out_first = gather_start(after(out_rows, *two_parts[6]))
+    up_slope = after(up_slope, *out_first)
     ggu, gtwo_even, gtwo_odd = run_gate_back(cot_all, up_slope, gate_slope, wdown, wgu)
     gtwo_twin = reduce_start(gtwo_odd)
-    out_far = gather_far(out_first)
-    ggu = after(ggu, *out_far)
+    gwdown = jnp.einsum("brf,brd->fd", after(inner, ggu), cot_all, preferred_element_type=WIDE).astype(LOW)
+    gtwo_even, gwdown = lax.optimization_barrier((gtwo_even, gwdown))
+    gwdown = to_owner(gwdown)
+    gtwo_state = reduce_add(gtwo_even, gtwo_twin)
+    ggu, *gtwo_state = lax.optimization_barrier((ggu, *gtwo_state))
+    gtwo_state = reduce_far(gtwo_state)
     gwgu = jnp.einsum("brd,brf->df", two_all, ggu, preferred_element_type=WIDE).astype(LOW)
-    gtwo_even, gwgu = lax.optimization_barrier((gtwo_even, gwgu))
-    gtwo_state = reduce_far(gtwo_even, gtwo_twin)
-    down_even, down_odd = run_pairs([(after(inner, gwgu), wdown, 0)], width, "down")
-    gwgu = to_owner(after(gwgu, gwdown))
-    gtwo_parts = reduce_last(gtwo_state)
+    gtwo_state[0], gwgu = lax.optimization_barrier((gtwo_state[0], gwgu))
+    gtwo_parts = reduce_last(reduce_more(gtwo_state))
+    down_even, down_odd = run_pairs([(after(inner, gwgu), wdown, 0)], width, "down", 12)
     hidden_late = after(hidden, down_odd)
-
-    ghidden, gsecond, gbranch, *gouts = run_branch_back(
-        place_arr, wout_parts, gtwo_parts, hidden_late, cot_own, second_weight[None], seqs
-    )
-    gouts = [exchange_xor(g) for g in gouts]
-    gwdown_first = gather_start(after(gwdown, ghidden))
-    gwdown_far = gather_far(gwdown_first)
+    gwgu = to_owner(gwgu)
+
+    ghidden, gsecond, gbranch, gout = run_branch_back(
+        place_arr, wout_parts, gtwo_parts, hidden_late, cot_own, second_weight[None]
+    )
     down_twin = reduce_start(after(down_odd, ghidden))
-    held, gtaps, ggain = None, [], []
-    for b in range(seqs):
-        gout = gouts[b]
-        if b == seqs - 1:
-            gout[0] = after(gout[0], *gwdown_first)
-        *held, gtap, ghead = run_mixer_backward(
-            b, place_arr, proj, conv_own, logits, head_weight, gout, saved[b], held
-        )
-        gtaps.append(gtap)
-        ggain.append(ghead)
-    gproj, glogit = held
-    gproj = after(gproj, *gwdown_far, gwgu, down_twin)
+    gout = exchange(gout)
+    down_state = reduce_add(down_even, down_twin)
+    gout, gwdown, *down_state = lax.optimization_barrier((gout, gwdown, *down_state))
+    gwdown_first = gather_start(gwdown, True)
+    out_far = gather_far([after(x, gout) for x in out_first])
+    down_state = reduce_far(down_state)
+    gproj, glogit, gtaps, ggain = run_mixer_backward(
+        place_arr, proj, conv_own, logits, head_weight, gout, saved
+    )
+    gproj, *both = lax.optimization_barrier((gproj, *out_far, *down_state))
+    out_far, down_state = both[: len(out_far)], both[len(out_far) :]
     gproj = gproj.reshape(count, rows, 3 * wide)
     glogit = glogit.reshape(count, rows, 128)
+    gnormed_even, gnormed_odd = run_pairs([(gproj, wio, 1), (glogit, beta_own, 0)], width, "input_back", 1)
+    gnormed_twin = reduce_start(gnormed_odd)
+    gbeta = jnp.einsum(
+        "brh,brd->hd", after(glogit, gnormed_even), normed_all, preferred_element_type=WIDE
+    )[:heads]
+    gnormed_twin, gbeta, *gwdown_first = lax.optimization_barrier((gnormed_twin, gbeta, *gwdown_first))
+    gwdown_far = gather_far(gwdown_first)
+    gwdown_parts = gather_rest(gwdown_first, gwdown_far)
+    gnormed_state = reduce_add(gnormed_even, gnormed_twin)
+    gproj, *gnormed_state = lax.optimization_barrier((gproj, *gnormed_state))
+    gproj, gwgu = lax.optimization_barrier((gproj, gwgu))
     gwin = jnp.einsum("brd,bre->de", normed_all, gproj, preferred_element_type=WIDE).astype(LOW)
-    down_state = reduce_far(down_even, down_twin)
-    gbranch_cols = exchange_xor(after(gbranch, gouts[-1][-1]))
-    gproj, gwin = lax.optimization_barrier((gproj, gwin, *down_state, *gbranch_cols))[:2]
-    gwin = to_owner(gwin)
-    gnormed_even, gnormed_odd = run_pairs([(gproj, wio, 1), (glogit, beta_own, 0)], width, "input_back")
-    gnormed_twin = reduce_start(gnormed_odd)
-    down = reduce_last(down_state)
-    output = (hidden + sum(jnp.concatenate(e).astype(WIDE) for e in down)).astype(LOW)
-    gnormed_state = reduce_far(gnormed_even, after(gnormed_twin, output))
-    out_all_parts = gather_rest(out_first, out_far)
-    gwout = run_outer(out_all_parts, [after(gbranch_cols[0], *gnormed_twin)] + gbranch_cols[1:], "output_weights")
-    gnormed_state[0], gwout = lax.optimization_barrier((gnormed_state[0], gwout))
-    gnormed = reduce_last(gnormed_state)
-    gwgu_first = gather_start(after(gwgu, *gnormed_state[4:]))
-    gwdown_parts = gather_rest(gwdown_first, gwdown_far)
-    gnormed[0][0], gwin, *_ = lax.optimization_barrier((gnormed[0][0], gwin, *gwgu_first))
-    gwout = to_owner(after(gwout, gwin))
-
-    gnormed = sum(jnp.concatenate(e).astype(WIDE) for e in gnormed)
-    input_grad = ghidden + norm_back(inputs, first_scale, gnormed, first_weight)
-    gfirst = jnp.sum(gnormed * inputs * first_scale, axis=0)
-    gtaps, ggain = sum(gtaps), sum(ggain)
-
+    gnormed_state = reduce_far(gnormed_state)
     lanes = min(256, width)
     gwdown = run_spread(
         place_arr,
@@ -942,9 +962,51 @@
         lambda g: (0, g),
         "spread_down",
     )
-    tall = min(64, part)
-    gwgu_far = gather_far([after(g, gwdown) for g in gwgu_first])
+    gnormed_state[0], gwin = lax.optimization_barrier((gnormed_state[0], gwin))
+    gwin = to_owner(gwin)
+    gnormed_state = reduce_more(gnormed_state)
+    gnormed = reduce_last(gnormed_state)
+    down_state[0] = after(down_state[0], *gnormed_state)
+    down_state = reduce_more(down_state)
+    gbranch_cols = exchange(after(gbranch, *gnormed_state[2:4]))
+    gwgu_first = gather_start(after(gwgu, *gnormed_state[2:]), True)
+    gnormed = total_of(gnormed)
+    input_grad = ghidden + norm_back(inputs, first_scale, gnormed, first_weight)
+    gfirst = jnp.sum(gnormed * inputs * first_scale, axis=0)
+    down_state[0], gfirst = lax.optimization_barrier((down_state[0], gfirst))
+    down = reduce_last(down_state)
+    output = (hidden + total_of(down)).astype(LOW)
+
+
+    out_all_parts = gather_rest(out_first, out_far)
+    gwout = run_outer(place_arr, out_all_parts, gbranch_cols, "output_weights")
+    gtaps = jnp.sum(gtaps, axis=0).transpose(1, 2, 0, 3).reshape(3 * taps, wide)
+    ggain = jnp.sum(ggain, axis=(0, 1)).reshape(shards, 1, dim // shards)
+    ggain = jnp.pad(ggain, ((0, 0), (0, 0), (0, wide - dim // shards)))
+    owner = (iota((shards, 1, 1), 0) == place * wide // part).astype(WIDE)
+    cells = part // wide
+    gains = jnp.stack([gfirst, gsecond[0]]).reshape(2, shards, cells, wide).transpose(1, 0, 2, 3)
+    gbeta = gbeta.reshape(heads, shards, cells, wide).transpose(1, 0, 2, 3)
+    extra = jnp.concatenate(
+        [
+            gains.reshape(shards, 2 * cells, wide),
+            gbeta.reshape(shards, heads * cells, wide),
+            owner * gtaps[None],
+            ggain,
+        ],
+        axis=1,
+    )
+    used = extra.shape[1]
+    extra = jnp.pad(extra, ((0, 0), (0, -used % 32), (0, 0))).astype(LOW)
+    more = extra.shape[1]
+    gwout = jnp.concatenate([gwout.reshape(shards, part, wide), extra], axis=1)
+    gwout = gwout.reshape(shards * (part + more), wide)
+    gwgu_first[0], gwout, gwdown = lax.optimization_barrier((gwgu_first[0], gwout, gwdown))
+    gwgu_far = gather_far([after(x, gwgu_first[0]) for x in gwgu_first])
+    gwout = to_owner(gwout)
+
     gwgu_parts = gather_rest(gwgu_first, gwgu_far)
+    tall = min(128, part)
     gwin_first = gather_start(after(gwin, *gwgu_far))
     gwgu = run_spread(
         place_arr,
@@ -967,7 +1029,8 @@
     )
     gwin_far = gather_far([after(g, gwgu) for g in gwin_first])
     gwin_parts = gather_rest(gwin_first, gwin_far)
-    gwout_parts = gather_xor(after(gwout, *gwin_far))
+    gwout_first = gather_start(after(gwout, *gwin_far))
+    gwout_parts = gather_rest(gwout_first, gather_far(gwout_first, False))
     gwin = run_spread(
         place_arr,
         gwin_parts,
@@ -988,7 +1051,7 @@
         "spread_inputs",
     )
     gwout = run_spread(
-        after(place_arr, gwin),
+        place_arr,
         gwout_parts,
         (tall, wide),
         part // tall,
@@ -998,31 +1061,29 @@
         lambda g: (g, 0),
         "spread_output",
     )
-
-    gbeta = jnp.einsum("brh,brd->hd", glogit, normed_all, preferred_element_type=WIDE)[:heads]
-    gtaps = gtaps.transpose(1, 2, 0, 3).reshape(3 * taps, wide)
-    ggain = jnp.pad(jnp.sum(ggain, axis=0), ((0, 0), (0, width - dim)))
-    small = sum_over("fsdp", jnp.concatenate([gsecond, ggain, gbeta]))
-    gbeta = lax.dynamic_update_slice(
-        jnp.zeros((all_heads, width), WIDE), small[2:], (place * heads, 0)
-    )
-    gtaps = lax.dynamic_update_slice(
-        jnp.zeros((3 * taps, width), WIDE), sum_over("fsdp", gtaps), (0, place * wide)
-    )
-    small = sum_over("seq", jnp.concatenate([small[:2], gtaps, gbeta]))
-    own = lax.dynamic_slice_in_dim(small, shard * part, part, 1)
-    gfirst = lax.dynamic_slice_in_dim(sum_over("fsdp", sum_over("seq", gfirst[None])), shard * part, part, 1)
-    ggain = lax.dynamic_slice_in_dim(small[1], shard * (dim // shards), dim // shards, 0)
+    extra = jnp.stack([e[0][part:] for e in gwout_parts]).astype(WIDE)
+    summed = jnp.sum(extra, axis=0)
+    gains = summed[: 2 * cells].reshape(2, part)
+    ggain = summed[used - 1, : dim // shards]
+    gbeta, gtaps = [], []
+    for i in range(count):
+        rows_i = lax.dynamic_index_in_dim(extra, place ^ i, 0, False)
+        gbeta.append(rows_i[2 * cells : (2 + heads) * cells].reshape(heads, part))
+    for i in range(cells):
+        rows_i = lax.dynamic_index_in_dim(extra, place ^ (shard * cells + i), 0, False)
+        gtaps.append(rows_i[(2 + heads) * cells : used - 1])
+    gbeta = jnp.concatenate(gbeta).T
+    gtaps = jnp.concatenate(gtaps, axis=1).reshape(3, taps, part)
     return (
         output.reshape(tokens.shape),
         input_grad.reshape(tokens.shape),
-        gfirst[0],
+        gains[0],
         gwin,
-        own[2 : 2 + 3 * taps].reshape(3, taps, part),
-        own[2 + 3 * taps :].T,
+        gtaps,
+        gbeta,
         ggain,
         gwout,
-        own[0],
+        gains[1],
         gwgu,
         gwdown,
     )

time: 765 us -> 701 us (0.916)
  local copies, waits for them, and re-layouts: 67.4 us -> 40.3 us
  starting transfers between devices: 98.4 us -> 78.4 us
  waiting for transfers between devices: 257 us -> 246 us
  Pallas kernels: 217 us -> 208 us
    ppermute x120 -> x92, waiting for transfers between devices: 254 us -> 220 us  [swap(): return lax.ppermute(x, 'seq', [(i, i ^ bits) for i in range(count)])]
    ppermute x120 -> x92, starting transfers between devices: 84.2 us -> 61.5 us  [swap(): return lax.ppermute(x, 'seq', [(i, i ^ bits) for i in range(count)])]
    all_to_all x0 -> x4, starting transfers between devices: none -> 15.7 us  [exchange(): return lax.all_to_all(parts, 'seq', split_axis=0, concat_axis=0, tiled=True)]
    squeeze x13 -> x3, local copies, waits for them, and re-layouts: 17 us -> 1.75 us  [the longest x2 1.22 us: total_of(): a[0]]
    all_to_all x0 -> x4, waiting for transfers between devices: none -> 14.2 us  [exchange(): return lax.all_to_all(parts, 'seq', split_axis=0, concat_axis=0, tiled=True)]
    ppermute x12 -> x0, starting transfers between devices: 12.5 us -> none  [sum_over(): x = x + lax.ppermute(x, axis, [(i, i ^ bits) for i in range(count)])]
    all_gather x3, waiting for transfers between devices: 0.02 us -> 12 us  [over_shards(): return lax.all_gather(x, 'fsdp', axis=axis, tiled=True)]
    slice x20 -> x4, local copies, waits for them, and re-layouts: 11.3 us -> 1.34 us  [the longest x1 1.29 us: local(): wout_first = gather_start(wio_late[:, 3 * wide:])]
  transfers between devices with their start and end apart: 139 -> 103, of which waited for: 52 -> 35; matrix products, arithmetic and copies ran while one was open for 19% -> 16% of each run, Pallas kernels for 26% -> 25%
where the time goes in v2:
time: 701 us; the launch traced here: 691 us
  waiting for transfers between devices  246 us (35%)
  Pallas kernels  208 us (30%)
  starting transfers between devices  78.4 us (11%)
  matrix products  44.1 us (6%)
  other arithmetic  43.5 us (6%)
  local copies, waits for them, and re-layouts  40.3 us (6%)
  between operations  15.6 us (2%)
  blocking collectives  14.9 us (2%)
    ppermute x92, waiting for transfers between devices, swap(): return lax.ppermute(x, 'seq', [(i, i ^ bits) for i in range(count)])  220 us
    ppermute x92, starting transfers between devices, swap(): return lax.ppermute(x, 'seq', [(i, i ^ bits) for i in range(count)])  61.5 us
    pallas_call x4, Pallas kernels, run_spread(): pl.pallas_call(functools.partial(spread_kernel, heights(entries), layout)...  35.8 us
    pallas_call x1, Pallas kernels, run_gate_back(): pl.pallas_call(gate_back_kernel, grid=(count // 2,), in_specs=[block(widt...  32.1 us
    pallas_call x1, Pallas kernels, run_mixer_backward(): pl.pallas_call(mixer_backward, out_shape=shapes, grid_spec=pltpu.Prefetch...  26.5 us
    pallas_call x1, Pallas kernels, run_gate(): pl.pallas_call(functools.partial(gate_kernel, sizes, heights(others)), gr...  25.6 us
    convert_element_type x12, other arithmetic, add(): return (first.astype(WIDE) + second.astype(WIDE)).astype(LOW)  24.3 us
    pallas_call x2, Pallas kernels, run_pairs(): pl.pallas_call(functools.partial(pairs_kernel, len(terms), [t[2] for t in...  23.7 us
  transfers between devices with their start and end apart: 103, of which 35 were waited for; matrix products, arithmetic and copies ran while one was open for 16% of the time, Pallas kernels for 25%

profile of v2, /device:TPU:0, one launch (start us, length us, event | category | flops | bytes accessed | tf_op | source)
XLA Modules:
  0.0 691.0 jit_solution(11330838056760712189)
XLA Ops:
  23.1 14.9 %all-gather.1 = bf16[4,31,512]{2,1,0:T(8,128)(2,1)S(1)} all-gather(bf16[1,31,512]{2,1,0:T(8,128)(2,1)S(1)} %bitcast.192), channel_id=2, replica_groups=mesh['fsdp'=4,'seq'=8] {'fsdp'}, dimensions={0}, use_global_device_ids=true | all-gather | bytes 158720 | tf_op jit(solution)/shard_map/all_gather | solution.py:845
  42.8 22.2 %collective-permute-done.3.refs_4_ = bf16[256,2048]{1,0:T(8,128)(2,1)} collective-permute-done((bf16[256,2048]{1,0:T(8,128)(2,1)S(1)}, bf16[256,2048]{1,0:T(8,128)(2,1)}, u32[]{:S(2)}, u32[]{:S(2)}) %collective-permute-start.3) | collective-permute-done | bytes 1048608 | tf_op jit(solution)/shard_map/ppermute | solution.py:16
  69.4 8.9 %collective-permute-done.4.refs_6_ = bf16[128,2048]{1,0:T(8,128)(2,1)S(1)} collective-permute-done((bf16[128,2048]{1,0:T(8,128)(2,1)S(1)}, bf16[128,2048]{1,0:T(8,128)(2,1)S(1)}, u32[]{:S(2)}, u32[]{:S(2)}) %collective-permute-start.4) | collective-permute-done | bytes 524320 | tf_op jit(solution)/shard_map/ppermute | solution.py:16
  85.8 7.5 %collective-permute-done.7.refs_16_ = bf16[128,2048]{1,0:T(8,128)(2,1)S(1)} collective-permute-done((bf16[128,2048]{1,0:T(8,128)(2,1)S(1)}, bf16[128,2048]{1,0:T(8,128)(2,1)S(1)}, u32[]{:S(2)}, u32[]{:S(2)}) %collective-permute-start.7) | collective-permute-done | bytes 524320 | tf_op jit(solution)/shard_map/ppermute | solution.py:16
  102.3 14.6 %project.1 = (bf16[8,256,768]{2,1,0:T(8,128)(2,1)}, f32[8,256,128]{2,1,0:T(8,128)}, bf16[8,256,2048]{2,1,0:T(8,128)(2,1)}) custom-call(bf16[256,2048]{1,0:T(8,128)(2,1)} %copy-done.17, bf16[256,2048]{1,0:T(8,128)(2,1)} %collective-permute-done.18.refs_1_, bf16[256,2048]{1,0:T(8,128)(2,1)} %collective-permute-done.5.refs_2_, ...), custom_call_target="tpu_custom_call" | custom-call | flops 18400000000 | bytes 56000000 | tf_op jit(solution)/shard_map/project/pallas_call | solution.py:456
  117.0 8.6 %collective-permute-done.12.refs_4_ = bf16[2048,256]{1,0:T(8,128)(2,1)S(1)} collective-permute-done((bf16[2048,256]{1,0:T(8,128)(2,1)S(1)}, bf16[2048,256]{1,0:T(8,128)(2,1)S(1)}, u32[]{:S(2)}, u32[]{:S(2)}) %collective-permute-start.12) | collective-permute-done | bytes 1048608 | tf_op jit(solution)/shard_map/ppermute | solution.py:16
  128.9 10.9 %mixer_forward.2 = (bf16[8,128,256]{2,1,0:T(8,128)(2,1)}, f32[2,2,8,128,128]{4,3,2,1,0:T(8,128)}, bf16[2,2,8,128,128]{4,3,2,1,0:T(8,128)(2,1)}, bf16[2,2,8,128,1...) custom-call(s32[1]{0:T(128)} %bitcast.place_ref, ...), custom_call_target="tpu_custom_call" | custom-call | flops 11500000256 | bytes 35000000 | tf_op jit(solution)/shard_map/mixer_forward/pallas_call | solution.py:332
  139.8 3.7 all-to-all-start
  144.6 10.9 %mixer_forward.3 = (bf16[8,128,256]{2,1,0:T(8,128)(2,1)}, f32[2,2,8,128,128]{4,3,2,1,0:T(8,128)}, bf16[2,2,8,128,128]{4,3,2,1,0:T(8,128)(2,1)}, bf16[2,2,8,128,1...) custom-call(s32[1]{0:T(128)} %bitcast.place_ref, ...), custom_call_target="tpu_custom_call", output_to_operand_aliasing={{1}: (5, {}), {2}: (6, {}), {3}: (7, {}), {4}: (8, {}), {5}... | custom-call | flops 11500000256 | bytes 35000000 | tf_op jit(solution)/shard_map/mixer_forward/pallas_call | solution.py:332
  155.5 4.2 all-to-all-start.1
  160.4 9.1 %all-to-all-done.1.refs_11_ = bf16[8,128,256]{2,1,0:T(8,128)(2,1)S(1)} async-done(((bf16[8,128,256]{2,1,0:T(8,128)(2,1)}), bf16[8,128,256]{2,1,0:T(8,128)(2,1)S(1)}, u32[]{:S(2)}, u32[]{:S(2)}) %all-to-all-start.1) | async-done | bytes 524320 | tf_op jit(solution)/shard_map/all_to_all | solution.py:112
  170.8 10.6 %branch.1 = (f32[256,2048]{1,0:T(8,128)}, bf16[256,2048]{1,0:T(8,128)(2,1)}, bf16[256,2048]{1,0:T(8,128)(2,1)}) custom-call(s32[1]{0:T(128)} %bitcast.place_ref, bf16[2048,256]{1,0:T(8,128)(2,1)} %copy-done.15, bf16[2048,256]{1,0:T(8,128)(2,1)} %collective-permute-done.9.refs_1_, bf16[2048,256]{1,0:T(8,128)(2,1)} %collective-permute-done.10.refs_2_, ...), custom_call_target="tpu_custom_call" | custom-call | flops 11500000256 | bytes 35000000 | tf_op jit(solution)/shard_map/branch/pallas_call | solution.py:632
  183.7 21.0 %collective-permute-done.26.refs_4_ = bf16[256,2048]{1,0:T(8,128)(2,1)S(1)} collective-permute-done((bf16[256,2048]{1,0:T(8,128)(2,1)}, bf16[256,2048]{1,0:T(8,128)(2,1)S(1)}, u32[]{:S(2)}, u32[]{:S(2)}) %collective-permute-start.26) | collective-permute-done | bytes 1048608 | tf_op jit(solution)/shard_map/ppermute | solution.py:16
  210.0 11.1 %collective-permute-done.28.refs_6_ = bf16[128,2048]{1,0:T(8,128)(2,1)} collective-permute-done((bf16[128,2048]{1,0:T(8,128)(2,1)S(1)}, bf16[128,2048]{1,0:T(8,128)(2,1)}, u32[]{:S(2)}, u32[]{:S(2)}) %collective-permute-start.28) | collective-permute-done | bytes 524320 | tf_op jit(solution)/shard_map/ppermute | solution.py:16
  226.6 25.6 %gate.1 = (bf16[8,256,704]{2,1,0:T(8,128)(2,1)}, bf16[8,256,704]{2,1,0:T(8,128)(2,1)}, bf16[8,256,704]{2,1,0:T(8,128)(2,1)}, bf16[8,256,2048]{2,1,0:T(8,128)(2,1)}, bf16[8,256,2048]{2,1,0:T(8,128)(2,1)}) custom-call(bf16[256,2048]{1,0:T(8,128)(2,1)} %get-tuple-element.167.refs_0_, bf16[256,2048]{1,0:T(8,128)(2,1)} %copy-done.50, ...), custom_call_target="tpu_custom_call" | custom-call | flops 28750000128 | bytes 87500000 | tf_op jit(solution)/shard_map/gate/pallas_call | solution.py:513
  252.3 11.3 %all-gather.10.cloned.1.call-done.down_ref.refs_1_ = bf16[704,2048]{1,0:T(8,128)(2,1)} async-done(((bf16[176,2048]{1,0:T(8,128)(2,1)}), bf16[704,2048]{1,0:T(8,128)(2,1)}) %all-gather.10.cloned.1.call-update) | async-done | bytes 2883600 | tf_op jit(solution)/shard_map/all_gather | solution.py:834
  263.7 32.1 %gate_back.1 = (bf16[8,256,1408]{2,1,0:T(8,128)(2,1)}, bf16[4,256,2048]{2,1,0:T(8,128)(2,1)}, bf16[4,256,2048]{2,1,0:T(8,128)(2,1)}) custom-call(bf16[8,256,2048]{2,1,0:T(8,128)(2,1)} %get-tuple-element.168.cot_ref, bf16[8,256,704]{2,1,0:T(8,128)(2,1)} %get-tuple-element.172.up_ref, bf16[8,256,704]{2,1,0:T(8,128)(2,1)} %get-tuple-element.173.gate_ref, ...), custom_call_target="tpu_custom_call" | custom-call | flops 36800000000 | bytes 112000000 | tf_op jit(solution)/shard_map/gate_back/pallas_call | solution.py:557
  295.8 10.7 %bitcast_convert_fusion.2 = bf16[704,2048]{1,0:T(8,128)(2,1)} fusion(bf16[8,256,704]{2,1,0:T(8,128)(2,1)} %get-tuple-element.196.refs_0_, bf16[8,256,2048]{2,1,0:T(8,128)(2,1)} %get-tuple-element.168.cot_ref), kind=kOutput, calls=%fused_computation.2 | convolution fusion | flops 5907021824 | bytes 14155776 | tf_op jit(solution)/shard_map/brf,brd->fd/dot_general | solution.py:910
  315.3 17.1 %bitcast_convert_fusion = bf16[2048,1408]{1,0:T(8,128)(2,1)} fusion(bf16[8,256,2048]{2,1,0:T(8,128)(2,1)S(1)} %copy-done.67, bf16[8,256,1408]{2,1,0:T(8,128)(2,1)} %get-tuple-element.182), kind=kOutput, calls=%fused_computation | convolution fusion | flops 11814043648 | bytes 19922944 | tf_op jit(solution)/shard_map/brd,brf->df/dot_general | solution.py:916
  332.4 5.7 collective-permute-done.40.refs_12_
  343.7 10.6 %down.1 = (bf16[4,256,2048]{2,1,0:T(8,128)(2,1)}, bf16[4,256,2048]{2,1,0:T(8,128)(2,1)}) custom-call(bf16[8,256,704]{2,1,0:T(8,128)(2,1)} %get-tuple-element.196.refs_0_, bf16[704,2048]{1,0:T(8,128)(2,1)} %all-gather.10.cloned.1.call-done.down_ref.refs_1_), custom_call_target="tpu_custom_call" | custom-call | flops 13799999488 | bytes 42000000 | tf_op jit(solution)/shard_map/down/pallas_call | solution.py:588
  356.2 9.8 %branch_back.1 = (f32[256,2048]{1,0:T(8,128)}, f32[1,2048]{1,0:T(1,128)}, bf16[8,256,256]{2,1,0:T(8,128)(2,1)}, bf16[8,256,256]{2,1,0:T(8,128)(2,1)}) custom-call(s32[1]{0:T(128)} %bitcast.place_ref, bf16[2048,256]{1,0:T(8,128)(2,1)} %copy-done.15, bf16[2048,256]{1,0:T(8,128)(2,1)} %collective-permute-done.9.refs_1_, ...), custom_call_target="tpu_custom_call" | custom-call | flops 11500000256 | bytes 35000000 | tf_op jit(solution)/shard_map/branch_back/pallas_call | solution.py:704
  366.1 3.6 all-to-all-start.2
  375.5 4.5 add_convert_fusion.2
  379.9 5.1 all-to-all-done.2.gout_ref
  390.8 26.5 %mixer_backward.1 = (bf16[8,2,128,768]{3,2,1,0:T(8,128)(2,1)}, bf16[8,2,128,128]{3,2,1,0:T(8,128)(2,1)}, f32[2,2,3,4,128]{4,3,2,1,0:T(4,128)}, f32[2,2,1,128]{3,2,1,0:T(1,128)}) custom-call(s32[1]{0:T(128)} %bitcast.place_ref, bf16[8,2,128,768]{3,2,1,0:T(8,128)(2,1)} %bitcast.210, f32[2,3,4,128]{3,2,1,0:T(4,128)} %copy_bitcast_fusion.taps_ref, ...), custom_call_target="tpu_custom_call" | custom-call | flops 29899999232 | bytes 91000000 | tf_op jit(solution)/shard_map/mixer_backward/pallas_call | solution.py:364
  417.3 4.6 collective-permute-done.47
  424.3 13.1 %input_back.1 = (bf16[4,256,2048]{2,1,0:T(8,128)(2,1)}, bf16[4,256,2048]{2,1,0:T(8,128)(2,1)}) custom-call(bf16[8,256,768]{2,1,0:T(8,128)(2,1)} %bitcast.185, bf16[8,256,128]{2,1,0:T(8,128)(2,1)} %bitcast.187, bf16[2048,1024]{1,0:T(8,128)(2,1)} %all-gather.6.cloned.1.call-done.refs_10_.refs_2_, bf16[128,2048]{1,0:T(8,128)(2,1)} %pad.19.refs_11_.refs_3_), custom_call_target="tpu_custom_call" | custom-call | flops 1150000000 | bytes 3500000 | tf_op jit(solution)/shard_map/input_back/pallas_call | solution.py:588
  439.1 6.5 collective-permute-done.50.refs_1_
  446.0 10.4 %collective-permute-done.51.refs_2_ = bf16[176,2048]{1,0:T(8,128)(2,1)} collective-permute-done((bf16[176,2048]{1,0:T(8,128)(2,1)}, bf16[176,2048]{1,0:T(8,128)(2,1)}, u32[]{:S(2)}, u32[]{:S(2)}) %collective-permute-start.51) | collective-permute-done | bytes 720928 | tf_op jit(solution)/shard_map/ppermute | solution.py:16
  456.5 4.9 convolution_bitcast_fusion
  463.1 3.6 add_convert_fusion
  469.1 11.4 %bitcast_convert_fusion.1 = bf16[2048,768]{1,0:T(8,128)(2,1)} fusion(bf16[8,256,2048]{2,1,0:T(8,128)(2,1)} %get-tuple-element.229, bf16[8,256,768]{2,1,0:T(8,128)(2,1)} %bitcast.186), kind=kOutput, calls=%fused_computation.1 | convolution fusion | flops 6444023808 | bytes 14680064 | tf_op jit(solution)/shard_map/brd,bre->de/dot_general | solution.py:951
  483.7 22.9 %collective-permute-done.65.refs_6_ = bf16[176,2048]{1,0:T(8,128)(2,1)} collective-permute-done((bf16[176,2048]{1,0:T(8,128)(2,1)}, bf16[176,2048]{1,0:T(8,128)(2,1)}, u32[]{:S(2)}, u32[]{:S(2)}) %collective-permute-start.65) | collective-permute-done | bytes 720928 | tf_op jit(solution)/shard_map/ppermute | solution.py:16
  510.1 4.2 all-to-all-start.3
  519.1 9.1 %spread_down.1 = f32[1408,2048]{1,0:T(8,128)} custom-call(s32[1]{0:T(128)} %bitcast.place_ref, bf16[176,2048]{1,0:T(8,128)(2,1)} %reduce-scatter.5.cloned.1.call-done.refs_0_, bf16[176,2048]{1,0:T(8,128)(2,1)} %copy-done.54, bf16[176,2048]{1,0:T(8,128)(2,1)} %collective-permute-done.51.refs_2_, bf16[176,2048]{1,0:T(8,128)(2,1)} %collective-permute-done.63.refs_3_, ...), custom_call_target="tpu_custom_call" | custom-call | flops 11500000256 | bytes 35000000 | tf_op jit(solution)/shard_map/spread_down/pallas_call | solution.py:788
  528.2 11.8 %collective-permute-done.55 = bf16[128,2048]{1,0:T(8,128)(2,1)S(1)} collective-permute-done((bf16[128,2048]{1,0:T(8,128)(2,1)}, bf16[128,2048]{1,0:T(8,128)(2,1)S(1)}, u32[]{:S(2)}, u32[]{:S(2)}) %collective-permute-start.55) | collective-permute-done | bytes 524320 | tf_op jit(solution)/shard_map/ppermute | solution.py:16
  545.6 4.6 fusion.9
  550.3 7.6 %output_weights.1 = bf16[2048,256]{1,0:T(8,128)(2,1)} custom-call(s32[1]{0:T(128)} %bitcast.place_ref, bf16[8,256,256]{2,1,0:T(8,128)(2,1)} %all-to-all-done.3.cols_ref, bf16[256,2048]{1,0:T(8,128)(2,1)} %get-tuple-element.171.refs_0_, bf16[256,2048]{1,0:T(8,128)(2,1)} %collective-permute-done.36.refs_1_, bf16[256,2048]{1,0:T(8,128)(2,1)} %copy-done.21, ...), custom_call_target="tpu_custom_call" | custom-call | flops 9200000000 | bytes 28000000 | tf_op jit(solution)/shard_map/output_weights/pallas_call | solution.py:751
  560.2 17.7 %collective-permute-done.68.refs_2_ = bf16[512,1408]{1,0:T(8,128)(2,1)} collective-permute-done((bf16[512,1408]{1,0:T(8,128)(2,1)}, bf16[512,1408]{1,0:T(8,128)(2,1)}, u32[]{:S(2)}, u32[]{:S(2)}) %collective-permute-start.68) | collective-permute-done | bytes 1441824 | tf_op jit(solution)/shard_map/ppermute | solution.py:16
  585.8 12.2 %collective-permute-done.70.refs_6_ = bf16[256,1408]{1,0:T(8,128)(2,1)} collective-permute-done((bf16[256,1408]{1,0:T(8,128)(2,1)}, bf16[256,1408]{1,0:T(8,128)(2,1)}, u32[]{:S(2)}, u32[]{:S(2)}) %collective-permute-start.70) | collective-permute-done | bytes 720928 | tf_op jit(solution)/shard_map/ppermute | solution.py:16
  607.2 13.8 %spread_gate_up.1 = f32[2,512,5632]{2,1,0:T(8,128)} custom-call(s32[1]{0:T(128)} %bitcast.place_ref, bf16[512,1408]{1,0:T(8,128)(2,1)} %reduce-scatter.7.cloned.1.call-done.refs_0_, bf16[512,1408]{1,0:T(8,128)(2,1)} %collective-permute-done.67.refs_1_, bf16[512,1408]{1,0:T(8,128)(2,1)} %collective-permute-done.68.refs_2_, ...), custom_call_target="tpu_custom_call" | custom-call | flops 11500000256 | bytes 35000000 | tf_op jit(solution)/shard_map/spread_gate_up/pallas_call | solution.py:788
  621.0 13.9 %collective-permute-done.72.refs_4_ = bf16[512,768]{1,0:T(8,128)(2,1)} collective-permute-done((bf16[512,768]{1,0:T(8,128)(2,1)}, bf16[512,768]{1,0:T(8,128)(2,1)}, u32[]{:S(2)}, u32[]{:S(2)}) %collective-permute-start.72) | collective-permute-done | bytes 786464 | tf_op jit(solution)/shard_map/ppermute | solution.py:16
  641.5 5.1 collective-permute-done.77.refs_6_
  650.3 4.4 fusion.12
  659.0 4.6 collective-permute-done.83.refs_4_
  665.6 8.4 %spread_inputs.1 = f32[3,512,2048]{2,1,0:T(8,128)} custom-call(s32[1]{0:T(128)} %bitcast.place_ref, bf16[512,768]{1,0:T(8,128)(2,1)} %reduce-scatter.11.cloned.1.call-done.refs_0_, bf16[512,768]{1,0:T(8,128)(2,1)} %copy-done.53, bf16[512,768]{1,0:T(8,128)(2,1)} %collective-permute-done.78.refs_2_, bf16[512,768]{1,0:T(8,128)(2,1)} %collective-permute-done.88.refs_3_, ...), custom_call_target="tpu_custom_call" | custom-call | flops 11500000256 | bytes 35000000 | tf_op jit(solution)/shard_map/spread_inputs/pallas_call | solution.py:788
  679.5 4.5 spread_output.1
  (435 shorter events, 155.4 us)
Async XLA Ops:
  7.2 90.2 %all-gather.6.cloned.1.call-start = ((), (), s32[]{:S(2)}) async-start(), calls=%async_computation.8 | async-start | bytes 5242880 | tf_op jit(solution)/shard_map/all_gather | solution.py:834
  11.8 214.8 %all-gather.8.cloned.1.call-start = ((), (), s32[]{:S(2)}) async-start(), calls=%async_computation.9 | async-start | bytes 7208960 | tf_op jit(solution)/shard_map/all_gather | solution.py:834
  11.9 28.6 %collective-permute-start = (bf16[256,2048]{1,0:T(8,128)(2,1)}, bf16[256,2048]{1,0:T(8,128)(2,1)}, u32[]{:S(2)}, u32[]{:S(2)}) collective-permute-start(bf16[256,2048]{1,0:T(8,128)(2,1)} %bitcast.18.refs_10_.refs_17_), channel_id=1, source_target_pairs={{0,1},{1,0},{2,3},{3,2},{4,5},{5,4},{6,7},{7,6},{8,9},{9,8},{10,11... | collective-permute-start | bytes 3145736 | tf_op jit(solution)/shard_map/ppermute | solution.py:16
  12.4 28.1 %collective-permute-start.1 = (bf16[256,2048]{1,0:T(8,128)(2,1)}, bf16[256,2048]{1,0:T(8,128)(2,1)}, u32[]{:S(2)}, u32[]{:S(2)}) collective-permute-start(bf16[256,2048]{1,0:T(8,128)(2,1)} %bitcast.18.refs_10_.refs_17_), channel_id=1, source_target_pairs={{0,2},{1,3},{2,0},{3,1},{4,6},{5,7},{6,4},{7,5},{8,10},{9,11},{10,... | collective-permute-start | bytes 3145736 | tf_op jit(solution)/shard_map/ppermute | solution.py:16
  14.9 25.5 %collective-permute-start.2 = (bf16[256,2048]{1,0:T(8,128)(2,1)}, bf16[256,2048]{1,0:T(8,128)(2,1)}, u32[]{:S(2)}, u32[]{:S(2)}) collective-permute-start(bf16[256,2048]{1,0:T(8,128)(2,1)} %bitcast.18.refs_10_.refs_17_), channel_id=1, source_target_pairs={{0,4},{1,5},{2,6},{3,7},{4,0},{5,1},{6,2},{7,3},{8,12},{9,13},{10,... | collective-permute-start | bytes 3145736 | tf_op jit(solution)/shard_map/ppermute | solution.py:16
  40.5 24.5 %collective-permute-start.3 = (bf16[256,2048]{1,0:T(8,128)(2,1)S(1)}, bf16[256,2048]{1,0:T(8,128)(2,1)}, u32[]{:S(2)}, u32[]{:S(2)}) collective-permute-start(bf16[256,2048]{1,0:T(8,128)(2,1)S(1)} %fusion.4.refs_0_), channel_id=1, source_target_pairs={{0,4},{1,5},{2,6},{3,7},{4,0},{5,1},{6,2},{7,3},{8,12},{9,13},{10,... | collective-permute-start | bytes 3145736 | tf_op jit(solution)/shard_map/ppermute | solution.py:16
  42.0 25.5 %collective-permute-start.5 = (bf16[256,2048]{1,0:T(8,128)(2,1)S(1)}, bf16[256,2048]{1,0:T(8,128)(2,1)}, u32[]{:S(2)}, u32[]{:S(2)}) collective-permute-start(bf16[256,2048]{1,0:T(8,128)(2,1)S(1)} %fusion.4.refs_0_), channel_id=1, source_target_pairs={{0,2},{1,3},{2,0},{3,1},{4,6},{5,7},{6,4},{7,5},{8,10},{9,11},{10,... | collective-permute-start | bytes 3145736 | tf_op jit(solution)/shard_map/ppermute | solution.py:16
  98.8 44.8 %collective-permute-start.9 = (bf16[2048,256]{1,0:T(8,128)(2,1)S(1)}, bf16[2048,256]{1,0:T(8,128)(2,1)}, u32[]{:S(2)}, u32[]{:S(2)}) collective-permute-start(bf16[2048,256]{1,0:T(8,128)(2,1)S(1)} %slice.292.refs_0_), channel_id=1, source_target_pairs={{0,1},{1,0},{2,3},{3,2},{4,5},{5,4},{6,7},{7,6},{8,9},{9,8},{10,11... | collective-permute-start | bytes 3145736 | tf_op jit(solution)/shard_map/ppermute | solution.py:16
  98.9 27.8 %collective-permute-start.10 = (bf16[2048,256]{1,0:T(8,128)(2,1)S(1)}, bf16[2048,256]{1,0:T(8,128)(2,1)}, u32[]{:S(2)}, u32[]{:S(2)}) collective-permute-start(bf16[2048,256]{1,0:T(8,128)(2,1)S(1)} %slice.292.refs_0_), channel_id=1, source_target_pairs={{0,2},{1,3},{2,0},{3,1},{4,6},{5,7},{6,4},{7,5},{8,10},{9,11},{10,... | collective-permute-start | bytes 3145736 | tf_op jit(solution)/shard_map/ppermute | solution.py:16
  100.4 25.2 %collective-permute-start.12 = (bf16[2048,256]{1,0:T(8,128)(2,1)S(1)}, bf16[2048,256]{1,0:T(8,128)(2,1)S(1)}, u32[]{:S(2)}, u32[]{:S(2)}) collective-permute-start(bf16[2048,256]{1,0:T(8,128)(2,1)S(1)} %slice.292.refs_0_), channel_id=1, source_target_pairs={{0,4},{1,5},{2,6},{3,7},{4,0},{5,1},{6,2},{7,3},{8,12},{9,13},{10,... | collective-permute-start | bytes 3145736 | tf_op jit(solution)/shard_map/ppermute | solution.py:16
  143.5 25.9 %collective-permute-start.11 = (bf16[2048,256]{1,0:T(8,128)(2,1)}, bf16[2048,256]{1,0:T(8,128)(2,1)S(1)}, u32[]{:S(2)}, u32[]{:S(2)}) collective-permute-start(bf16[2048,256]{1,0:T(8,128)(2,1)} %collective-permute-done.10.refs_2_), channel_id=1, source_target_pairs={{0,1},{1,0},{2,3},{3,2},{4,5},{5,4},{6,7},{7,6},{8,9},{9,8},{10,11... | collective-permute-start | bytes 3145736 | tf_op jit(solution)/shard_map/ppermute | solution.py:16
  144.0 25.4 %collective-permute-start.13 = (bf16[2048,256]{1,0:T(8,128)(2,1)}, bf16[2048,256]{1,0:T(8,128)(2,1)}, u32[]{:S(2)}, u32[]{:S(2)}) collective-permute-start(bf16[2048,256]{1,0:T(8,128)(2,1)} %copy-done.24), channel_id=1, source_target_pairs={{0,1},{1,0},{2,3},{3,2},{4,5},{5,4},{6,7},{7,6},{8,9},{9,8},{10,11... | collective-permute-start | bytes 3145736 | tf_op jit(solution)/shard_map/ppermute | solution.py:16
  144.1 25.4 %collective-permute-start.16 = (bf16[1024,256]{1,0:T(8,128)(2,1)S(1)}, bf16[1024,256]{1,0:T(8,128)(2,1)}, u32[]{:S(2)}, u32[]{:S(2)}) collective-permute-start(bf16[1024,256]{1,0:T(8,128)(2,1)S(1)} %collective-permute-done.14.refs_6_), channel_id=1, source_target_pairs={{0,1},{1,0},{2,3},{3,2},{4,5},{5,4},{6,7},{7,6},{8,9},{9,8},{10,11... | collective-permute-start | bytes 1572872 | tf_op jit(solution)/shard_map/ppermute | solution.py:16
  144.6 24.9 %collective-permute-start.17 = (bf16[1024,256]{1,0:T(8,128)(2,1)}, bf16[1024,256]{1,0:T(8,128)(2,1)S(1)}, u32[]{:S(2)}, u32[]{:S(2)}) collective-permute-start(bf16[1024,256]{1,0:T(8,128)(2,1)} %collective-permute-done.15.refs_7_), channel_id=1, source_target_pairs={{0,1},{1,0},{2,3},{3,2},{4,5},{5,4},{6,7},{7,6},{8,9},{9,8},{10,11... | collective-permute-start | bytes 1572872 | tf_op jit(solution)/shard_map/ppermute | solution.py:16
  159.7 103.9 %all-gather.10.cloned.1.call-start = ((), (), s32[]{:S(2)}) async-start(), calls=%async_computation.10 | async-start | bytes 3604480 | tf_op jit(solution)/shard_map/all_gather | solution.py:834
  182.0 23.8 %collective-permute-start.24 = (bf16[256,2048]{1,0:T(8,128)(2,1)}, bf16[256,2048]{1,0:T(8,128)(2,1)S(1)}, u32[]{:S(2)}, u32[]{:S(2)}) collective-permute-start(bf16[256,2048]{1,0:T(8,128)(2,1)} %get-tuple-element.167.refs_0_), channel_id=1, source_target_pairs={{0,2},{1,3},{2,0},{3,1},{4,6},{5,7},{6,4},{7,5},{8,10},{9,11},{10,... | collective-permute-start | bytes 3145736 | tf_op jit(solution)/shard_map/ppermute | solution.py:16
  182.6 23.3 %collective-permute-start.32 = (bf16[256,2048]{1,0:T(8,128)(2,1)}, bf16[256,2048]{1,0:T(8,128)(2,1)}, u32[]{:S(2)}, u32[]{:S(2)}) collective-permute-start(bf16[256,2048]{1,0:T(8,128)(2,1)} %collective-permute-done.1.refs_12_), channel_id=1, source_target_pairs={{0,1},{1,0},{2,3},{3,2},{4,5},{5,4},{6,7},{7,6},{8,9},{9,8},{10,11... | collective-permute-start | bytes 3145736 | tf_op jit(solution)/shard_map/ppermute | solution.py:16
  182.6 23.9 %collective-permute-start.33 = (bf16[256,2048]{1,0:T(8,128)(2,1)}, bf16[256,2048]{1,0:T(8,128)(2,1)}, u32[]{:S(2)}, u32[]{:S(2)}) collective-permute-start(bf16[256,2048]{1,0:T(8,128)(2,1)} %collective-permute-done.2.refs_14_), channel_id=1, source_target_pairs={{0,1},{1,0},{2,3},{3,2},{4,5},{5,4},{6,7},{7,6},{8,9},{9,8},{10,11... | collective-permute-start | bytes 3145736 | tf_op jit(solution)/shard_map/ppermute | solution.py:16
  183.2 196.8 %reduce-scatter.5.cloned.1.call-start = ((), (), s32[]{:S(2)}) async-start(), calls=%async_computation.11 | async-start | bytes 3604480 | tf_op jit(solution)/shard_map/reduce_scatter | solution.py:904
  222.5 29.8 %collective-permute-start.36 = (bf16[256,2048]{1,0:T(8,128)(2,1)}, bf16[256,2048]{1,0:T(8,128)(2,1)}, u32[]{:S(2)}, u32[]{:S(2)}) collective-permute-start(bf16[256,2048]{1,0:T(8,128)(2,1)} %get-tuple-element.171.refs_0_), channel_id=1, source_target_pairs={{0,1},{1,0},{2,3},{3,2},{4,5},{5,4},{6,7},{7,6},{8,9},{9,8},{10,11... | collective-permute-start | bytes 3145736 | tf_op jit(solution)/shard_map/ppermute | solution.py:16
  223.0 29.3 %collective-permute-start.37 = (bf16[256,2048]{1,0:T(8,128)(2,1)}, bf16[256,2048]{1,0:T(8,128)(2,1)S(1)}, u32[]{:S(2)}, u32[]{:S(2)}) collective-permute-start(bf16[256,2048]{1,0:T(8,128)(2,1)} %get-tuple-element.171.refs_0_), channel_id=1, source_target_pairs={{0,2},{1,3},{2,0},{3,1},{4,6},{5,7},{6,4},{7,5},{8,10},{9,11},{10,... | collective-permute-start | bytes 3145736 | tf_op jit(solution)/shard_map/ppermute | solution.py:16
  225.3 27.1 %collective-permute-start.38 = (bf16[256,2048]{1,0:T(8,128)(2,1)}, bf16[256,2048]{1,0:T(8,128)(2,1)S(1)}, u32[]{:S(2)}, u32[]{:S(2)}) collective-permute-start(bf16[256,2048]{1,0:T(8,128)(2,1)} %get-tuple-element.171.refs_0_), channel_id=1, source_target_pairs={{0,4},{1,5},{2,6},{3,7},{4,0},{5,1},{6,2},{7,3},{8,12},{9,13},{10,... | collective-permute-start | bytes 3145736 | tf_op jit(solution)/shard_map/ppermute | solution.py:16
  306.5 162.5 %reduce-scatter.7.cloned.1.call-start = ((), (), s32[]{:S(2)}) async-start(), calls=%async_computation.12 | async-start | bytes 7208960 | tf_op jit(solution)/shard_map/reduce_scatter | solution.py:904
  312.3 25.8 %collective-permute-start.40 = (bf16[2,128,2048]{2,1,0:T(8,128)(2,1)S(1)}, bf16[2,128,2048]{2,1,0:T(8,128)(2,1)}, u32[]{:S(2)}, u32[]{:S(2)}) collective-permute-start(bf16[2,128,2048]{2,1,0:T(8,128)(2,1)S(1)} %get-tuple-element.187), channel_id=1, source_target_pairs={{0,2},{1,3},{2,0},{3,1},{4,6},{5,7},{6,4},{7,5},{8,10},{9,11},{10,... | collective-permute-start | bytes 3145736 | tf_op jit(solution)/shard_map/ppermute | solution.py:16
  313.8 25.4 %collective-permute-start.41 = (bf16[2,128,2048]{2,1,0:T(8,128)(2,1)S(1)}, bf16[2,128,2048]{2,1,0:T(8,128)(2,1)}, u32[]{:S(2)}, u32[]{:S(2)}) collective-permute-start(bf16[2,128,2048]{2,1,0:T(8,128)(2,1)S(1)} %get-tuple-element.188), channel_id=1, source_target_pairs={{0,4},{1,5},{2,6},{3,7},{4,0},{5,1},{6,2},{7,3},{8,12},{9,13},{10,... | collective-permute-start | bytes 3145736 | tf_op jit(solution)/shard_map/ppermute | solution.py:16
  369.6 234.1 %reduce-scatter.11.cloned.1.call-start = ((), (), s32[]{:S(2)}) async-start(), calls=%async_computation.14 | async-start | bytes 3932160 | tf_op jit(solution)/shard_map/reduce_scatter | solution.py:904
  386.5 36.9 %collective-permute-start.45 = (bf16[128,2048]{1,0:T(8,128)(2,1)S(1)}, bf16[128,2048]{1,0:T(8,128)(2,1)S(1)}, u32[]{:S(2)}, u32[]{:S(2)}) collective-permute-start(bf16[128,2048]{1,0:T(8,128)(2,1)S(1)} %slice.319), channel_id=1, source_target_pairs={{0,2},{1,3},{2,0},{3,1},{4,6},{5,7},{6,4},{7,5},{8,10},{9,11},{10,... | collective-permute-start | bytes 1572872 | tf_op jit(solution)/shard_map/ppermute | solution.py:16
  387.2 36.3 %collective-permute-start.46 = (bf16[128,2048]{1,0:T(8,128)(2,1)S(1)}, bf16[128,2048]{1,0:T(8,128)(2,1)}, u32[]{:S(2)}, u32[]{:S(2)}) collective-permute-start(bf16[128,2048]{1,0:T(8,128)(2,1)S(1)} %slice.320), channel_id=1, source_target_pairs={{0,4},{1,5},{2,6},{3,7},{4,0},{5,1},{6,2},{7,3},{8,12},{9,13},{10,... | collective-permute-start | bytes 1572872 | tf_op jit(solution)/shard_map/ppermute | solution.py:16
  387.9 34.0 %collective-permute-start.47 = (bf16[2,128,2048]{2,1,0:T(8,128)(2,1)}, bf16[2,128,2048]{2,1,0:T(8,128)(2,1)S(1)}, u32[]{:S(2)}, u32[]{:S(2)}) collective-permute-start(bf16[2,128,2048]{2,1,0:T(8,128)(2,1)} %get-tuple-element.219), channel_id=1, source_target_pairs={{0,2},{1,3},{2,0},{3,1},{4,6},{5,7},{6,4},{7,5},{8,10},{9,11},{10,... | collective-permute-start | bytes 3145736 | tf_op jit(solution)/shard_map/ppermute | solution.py:16
  389.3 34.1 %collective-permute-start.48 = (bf16[2,128,2048]{2,1,0:T(8,128)(2,1)S(1)}, bf16[2,128,2048]{2,1,0:T(8,128)(2,1)S(1)}, u32[]{:S(2)}, u32[]{:S(2)}) collective-permute-start(bf16[2,128,2048]{2,1,0:T(8,128)(2,1)S(1)} %copy-done.18), channel_id=1, source_target_pairs={{0,4},{1,5},{2,6},{3,7},{4,0},{5,1},{6,2},{7,3},{8,12},{9,13},{10,... | collective-permute-start | bytes 3145736 | tf_op jit(solution)/shard_map/ppermute | solution.py:16
  437.4 24.0 %collective-permute-start.49 = (bf16[4,256,2048]{2,1,0:T(8,128)(2,1)}, bf16[4,256,2048]{2,1,0:T(8,128)(2,1)}, u32[]{:S(2)}, u32[]{:S(2)}) collective-permute-start(bf16[4,256,2048]{2,1,0:T(8,128)(2,1)} %get-tuple-element.227), channel_id=1, source_target_pairs={{0,1},{1,0},{2,3},{3,2},{4,5},{5,4},{6,7},{7,6},{8,9},{9,8},{10,11... | collective-permute-start | bytes 12582920 | tf_op jit(solution)/shard_map/ppermute | solution.py:16
  438.7 104.8 %collective-permute-start.59 = (bf16[256,2048]{1,0:T(8,128)(2,1)}, bf16[256,2048]{1,0:T(8,128)(2,1)}, u32[]{:S(2)}, u32[]{:S(2)}) collective-permute-start(bf16[256,2048]{1,0:T(8,128)(2,1)} %copy-done.21), channel_id=1, source_target_pairs={{0,1},{1,0},{2,3},{3,2},{4,5},{5,4},{6,7},{7,6},{8,9},{9,8},{10,11... | collective-permute-start | bytes 3145736 | tf_op jit(solution)/shard_map/ppermute | solution.py:16
  445.6 99.4 %collective-permute-start.60 = (bf16[256,2048]{1,0:T(8,128)(2,1)}, bf16[256,2048]{1,0:T(8,128)(2,1)}, u32[]{:S(2)}, u32[]{:S(2)}) collective-permute-start(bf16[256,2048]{1,0:T(8,128)(2,1)} %copy-done.23), channel_id=1, source_target_pairs={{0,1},{1,0},{2,3},{3,2},{4,5},{5,4},{6,7},{7,6},{8,9},{9,8},{10,11... | collective-permute-start | bytes 3145736 | tf_op jit(solution)/shard_map/ppermute | solution.py:16
  466.7 39.9 %collective-permute-start.53 = (bf16[2,128,2048]{2,1,0:T(8,128)(2,1)}, bf16[2,128,2048]{2,1,0:T(8,128)(2,1)S(1)}, u32[]{:S(2)}, u32[]{:S(2)}) collective-permute-start(bf16[2,128,2048]{2,1,0:T(8,128)(2,1)} %get-tuple-element.243), channel_id=1, source_target_pairs={{0,2},{1,3},{2,0},{3,1},{4,6},{5,7},{6,4},{7,5},{8,10},{9,11},{10,... | collective-permute-start | bytes 3145736 | tf_op jit(solution)/shard_map/ppermute | solution.py:16
  468.4 38.7 %collective-permute-start.54 = (bf16[2,128,2048]{2,1,0:T(8,128)(2,1)}, bf16[2,128,2048]{2,1,0:T(8,128)(2,1)}, u32[]{:S(2)}, u32[]{:S(2)}) collective-permute-start(bf16[2,128,2048]{2,1,0:T(8,128)(2,1)} %get-tuple-element.244), channel_id=1, source_target_pairs={{0,4},{1,5},{2,6},{3,7},{4,0},{5,1},{6,2},{7,3},{8,12},{9,13},{10,... | collective-permute-start | bytes 3145736 | tf_op jit(solution)/shard_map/ppermute | solution.py:16
  468.6 38.0 %collective-permute-start.65 = (bf16[176,2048]{1,0:T(8,128)(2,1)}, bf16[176,2048]{1,0:T(8,128)(2,1)}, u32[]{:S(2)}, u32[]{:S(2)}) collective-permute-start(bf16[176,2048]{1,0:T(8,128)(2,1)} %collective-permute-done.52.refs_4_), channel_id=1, source_target_pairs={{0,2},{1,3},{2,0},{3,1},{4,6},{5,7},{6,4},{7,5},{8,10},{9,11},{10,... | collective-permute-start | bytes 2162696 | tf_op jit(solution)/shard_map/ppermute | solution.py:16
  510.1 40.2 %all-to-all-start.3 = ((bf16[8,256,256]{2,1,0:T(8,128)(2,1)}), bf16[8,256,256]{2,1,0:T(8,128)(2,1)}, u32[]{:S(2)}, u32[]{:S(2)}) async-start(bf16[8,256,256]{2,1,0:T(8,128)(2,1)} %get-tuple-element.262), calls=%async_computation.5 | async-start | bytes 2097152 | tf_op jit(solution)/shard_map/all_to_all | solution.py:112
  514.3 127.2 %reduce-scatter.9.cloned.1.call-start = ((), (), s32[]{:S(2)}) async-start(), calls=%async_computation.13 | async-start | bytes 1392640 | tf_op jit(solution)/shard_map/reduce_scatter | solution.py:904
  515.5 34.7 %collective-permute-start.61 = (bf16[128,2048]{1,0:T(8,128)(2,1)}, bf16[128,2048]{1,0:T(8,128)(2,1)}, u32[]{:S(2)}, u32[]{:S(2)}) collective-permute-start(bf16[128,2048]{1,0:T(8,128)(2,1)} %copy-done.56), channel_id=1, source_target_pairs={{0,1},{1,0},{2,3},{3,2},{4,5},{5,4},{6,7},{7,6},{8,9},{9,8},{10,11... | collective-permute-start | bytes 1572872 | tf_op jit(solution)/shard_map/ppermute | solution.py:16
  516.0 24.0 %collective-permute-start.55 = (bf16[128,2048]{1,0:T(8,128)(2,1)}, bf16[128,2048]{1,0:T(8,128)(2,1)S(1)}, u32[]{:S(2)}, u32[]{:S(2)}) collective-permute-start(bf16[128,2048]{1,0:T(8,128)(2,1)} %fusion.18), channel_id=1, source_target_pairs={{0,2},{1,3},{2,0},{3,1},{4,6},{5,7},{6,4},{7,5},{8,10},{9,11},{10,... | collective-permute-start | bytes 1572872 | tf_op jit(solution)/shard_map/ppermute | solution.py:16
  543.5 34.4 %collective-permute-start.68 = (bf16[512,1408]{1,0:T(8,128)(2,1)}, bf16[512,1408]{1,0:T(8,128)(2,1)}, u32[]{:S(2)}, u32[]{:S(2)}) collective-permute-start(bf16[512,1408]{1,0:T(8,128)(2,1)} %reduce-scatter.7.cloned.1.call-done.refs_0_), channel_id=1, source_target_pairs={{0,2},{1,3},{2,0},{3,1},{4,6},{5,7},{6,4},{7,5},{8,10},{9,11},{10,... | collective-permute-start | bytes 4325384 | tf_op jit(solution)/shard_map/ppermute | solution.py:16
  544.9 33.6 %collective-permute-start.69 = (bf16[512,1408]{1,0:T(8,128)(2,1)}, bf16[512,1408]{1,0:T(8,128)(2,1)}, u32[]{:S(2)}, u32[]{:S(2)}) collective-permute-start(bf16[512,1408]{1,0:T(8,128)(2,1)} %reduce-scatter.7.cloned.1.call-done.refs_0_), channel_id=1, source_target_pairs={{0,4},{1,5},{2,6},{3,7},{4,0},{5,1},{6,2},{7,3},{8,12},{9,13},{10,... | collective-permute-start | bytes 4325384 | tf_op jit(solution)/shard_map/ppermute | solution.py:16
  602.2 38.6 %collective-permute-start.57 = (bf16[128,2048]{1,0:T(8,128)(2,1)}, bf16[128,2048]{1,0:T(8,128)(2,1)}, u32[]{:S(2)}, u32[]{:S(2)}) collective-permute-start(bf16[128,2048]{1,0:T(8,128)(2,1)} %fusion.16), channel_id=1, source_target_pairs={{0,2},{1,3},{2,0},{3,1},{4,6},{5,7},{6,4},{7,5},{8,10},{9,11},{10,... | collective-permute-start | bytes 1572872 | tf_op jit(solution)/shard_map/ppermute | solution.py:16
  603.7 37.1 %collective-permute-start.58 = (bf16[128,2048]{1,0:T(8,128)(2,1)}, bf16[128,2048]{1,0:T(8,128)(2,1)}, u32[]{:S(2)}, u32[]{:S(2)}) collective-permute-start(bf16[128,2048]{1,0:T(8,128)(2,1)} %fusion.15), channel_id=1, source_target_pairs={{0,4},{1,5},{2,6},{3,7},{4,0},{5,1},{6,2},{7,3},{8,12},{9,13},{10,... | collective-permute-start | bytes 1572872 | tf_op jit(solution)/shard_map/ppermute | solution.py:16
  605.2 29.7 %collective-permute-start.72 = (bf16[512,768]{1,0:T(8,128)(2,1)}, bf16[512,768]{1,0:T(8,128)(2,1)}, u32[]{:S(2)}, u32[]{:S(2)}) collective-permute-start(bf16[512,768]{1,0:T(8,128)(2,1)} %reduce-scatter.11.cloned.1.call-done.refs_0_), channel_id=1, source_target_pairs={{0,4},{1,5},{2,6},{3,7},{4,0},{5,1},{6,2},{7,3},{8,12},{9,13},{10,... | collective-permute-start | bytes 2359304 | tf_op jit(solution)/shard_map/ppermute | solution.py:16
  605.8 31.7 %collective-permute-start.78 = (bf16[512,768]{1,0:T(8,128)(2,1)}, bf16[512,768]{1,0:T(8,128)(2,1)}, u32[]{:S(2)}, u32[]{:S(2)}) collective-permute-start(bf16[512,768]{1,0:T(8,128)(2,1)} %reduce-scatter.11.cloned.1.call-done.refs_0_), channel_id=1, source_target_pairs={{0,2},{1,3},{2,0},{3,1},{4,6},{5,7},{6,4},{7,5},{8,10},{9,11},{10,... | collective-permute-start | bytes 2359304 | tf_op jit(solution)/shard_map/ppermute | solution.py:16
  640.9 24.6 %collective-permute-start.88 = (bf16[512,768]{1,0:T(8,128)(2,1)}, bf16[512,768]{1,0:T(8,128)(2,1)}, u32[]{:S(2)}, u32[]{:S(2)}) collective-permute-start(bf16[512,768]{1,0:T(8,128)(2,1)} %collective-permute-done.78.refs_2_), channel_id=1, source_target_pairs={{0,1},{1,0},{2,3},{3,2},{4,5},{5,4},{6,7},{7,6},{8,9},{9,8},{10,11... | collective-permute-start | bytes 2359304 | tf_op jit(solution)/shard_map/ppermute | solution.py:16
  641.4 24.1 %collective-permute-start.89 = (bf16[512,768]{1,0:T(8,128)(2,1)}, bf16[512,768]{1,0:T(8,128)(2,1)}, u32[]{:S(2)}, u32[]{:S(2)}) collective-permute-start(bf16[512,768]{1,0:T(8,128)(2,1)} %collective-permute-done.72.refs_4_), channel_id=1, source_target_pairs={{0,1},{1,0},{2,3},{3,2},{4,5},{5,4},{6,7},{7,6},{8,9},{9,8},{10,11... | collective-permute-start | bytes 2359304 | tf_op jit(solution)/shard_map/ppermute | solution.py:16
  (123 other events, 1371.1 us)
Sparse Core Ops, SparseCore 0:
  11.9 85.4 all-gather.5
  99.6 104.9 all-gather.7
  206.1 57.4 all-gather.9
  306.7 54.9 reduce-scatter.4
  366.2 100.7 reduce-scatter.6
  480.6 59.0 reduce-scatter.10
  585.9 25.2 reduce-scatter.8

commit v3 on v2

--- a/solution.py
+++ b/solution.py
@@ -933,6 +933,7 @@
     gproj, glogit, gtaps, ggain = run_mixer_backward(
         place_arr, proj, conv_own, logits, head_weight, gout, saved
     )
+    gbranch_cols = exchange(after(gbranch, gproj))
     gproj, *both = lax.optimization_barrier((gproj, *out_far, *down_state))
     out_far, down_state = both[: len(out_far)], both[len(out_far) :]
     gproj = gproj.reshape(count, rows, 3 * wide)
@@ -942,44 +943,26 @@
     gbeta = jnp.einsum(
         "brh,brd->hd", after(glogit, gnormed_even), normed_all, preferred_element_type=WIDE
     )[:heads]
-    gnormed_twin, gbeta, *gwdown_first = lax.optimization_barrier((gnormed_twin, gbeta, *gwdown_first))
-    gwdown_far = gather_far(gwdown_first)
-    gwdown_parts = gather_rest(gwdown_first, gwdown_far)
+    gnormed_twin, gbeta, gbranch_cols, *gwdown_first = lax.optimization_barrier(
+        (gnormed_twin, gbeta, gbranch_cols, *gwdown_first)
+    )
     gnormed_state = reduce_add(gnormed_even, gnormed_twin)
-    gproj, *gnormed_state = lax.optimization_barrier((gproj, *gnormed_state))
-    gproj, gwgu = lax.optimization_barrier((gproj, gwgu))
+    gproj, gnormed_odd = lax.optimization_barrier((gproj, gnormed_odd))
     gwin = jnp.einsum("brd,bre->de", normed_all, gproj, preferred_element_type=WIDE).astype(LOW)
     gnormed_state = reduce_far(gnormed_state)
-    lanes = min(256, width)
-    gwdown = run_spread(
-        place_arr,
-        gwdown_parts,
-        (piece, lanes),
-        width // lanes,
-        lambda i: [(0, lanes, (slice(i * piece, (i + 1) * piece), slice(None)))],
-        (hidden_part, width),
-        (hidden_part, lanes),
-        lambda g: (0, g),
-        "spread_down",
-    )
-    gnormed_state[0], gwin = lax.optimization_barrier((gnormed_state[0], gwin))
     gwin = to_owner(gwin)
     gnormed_state = reduce_more(gnormed_state)
     gnormed = reduce_last(gnormed_state)
     down_state[0] = after(down_state[0], *gnormed_state)
     down_state = reduce_more(down_state)
-    gbranch_cols = exchange(after(gbranch, *gnormed_state[2:4]))
-    gwgu_first = gather_start(after(gwgu, *gnormed_state[2:]), True)
+    gwgu_first = gather_start(after(gwgu, *[e[-1] for e in gnormed]), True)
     gnormed = total_of(gnormed)
     input_grad = ghidden + norm_back(inputs, first_scale, gnormed, first_weight)
     gfirst = jnp.sum(gnormed * inputs * first_scale, axis=0)
-    down_state[0], gfirst = lax.optimization_barrier((down_state[0], gfirst))
-    down = reduce_last(down_state)
-    output = (hidden + total_of(down)).astype(LOW)
 
 
     out_all_parts = gather_rest(out_first, out_far)
-    gwout = run_outer(place_arr, out_all_parts, gbranch_cols, "output_weights")
+    gwout = run_outer(place_arr, out_all_parts, after(gbranch_cols, *gnormed_state), "output_weights")
     gtaps = jnp.sum(gtaps, axis=0).transpose(1, 2, 0, 3).reshape(3 * taps, wide)
     ggain = jnp.sum(ggain, axis=(0, 1)).reshape(shards, 1, dim // shards)
     ggain = jnp.pad(ggain, ((0, 0), (0, 0), (0, wide - dim // shards)))
@@ -1001,13 +984,13 @@
     more = extra.shape[1]
     gwout = jnp.concatenate([gwout.reshape(shards, part, wide), extra], axis=1)
     gwout = gwout.reshape(shards * (part + more), wide)
-    gwgu_first[0], gwout, gwdown = lax.optimization_barrier((gwgu_first[0], gwout, gwdown))
-    gwgu_far = gather_far([after(x, gwgu_first[0]) for x in gwgu_first])
+    gwgu_first, gwout = lax.optimization_barrier((gwgu_first, gwout))
+    gwgu_far = gather_far(gwgu_first)
     gwout = to_owner(gwout)
 
     gwgu_parts = gather_rest(gwgu_first, gwgu_far)
     tall = min(128, part)
-    gwin_first = gather_start(after(gwin, *gwgu_far))
+    gwin_first = gather_start(after(gwin, *gwgu_first))
     gwgu = run_spread(
         place_arr,
         gwgu_parts,
@@ -1028,8 +1011,25 @@
         "spread_gate_up",
     )
     gwin_far = gather_far([after(g, gwgu) for g in gwin_first])
+    down_state, gwdown_first, gwin_far = lax.optimization_barrier((down_state, gwdown_first, gwin_far))
+    gwdown_far = gather_far(gwdown_first)
+    down = reduce_last(down_state)
+    output = (hidden + total_of(down)).astype(LOW)
+    gwdown_parts = gather_rest(gwdown_first, gwdown_far)
+    lanes = min(256, width)
+    gwdown = run_spread(
+        place_arr,
+        gwdown_parts,
+        (piece, lanes),
+        width // lanes,
+        lambda i: [(0, lanes, (slice(i * piece, (i + 1) * piece), slice(None)))],
+        (hidden_part, width),
+        (hidden_part, lanes),
+        lambda g: (0, g),
+        "spread_down",
+    )
     gwin_parts = gather_rest(gwin_first, gwin_far)
-    gwout_first = gather_start(after(gwout, *gwin_far))
+    gwout_first = gather_start(after(gwout, *gwin_first))
     gwout_parts = gather_rest(gwout_first, gather_far(gwout_first, False))
     gwin = run_spread(
         place_arr,

time: 701 us -> 693 us (0.989)
  starting transfers between devices: 78.4 us -> 70.8 us
    ppermute x92, starting transfers between devices: 61.5 us -> 54 us  [swap(): return lax.ppermute(x, 'seq', [(i, i ^ bits) for i in range(count)])]
    convert_element_type x12 -> x9, other arithmetic: 24.3 us -> 23.9 us  [add(): return (first.astype(WIDE) + second.astype(WIDE)).astype(LOW)]
  transfers between devices with their start and end apart: 103 -> 103, of which waited for: 35 -> 42; matrix products, arithmetic and copies ran while one was open for 16% -> 17% of each run, Pallas kernels for 25% -> 24%
where the time goes in v3:
time: 693 us; the launch traced here: 683 us
  waiting for transfers between devices  245 us (35%)
  Pallas kernels  208 us (30%)
  starting transfers between devices  70.8 us (10%)
  other arithmetic  43.1 us (6%)
  matrix products  43.1 us (6%)
  local copies, waits for them, and re-layouts  42.3 us (6%)
  between operations  15.9 us (2%)
  blocking collectives  14.9 us (2%)
    ppermute x92, waiting for transfers between devices, swap(): return lax.ppermute(x, 'seq', [(i, i ^ bits) for i in range(count)])  214 us
    ppermute x92, starting transfers between devices, swap(): return lax.ppermute(x, 'seq', [(i, i ^ bits) for i in range(count)])  54 us
    pallas_call x4, Pallas kernels, run_spread(): pl.pallas_call(functools.partial(spread_kernel, heights(entries), layout)...  35.8 us
    pallas_call x1, Pallas kernels, run_gate_back(): pl.pallas_call(gate_back_kernel, grid=(count // 2,), in_specs=[block(widt...  32.1 us
    pallas_call x1, Pallas kernels, run_mixer_backward(): pl.pallas_call(mixer_backward, out_shape=shapes, grid_spec=pltpu.Prefetch...  26.5 us
    pallas_call x1, Pallas kernels, run_gate(): pl.pallas_call(functools.partial(gate_kernel, sizes, heights(others)), gr...  25.6 us
    convert_element_type x9, other arithmetic, add(): return (first.astype(WIDE) + second.astype(WIDE)).astype(LOW)  23.9 us
    pallas_call x2, Pallas kernels, run_pairs(): pl.pallas_call(functools.partial(pairs_kernel, len(terms), [t[2] for t in...  23.5 us
  transfers between devices with their start and end apart: 103, of which 42 were waited for; matrix products, arithmetic and copies ran while one was open for 17% of the time, Pallas kernels for 24%

profile of v3, /device:TPU:0, one launch (start us, length us, event | category | flops | bytes accessed | tf_op | source)
XLA Modules:
  0.0 683.3 jit_solution(8675649893353389655)
XLA Ops:
  23.1 14.9 %all-gather.1 = bf16[4,31,512]{2,1,0:T(8,128)(2,1)S(1)} all-gather(bf16[1,31,512]{2,1,0:T(8,128)(2,1)S(1)} %bitcast.186), channel_id=2, replica_groups=mesh['fsdp'=4,'seq'=8] {'fsdp'}, dimensions={0}, use_global_device_ids=true | all-gather | bytes 158720 | tf_op jit(solution)/shard_map/all_gather | solution.py:845
  42.8 22.2 %collective-permute-done.3.refs_4_ = bf16[256,2048]{1,0:T(8,128)(2,1)} collective-permute-done((bf16[256,2048]{1,0:T(8,128)(2,1)S(1)}, bf16[256,2048]{1,0:T(8,128)(2,1)}, u32[]{:S(2)}, u32[]{:S(2)}) %collective-permute-start.3) | collective-permute-done | bytes 1048608 | tf_op jit(solution)/shard_map/ppermute | solution.py:16
  69.4 9.0 %collective-permute-done.4.refs_6_ = bf16[128,2048]{1,0:T(8,128)(2,1)S(1)} collective-permute-done((bf16[128,2048]{1,0:T(8,128)(2,1)S(1)}, bf16[128,2048]{1,0:T(8,128)(2,1)S(1)}, u32[]{:S(2)}, u32[]{:S(2)}) %collective-permute-start.4) | collective-permute-done | bytes 524320 | tf_op jit(solution)/shard_map/ppermute | solution.py:16
  85.8 7.4 %collective-permute-done.7.refs_16_ = bf16[128,2048]{1,0:T(8,128)(2,1)S(1)} collective-permute-done((bf16[128,2048]{1,0:T(8,128)(2,1)S(1)}, bf16[128,2048]{1,0:T(8,128)(2,1)S(1)}, u32[]{:S(2)}, u32[]{:S(2)}) %collective-permute-start.7) | collective-permute-done | bytes 524320 | tf_op jit(solution)/shard_map/ppermute | solution.py:16
  102.3 14.6 %project.1 = (bf16[8,256,768]{2,1,0:T(8,128)(2,1)}, f32[8,256,128]{2,1,0:T(8,128)}, bf16[8,256,2048]{2,1,0:T(8,128)(2,1)}) custom-call(bf16[256,2048]{1,0:T(8,128)(2,1)} %copy-done.15, bf16[256,2048]{1,0:T(8,128)(2,1)} %collective-permute-done.18.refs_1_, bf16[256,2048]{1,0:T(8,128)(2,1)} %collective-permute-done.5.refs_2_, ...), custom_call_target="tpu_custom_call" | custom-call | flops 18400000000 | bytes 56000000 | tf_op jit(solution)/shard_map/project/pallas_call | solution.py:456
  117.0 8.7 %collective-permute-done.12.refs_4_ = bf16[2048,256]{1,0:T(8,128)(2,1)S(1)} collective-permute-done((bf16[2048,256]{1,0:T(8,128)(2,1)S(1)}, bf16[2048,256]{1,0:T(8,128)(2,1)S(1)}, u32[]{:S(2)}, u32[]{:S(2)}) %collective-permute-start.12) | collective-permute-done | bytes 1048608 | tf_op jit(solution)/shard_map/ppermute | solution.py:16
  128.9 10.9 %mixer_forward.2 = (bf16[8,128,256]{2,1,0:T(8,128)(2,1)}, f32[2,2,8,128,128]{4,3,2,1,0:T(8,128)}, bf16[2,2,8,128,128]{4,3,2,1,0:T(8,128)(2,1)}, bf16[2,2,8,128,1...) custom-call(s32[1]{0:T(128)} %bitcast.place_ref, ...), custom_call_target="tpu_custom_call" | custom-call | flops 11500000256 | bytes 35000000 | tf_op jit(solution)/shard_map/mixer_forward/pallas_call | solution.py:332
  139.8 3.7 all-to-all-start
  144.6 10.9 %mixer_forward.3 = (bf16[8,128,256]{2,1,0:T(8,128)(2,1)}, f32[2,2,8,128,128]{4,3,2,1,0:T(8,128)}, bf16[2,2,8,128,128]{4,3,2,1,0:T(8,128)(2,1)}, bf16[2,2,8,128,1...) custom-call(s32[1]{0:T(128)} %bitcast.place_ref, ...), custom_call_target="tpu_custom_call", output_to_operand_aliasing={{1}: (5, {}), {2}: (6, {}), {3}: (7, {}), {4}: (8, {}), {5}... | custom-call | flops 11500000256 | bytes 35000000 | tf_op jit(solution)/shard_map/mixer_forward/pallas_call | solution.py:332
  155.5 4.2 all-to-all-start.1
  160.3 9.1 %all-to-all-done.1.refs_11_ = bf16[8,128,256]{2,1,0:T(8,128)(2,1)S(1)} async-done(((bf16[8,128,256]{2,1,0:T(8,128)(2,1)}), bf16[8,128,256]{2,1,0:T(8,128)(2,1)S(1)}, u32[]{:S(2)}, u32[]{:S(2)}) %all-to-all-start.1) | async-done | bytes 524320 | tf_op jit(solution)/shard_map/all_to_all | solution.py:112
  170.8 10.6 %branch.1 = (f32[256,2048]{1,0:T(8,128)}, bf16[256,2048]{1,0:T(8,128)(2,1)}, bf16[256,2048]{1,0:T(8,128)(2,1)}) custom-call(s32[1]{0:T(128)} %bitcast.place_ref, bf16[2048,256]{1,0:T(8,128)(2,1)} %copy-done.10, bf16[2048,256]{1,0:T(8,128)(2,1)} %collective-permute-done.9.refs_1_, bf16[2048,256]{1,0:T(8,128)(2,1)} %collective-permute-done.10.refs_2_, ...), custom_call_target="tpu_custom_call" | custom-call | flops 11500000256 | bytes 35000000 | tf_op jit(solution)/shard_map/branch/pallas_call | solution.py:632
  183.5 21.2 %collective-permute-done.26.refs_4_ = bf16[256,2048]{1,0:T(8,128)(2,1)S(1)} collective-permute-done((bf16[256,2048]{1,0:T(8,128)(2,1)}, bf16[256,2048]{1,0:T(8,128)(2,1)S(1)}, u32[]{:S(2)}, u32[]{:S(2)}) %collective-permute-start.26) | collective-permute-done | bytes 1048608 | tf_op jit(solution)/shard_map/ppermute | solution.py:16
  209.9 11.1 %collective-permute-done.28.refs_6_ = bf16[128,2048]{1,0:T(8,128)(2,1)} collective-permute-done((bf16[128,2048]{1,0:T(8,128)(2,1)S(1)}, bf16[128,2048]{1,0:T(8,128)(2,1)}, u32[]{:S(2)}, u32[]{:S(2)}) %collective-permute-start.28) | collective-permute-done | bytes 524320 | tf_op jit(solution)/shard_map/ppermute | solution.py:16
  226.6 25.6 %gate.1 = (bf16[8,256,704]{2,1,0:T(8,128)(2,1)}, bf16[8,256,704]{2,1,0:T(8,128)(2,1)}, bf16[8,256,704]{2,1,0:T(8,128)(2,1)}, bf16[8,256,2048]{2,1,0:T(8,128)(2,1)}, bf16[8,256,2048]{2,1,0:T(8,128)(2,1)}) custom-call(bf16[256,2048]{1,0:T(8,128)(2,1)} %get-tuple-element.169.refs_0_, bf16[256,2048]{1,0:T(8,128)(2,1)} %copy-done.49, ...), custom_call_target="tpu_custom_call" | custom-call | flops 28750000128 | bytes 87500000 | tf_op jit(solution)/shard_map/gate/pallas_call | solution.py:513
  252.3 11.4 %all-gather.10.cloned.1.call-done.down_ref.refs_1_ = bf16[704,2048]{1,0:T(8,128)(2,1)} async-done(((bf16[176,2048]{1,0:T(8,128)(2,1)}), bf16[704,2048]{1,0:T(8,128)(2,1)}) %all-gather.10.cloned.1.call-update) | async-done | bytes 2883600 | tf_op jit(solution)/shard_map/all_gather | solution.py:834
  263.7 32.1 %gate_back.1 = (bf16[8,256,1408]{2,1,0:T(8,128)(2,1)}, bf16[4,256,2048]{2,1,0:T(8,128)(2,1)}, bf16[4,256,2048]{2,1,0:T(8,128)(2,1)}) custom-call(bf16[8,256,2048]{2,1,0:T(8,128)(2,1)} %get-tuple-element.170.cot_ref, bf16[8,256,704]{2,1,0:T(8,128)(2,1)} %get-tuple-element.174.up_ref, bf16[8,256,704]{2,1,0:T(8,128)(2,1)} %get-tuple-element.175.gate_ref, ...), custom_call_target="tpu_custom_call" | custom-call | flops 36800000000 | bytes 112000000 | tf_op jit(solution)/shard_map/gate_back/pallas_call | solution.py:557
  295.7 10.7 %bitcast_convert_fusion.2 = bf16[704,2048]{1,0:T(8,128)(2,1)} fusion(bf16[8,256,704]{2,1,0:T(8,128)(2,1)} %get-tuple-element.198.refs_0_, bf16[8,256,2048]{2,1,0:T(8,128)(2,1)} %get-tuple-element.170.cot_ref), kind=kOutput, calls=%fused_computation.2 | convolution fusion | flops 5907021824 | bytes 14155776 | tf_op jit(solution)/shard_map/brf,brd->fd/dot_general | solution.py:910
  315.4 17.1 %bitcast_convert_fusion = bf16[2048,1408]{1,0:T(8,128)(2,1)} fusion(bf16[8,256,2048]{2,1,0:T(8,128)(2,1)S(1)} %copy-done.68, bf16[8,256,1408]{2,1,0:T(8,128)(2,1)} %get-tuple-element.184), kind=kOutput, calls=%fused_computation | convolution fusion | flops 11814043648 | bytes 19922944 | tf_op jit(solution)/shard_map/brd,brf->df/dot_general | solution.py:916
  332.6 5.9 collective-permute-done.40.refs_12_
  344.0 10.6 %down.1 = (bf16[4,256,2048]{2,1,0:T(8,128)(2,1)}, bf16[4,256,2048]{2,1,0:T(8,128)(2,1)}) custom-call(bf16[8,256,704]{2,1,0:T(8,128)(2,1)} %get-tuple-element.198.refs_0_, bf16[704,2048]{1,0:T(8,128)(2,1)} %all-gather.10.cloned.1.call-done.down_ref.refs_1_), custom_call_target="tpu_custom_call" | custom-call | flops 13799999488 | bytes 42000000 | tf_op jit(solution)/shard_map/down/pallas_call | solution.py:588
  356.6 9.8 %branch_back.1 = (f32[256,2048]{1,0:T(8,128)}, f32[1,2048]{1,0:T(1,128)}, bf16[8,256,256]{2,1,0:T(8,128)(2,1)}, bf16[8,256,256]{2,1,0:T(8,128)(2,1)}) custom-call(s32[1]{0:T(128)} %bitcast.place_ref, bf16[2048,256]{1,0:T(8,128)(2,1)} %copy-done.10, bf16[2048,256]{1,0:T(8,128)(2,1)} %collective-permute-done.9.refs_1_, ...), custom_call_target="tpu_custom_call" | custom-call | flops 11500000256 | bytes 35000000 | tf_op jit(solution)/shard_map/branch_back/pallas_call | solution.py:704
  366.5 3.8 all-to-all-start.2
  370.3 3.7 collective-permute-done.44
  376.8 4.0 add_convert_fusion.2
  380.8 4.8 all-to-all-done.2.gout_ref
  392.4 26.5 %mixer_backward.1 = (bf16[8,2,128,768]{3,2,1,0:T(8,128)(2,1)}, bf16[8,2,128,128]{3,2,1,0:T(8,128)(2,1)}, f32[2,2,3,4,128]{4,3,2,1,0:T(4,128)}, f32[2,2,1,128]{3,2,1,0:T(1,128)}) custom-call(s32[1]{0:T(128)} %bitcast.place_ref, bf16[8,2,128,768]{3,2,1,0:T(8,128)(2,1)} %bitcast.204, f32[2,3,4,128]{3,2,1,0:T(4,128)} %copy_bitcast_fusion.taps_ref, ...), custom_call_target="tpu_custom_call" | custom-call | flops 29899999232 | bytes 91000000 | tf_op jit(solution)/shard_map/mixer_backward/pallas_call | solution.py:364
  426.1 13.0 %input_back.1 = (bf16[4,256,2048]{2,1,0:T(8,128)(2,1)}, bf16[4,256,2048]{2,1,0:T(8,128)(2,1)}) custom-call(bf16[8,256,768]{2,1,0:T(8,128)(2,1)} %bitcast.179, bf16[8,256,128]{2,1,0:T(8,128)(2,1)} %bitcast.181, bf16[2048,1024]{1,0:T(8,128)(2,1)} %all-gather.6.cloned.1.call-done.refs_10_.refs_2_, bf16[128,2048]{1,0:T(8,128)(2,1)} %pad.19.refs_11_.refs_3_), custom_call_target="tpu_custom_call" | custom-call | flops 1150000000 | bytes 3500000 | tf_op jit(solution)/shard_map/input_back/pallas_call | solution.py:588
  440.4 4.0 all-to-all-start.3
  447.7 11.1 %collective-permute-done.51.refs_2_ = bf16[176,2048]{1,0:T(8,128)(2,1)} collective-permute-done((bf16[176,2048]{1,0:T(8,128)(2,1)S(1)}, bf16[176,2048]{1,0:T(8,128)(2,1)}, u32[]{:S(2)}, u32[]{:S(2)}) %collective-permute-start.51) | collective-permute-done | bytes 720928 | tf_op jit(solution)/shard_map/ppermute | solution.py:16
  459.2 4.7 convolution_bitcast_fusion
  464.0 5.2 all-to-all-done.3.cols_ref
  469.2 4.4 add_convert_fusion
  475.8 10.5 %bitcast_convert_fusion.1 = bf16[2048,768]{1,0:T(8,128)(2,1)} fusion(bf16[8,256,2048]{2,1,0:T(8,128)(2,1)} %get-tuple-element.231, bf16[8,256,768]{2,1,0:T(8,128)(2,1)S(1)} %bitcast.180), kind=kOutput, calls=%fused_computation.1 | convolution fusion | flops 6444023808 | bytes 14680064 | tf_op jit(solution)/shard_map/brd,bre->de/dot_general | solution.py:951
  490.7 7.0 %collective-permute-done.53 = bf16[2,128,2048]{2,1,0:T(8,128)(2,1)S(1)} collective-permute-done((bf16[2,128,2048]{2,1,0:T(8,128)(2,1)}, bf16[2,128,2048]{2,1,0:T(8,128)(2,1)S(1)}, u32[]{:S(2)}, u32[]{:S(2)}) %collective-permute-start.53) | collective-permute-done | bytes 1048608 | tf_op jit(solution)/shard_map/ppermute | solution.py:16
  503.3 7.7 %output_weights.1 = bf16[2048,256]{1,0:T(8,128)(2,1)} custom-call(s32[1]{0:T(128)} %bitcast.place_ref, bf16[8,256,256]{2,1,0:T(8,128)(2,1)} %copy-done.11, bf16[256,2048]{1,0:T(8,128)(2,1)} %get-tuple-element.173.refs_0_, bf16[256,2048]{1,0:T(8,128)(2,1)} %copy-done.47, bf16[256,2048]{1,0:T(8,128)(2,1)} %collective-permute-done.37.refs_2_, ...), custom_call_target="tpu_custom_call" | custom-call | flops 9200000000 | bytes 28000000 | tf_op jit(solution)/shard_map/output_weights/pallas_call | solution.py:751
  521.7 4.8 fusion.9
  528.9 22.2 %collective-permute-done.58.refs_2_ = bf16[512,1408]{1,0:T(8,128)(2,1)} collective-permute-done((bf16[512,1408]{1,0:T(8,128)(2,1)}, bf16[512,1408]{1,0:T(8,128)(2,1)}, u32[]{:S(2)}, u32[]{:S(2)}) %collective-permute-start.58) | collective-permute-done | bytes 1441824 | tf_op jit(solution)/shard_map/ppermute | solution.py:16
  556.3 14.9 %collective-permute-done.67.refs_6_ = bf16[256,1408]{1,0:T(8,128)(2,1)} collective-permute-done((bf16[256,1408]{1,0:T(8,128)(2,1)S(1)}, bf16[256,1408]{1,0:T(8,128)(2,1)}, u32[]{:S(2)}, u32[]{:S(2)}) %collective-permute-start.67) | collective-permute-done | bytes 720928 | tf_op jit(solution)/shard_map/ppermute | solution.py:16
  576.3 14.0 %spread_gate_up.1 = f32[2,512,5632]{2,1,0:T(8,128)} custom-call(s32[1]{0:T(128)} %bitcast.place_ref, bf16[512,1408]{1,0:T(8,128)(2,1)} %reduce-scatter.9.cloned.1.call-done.refs_0_, bf16[512,1408]{1,0:T(8,128)(2,1)} %collective-permute-done.57.refs_1_, bf16[512,1408]{1,0:T(8,128)(2,1)} %collective-permute-done.58.refs_2_, ...), custom_call_target="tpu_custom_call" | custom-call | flops 11500000256 | bytes 35000000 | tf_op jit(solution)/shard_map/spread_gate_up/pallas_call | solution.py:788
  590.2 3.8 collective-permute-done.64.refs_4_
  599.4 6.5 collective-permute-done.71.refs_6_
  612.5 8.4 %spread_inputs.1 = f32[3,512,2048]{2,1,0:T(8,128)} custom-call(s32[1]{0:T(128)} %bitcast.place_ref, bf16[512,768]{1,0:T(8,128)(2,1)} %reduce-scatter.7.cloned.1.call-done.refs_0_, bf16[512,768]{1,0:T(8,128)(2,1)} %copy-done.53, bf16[512,768]{1,0:T(8,128)(2,1)} %collective-permute-done.72.refs_2_, bf16[512,768]{1,0:T(8,128)(2,1)} %collective-permute-done.84.refs_3_, ...), custom_call_target="tpu_custom_call" | custom-call | flops 11500000256 | bytes 35000000 | tf_op jit(solution)/shard_map/spread_inputs/pallas_call | solution.py:788
  620.9 18.9 %collective-permute-done.74 = bf16[128,2048]{1,0:T(8,128)(2,1)S(1)} collective-permute-done((bf16[128,2048]{1,0:T(8,128)(2,1)S(1)}, bf16[128,2048]{1,0:T(8,128)(2,1)S(1)}, u32[]{:S(2)}, u32[]{:S(2)}) %collective-permute-start.74) | collective-permute-done | bytes 524320 | tf_op jit(solution)/shard_map/ppermute | solution.py:16
  641.9 4.1 fusion.12
  650.4 6.7 collective-permute-done.82.refs_6_
  662.5 4.3 spread_output.1
  666.9 9.1 %spread_down.1 = f32[1408,2048]{1,0:T(8,128)} custom-call(s32[1]{0:T(128)} %bitcast.place_ref, bf16[176,2048]{1,0:T(8,128)(2,1)} %reduce-scatter.5.cloned.1.call-done.refs_0_, bf16[176,2048]{1,0:T(8,128)(2,1)} %collective-permute-done.50.refs_1_, bf16[176,2048]{1,0:T(8,128)(2,1)} %collective-permute-done.51.refs_2_, ...), custom_call_target="tpu_custom_call" | custom-call | flops 11500000256 | bytes 35000000 | tf_op jit(solution)/shard_map/spread_down/pallas_call | solution.py:788
  (436 shorter events, 157.8 us)
Async XLA Ops:
  7.2 90.2 %all-gather.6.cloned.1.call-start = ((), (), s32[]{:S(2)}) async-start(), calls=%async_computation.8 | async-start | bytes 5242880 | tf_op jit(solution)/shard_map/all_gather | solution.py:834
  11.8 214.7 %all-gather.8.cloned.1.call-start = ((), (), s32[]{:S(2)}) async-start(), calls=%async_computation.9 | async-start | bytes 7208960 | tf_op jit(solution)/shard_map/all_gather | solution.py:834
  11.9 28.5 %collective-permute-start = (bf16[256,2048]{1,0:T(8,128)(2,1)}, bf16[256,2048]{1,0:T(8,128)(2,1)}, u32[]{:S(2)}, u32[]{:S(2)}) collective-permute-start(bf16[256,2048]{1,0:T(8,128)(2,1)} %bitcast.18.refs_10_.refs_17_), channel_id=1, source_target_pairs={{0,1},{1,0},{2,3},{3,2},{4,5},{5,4},{6,7},{7,6},{8,9},{9,8},{10,11... | collective-permute-start | bytes 3145736 | tf_op jit(solution)/shard_map/ppermute | solution.py:16
  12.4 28.0 %collective-permute-start.1 = (bf16[256,2048]{1,0:T(8,128)(2,1)}, bf16[256,2048]{1,0:T(8,128)(2,1)}, u32[]{:S(2)}, u32[]{:S(2)}) collective-permute-start(bf16[256,2048]{1,0:T(8,128)(2,1)} %bitcast.18.refs_10_.refs_17_), channel_id=1, source_target_pairs={{0,2},{1,3},{2,0},{3,1},{4,6},{5,7},{6,4},{7,5},{8,10},{9,11},{10,... | collective-permute-start | bytes 3145736 | tf_op jit(solution)/shard_map/ppermute | solution.py:16
  14.9 25.5 %collective-permute-start.2 = (bf16[256,2048]{1,0:T(8,128)(2,1)}, bf16[256,2048]{1,0:T(8,128)(2,1)}, u32[]{:S(2)}, u32[]{:S(2)}) collective-permute-start(bf16[256,2048]{1,0:T(8,128)(2,1)} %bitcast.18.refs_10_.refs_17_), channel_id=1, source_target_pairs={{0,4},{1,5},{2,6},{3,7},{4,0},{5,1},{6,2},{7,3},{8,12},{9,13},{10,... | collective-permute-start | bytes 3145736 | tf_op jit(solution)/shard_map/ppermute | solution.py:16
  40.5 24.5 %collective-permute-start.3 = (bf16[256,2048]{1,0:T(8,128)(2,1)S(1)}, bf16[256,2048]{1,0:T(8,128)(2,1)}, u32[]{:S(2)}, u32[]{:S(2)}) collective-permute-start(bf16[256,2048]{1,0:T(8,128)(2,1)S(1)} %fusion.4.refs_0_), channel_id=1, source_target_pairs={{0,4},{1,5},{2,6},{3,7},{4,0},{5,1},{6,2},{7,3},{8,12},{9,13},{10,... | collective-permute-start | bytes 3145736 | tf_op jit(solution)/shard_map/ppermute | solution.py:16
  42.0 25.4 %collective-permute-start.5 = (bf16[256,2048]{1,0:T(8,128)(2,1)S(1)}, bf16[256,2048]{1,0:T(8,128)(2,1)}, u32[]{:S(2)}, u32[]{:S(2)}) collective-permute-start(bf16[256,2048]{1,0:T(8,128)(2,1)S(1)} %fusion.4.refs_0_), channel_id=1, source_target_pairs={{0,2},{1,3},{2,0},{3,1},{4,6},{5,7},{6,4},{7,5},{8,10},{9,11},{10,... | collective-permute-start | bytes 3145736 | tf_op jit(solution)/shard_map/ppermute | solution.py:16
  98.8 44.7 %collective-permute-start.9 = (bf16[2048,256]{1,0:T(8,128)(2,1)S(1)}, bf16[2048,256]{1,0:T(8,128)(2,1)}, u32[]{:S(2)}, u32[]{:S(2)}) collective-permute-start(bf16[2048,256]{1,0:T(8,128)(2,1)S(1)} %slice.292.refs_0_), channel_id=1, source_target_pairs={{0,1},{1,0},{2,3},{3,2},{4,5},{5,4},{6,7},{7,6},{8,9},{9,8},{10,11... | collective-permute-start | bytes 3145736 | tf_op jit(solution)/shard_map/ppermute | solution.py:16
  98.9 27.8 %collective-permute-start.10 = (bf16[2048,256]{1,0:T(8,128)(2,1)S(1)}, bf16[2048,256]{1,0:T(8,128)(2,1)}, u32[]{:S(2)}, u32[]{:S(2)}) collective-permute-start(bf16[2048,256]{1,0:T(8,128)(2,1)S(1)} %slice.292.refs_0_), channel_id=1, source_target_pairs={{0,2},{1,3},{2,0},{3,1},{4,6},{5,7},{6,4},{7,5},{8,10},{9,11},{10,... | collective-permute-start | bytes 3145736 | tf_op jit(solution)/shard_map/ppermute | solution.py:16
  100.4 25.2 %collective-permute-start.12 = (bf16[2048,256]{1,0:T(8,128)(2,1)S(1)}, bf16[2048,256]{1,0:T(8,128)(2,1)S(1)}, u32[]{:S(2)}, u32[]{:S(2)}) collective-permute-start(bf16[2048,256]{1,0:T(8,128)(2,1)S(1)} %slice.292.refs_0_), channel_id=1, source_target_pairs={{0,4},{1,5},{2,6},{3,7},{4,0},{5,1},{6,2},{7,3},{8,12},{9,13},{10,... | collective-permute-start | bytes 3145736 | tf_op jit(solution)/shard_map/ppermute | solution.py:16
  143.5 25.9 %collective-permute-start.11 = (bf16[2048,256]{1,0:T(8,128)(2,1)}, bf16[2048,256]{1,0:T(8,128)(2,1)S(1)}, u32[]{:S(2)}, u32[]{:S(2)}) collective-permute-start(bf16[2048,256]{1,0:T(8,128)(2,1)} %collective-permute-done.10.refs_2_), channel_id=1, source_target_pairs={{0,1},{1,0},{2,3},{3,2},{4,5},{5,4},{6,7},{7,6},{8,9},{9,8},{10,11... | collective-permute-start | bytes 3145736 | tf_op jit(solution)/shard_map/ppermute | solution.py:16
  144.0 25.4 %collective-permute-start.13 = (bf16[2048,256]{1,0:T(8,128)(2,1)}, bf16[2048,256]{1,0:T(8,128)(2,1)}, u32[]{:S(2)}, u32[]{:S(2)}) collective-permute-start(bf16[2048,256]{1,0:T(8,128)(2,1)} %copy-done.21), channel_id=1, source_target_pairs={{0,1},{1,0},{2,3},{3,2},{4,5},{5,4},{6,7},{7,6},{8,9},{9,8},{10,11... | collective-permute-start | bytes 3145736 | tf_op jit(solution)/shard_map/ppermute | solution.py:16
  144.1 25.4 %collective-permute-start.16 = (bf16[1024,256]{1,0:T(8,128)(2,1)S(1)}, bf16[1024,256]{1,0:T(8,128)(2,1)}, u32[]{:S(2)}, u32[]{:S(2)}) collective-permute-start(bf16[1024,256]{1,0:T(8,128)(2,1)S(1)} %collective-permute-done.14.refs_6_), channel_id=1, source_target_pairs={{0,1},{1,0},{2,3},{3,2},{4,5},{5,4},{6,7},{7,6},{8,9},{9,8},{10,11... | collective-permute-start | bytes 1572872 | tf_op jit(solution)/shard_map/ppermute | solution.py:16
  144.5 24.9 %collective-permute-start.17 = (bf16[1024,256]{1,0:T(8,128)(2,1)}, bf16[1024,256]{1,0:T(8,128)(2,1)S(1)}, u32[]{:S(2)}, u32[]{:S(2)}) collective-permute-start(bf16[1024,256]{1,0:T(8,128)(2,1)} %collective-permute-done.15.refs_7_), channel_id=1, source_target_pairs={{0,1},{1,0},{2,3},{3,2},{4,5},{5,4},{6,7},{7,6},{8,9},{9,8},{10,11... | collective-permute-start | bytes 1572872 | tf_op jit(solution)/shard_map/ppermute | solution.py:16
  159.7 104.0 %all-gather.10.cloned.1.call-start = ((), (), s32[]{:S(2)}) async-start(), calls=%async_computation.10 | async-start | bytes 3604480 | tf_op jit(solution)/shard_map/all_gather | solution.py:834
  181.4 23.2 %collective-permute-start.26 = (bf16[256,2048]{1,0:T(8,128)(2,1)}, bf16[256,2048]{1,0:T(8,128)(2,1)S(1)}, u32[]{:S(2)}, u32[]{:S(2)}) collective-permute-start(bf16[256,2048]{1,0:T(8,128)(2,1)} %get-tuple-element.169.refs_0_), channel_id=1, source_target_pairs={{0,4},{1,5},{2,6},{3,7},{4,0},{5,1},{6,2},{7,3},{8,12},{9,13},{10,... | collective-permute-start | bytes 3145736 | tf_op jit(solution)/shard_map/ppermute | solution.py:16
  182.0 23.8 %collective-permute-start.24 = (bf16[256,2048]{1,0:T(8,128)(2,1)}, bf16[256,2048]{1,0:T(8,128)(2,1)S(1)}, u32[]{:S(2)}, u32[]{:S(2)}) collective-permute-start(bf16[256,2048]{1,0:T(8,128)(2,1)} %get-tuple-element.169.refs_0_), channel_id=1, source_target_pairs={{0,2},{1,3},{2,0},{3,1},{4,6},{5,7},{6,4},{7,5},{8,10},{9,11},{10,... | collective-permute-start | bytes 3145736 | tf_op jit(solution)/shard_map/ppermute | solution.py:16
  182.6 23.3 %collective-permute-start.32 = (bf16[256,2048]{1,0:T(8,128)(2,1)}, bf16[256,2048]{1,0:T(8,128)(2,1)}, u32[]{:S(2)}, u32[]{:S(2)}) collective-permute-start(bf16[256,2048]{1,0:T(8,128)(2,1)} %collective-permute-done.1.refs_12_), channel_id=1, source_target_pairs={{0,1},{1,0},{2,3},{3,2},{4,5},{5,4},{6,7},{7,6},{8,9},{9,8},{10,11... | collective-permute-start | bytes 3145736 | tf_op jit(solution)/shard_map/ppermute | solution.py:16
  182.6 23.9 %collective-permute-start.33 = (bf16[256,2048]{1,0:T(8,128)(2,1)}, bf16[256,2048]{1,0:T(8,128)(2,1)}, u32[]{:S(2)}, u32[]{:S(2)}) collective-permute-start(bf16[256,2048]{1,0:T(8,128)(2,1)} %collective-permute-done.2.refs_14_), channel_id=1, source_target_pairs={{0,1},{1,0},{2,3},{3,2},{4,5},{5,4},{6,7},{7,6},{8,9},{9,8},{10,11... | collective-permute-start | bytes 3145736 | tf_op jit(solution)/shard_map/ppermute | solution.py:16
  183.1 197.7 %reduce-scatter.5.cloned.1.call-start = ((), (), s32[]{:S(2)}) async-start(), calls=%async_computation.11 | async-start | bytes 3604480 | tf_op jit(solution)/shard_map/reduce_scatter | solution.py:904
  183.4 23.2 %collective-permute-start.34 = (bf16[128,2048]{1,0:T(8,128)(2,1)}, bf16[128,2048]{1,0:T(8,128)(2,1)S(1)}, u32[]{:S(2)}, u32[]{:S(2)}) collective-permute-start(bf16[128,2048]{1,0:T(8,128)(2,1)} %copy-done.56), channel_id=1, source_target_pairs={{0,1},{1,0},{2,3},{3,2},{4,5},{5,4},{6,7},{7,6},{8,9},{9,8},{10,11... | collective-permute-start | bytes 1572872 | tf_op jit(solution)/shard_map/ppermute | solution.py:16
  222.5 29.7 %collective-permute-start.36 = (bf16[256,2048]{1,0:T(8,128)(2,1)}, bf16[256,2048]{1,0:T(8,128)(2,1)S(1)}, u32[]{:S(2)}, u32[]{:S(2)}) collective-permute-start(bf16[256,2048]{1,0:T(8,128)(2,1)} %get-tuple-element.173.refs_0_), channel_id=1, source_target_pairs={{0,1},{1,0},{2,3},{3,2},{4,5},{5,4},{6,7},{7,6},{8,9},{9,8},{10,11... | collective-permute-start | bytes 3145736 | tf_op jit(solution)/shard_map/ppermute | solution.py:16
  223.0 29.2 %collective-permute-start.37 = (bf16[256,2048]{1,0:T(8,128)(2,1)}, bf16[256,2048]{1,0:T(8,128)(2,1)}, u32[]{:S(2)}, u32[]{:S(2)}) collective-permute-start(bf16[256,2048]{1,0:T(8,128)(2,1)} %get-tuple-element.173.refs_0_), channel_id=1, source_target_pairs={{0,2},{1,3},{2,0},{3,1},{4,6},{5,7},{6,4},{7,5},{8,10},{9,11},{10,... | collective-permute-start | bytes 3145736 | tf_op jit(solution)/shard_map/ppermute | solution.py:16
  225.2 27.1 %collective-permute-start.38 = (bf16[256,2048]{1,0:T(8,128)(2,1)}, bf16[256,2048]{1,0:T(8,128)(2,1)}, u32[]{:S(2)}, u32[]{:S(2)}) collective-permute-start(bf16[256,2048]{1,0:T(8,128)(2,1)} %get-tuple-element.173.refs_0_), channel_id=1, source_target_pairs={{0,4},{1,5},{2,6},{3,7},{4,0},{5,1},{6,2},{7,3},{8,12},{9,13},{10,... | collective-permute-start | bytes 3145736 | tf_op jit(solution)/shard_map/ppermute | solution.py:16
  306.5 210.3 %reduce-scatter.9.cloned.1.call-start = ((), (), s32[]{:S(2)}) async-start(), calls=%async_computation.13 | async-start | bytes 7208960 | tf_op jit(solution)/shard_map/reduce_scatter | solution.py:904
  312.6 25.9 %collective-permute-start.40 = (bf16[2,128,2048]{2,1,0:T(8,128)(2,1)S(1)}, bf16[2,128,2048]{2,1,0:T(8,128)(2,1)}, u32[]{:S(2)}, u32[]{:S(2)}) collective-permute-start(bf16[2,128,2048]{2,1,0:T(8,128)(2,1)S(1)} %get-tuple-element.189), channel_id=1, source_target_pairs={{0,2},{1,3},{2,0},{3,1},{4,6},{5,7},{6,4},{7,5},{8,10},{9,11},{10,... | collective-permute-start | bytes 3145736 | tf_op jit(solution)/shard_map/ppermute | solution.py:16
  314.0 25.5 %collective-permute-start.41 = (bf16[2,128,2048]{2,1,0:T(8,128)(2,1)S(1)}, bf16[2,128,2048]{2,1,0:T(8,128)(2,1)}, u32[]{:S(2)}, u32[]{:S(2)}) collective-permute-start(bf16[2,128,2048]{2,1,0:T(8,128)(2,1)S(1)} %get-tuple-element.190), channel_id=1, source_target_pairs={{0,4},{1,5},{2,6},{3,7},{4,0},{5,1},{6,2},{7,3},{8,12},{9,13},{10,... | collective-permute-start | bytes 3145736 | tf_op jit(solution)/shard_map/ppermute | solution.py:16
  387.2 38.0 %collective-permute-start.45 = (bf16[128,2048]{1,0:T(8,128)(2,1)S(1)}, bf16[128,2048]{1,0:T(8,128)(2,1)S(1)}, u32[]{:S(2)}, u32[]{:S(2)}) collective-permute-start(bf16[128,2048]{1,0:T(8,128)(2,1)S(1)} %slice.319), channel_id=1, source_target_pairs={{0,2},{1,3},{2,0},{3,1},{4,6},{5,7},{6,4},{7,5},{8,10},{9,11},{10,... | collective-permute-start | bytes 1572872 | tf_op jit(solution)/shard_map/ppermute | solution.py:16
  388.8 36.3 %collective-permute-start.46 = (bf16[128,2048]{1,0:T(8,128)(2,1)S(1)}, bf16[128,2048]{1,0:T(8,128)(2,1)S(1)}, u32[]{:S(2)}, u32[]{:S(2)}) collective-permute-start(bf16[128,2048]{1,0:T(8,128)(2,1)S(1)} %slice.320), channel_id=1, source_target_pairs={{0,4},{1,5},{2,6},{3,7},{4,0},{5,1},{6,2},{7,3},{8,12},{9,13},{10,... | collective-permute-start | bytes 1572872 | tf_op jit(solution)/shard_map/ppermute | solution.py:16
  389.6 32.9 %collective-permute-start.47 = (bf16[2,128,2048]{2,1,0:T(8,128)(2,1)S(1)}, bf16[2,128,2048]{2,1,0:T(8,128)(2,1)S(1)}, u32[]{:S(2)}, u32[]{:S(2)}) collective-permute-start(bf16[2,128,2048]{2,1,0:T(8,128)(2,1)S(1)} %copy-done.16), channel_id=1, source_target_pairs={{0,2},{1,3},{2,0},{3,1},{4,6},{5,7},{6,4},{7,5},{8,10},{9,11},{10,... | collective-permute-start | bytes 3145736 | tf_op jit(solution)/shard_map/ppermute | solution.py:16
  391.0 34.2 %collective-permute-start.48 = (bf16[2,128,2048]{2,1,0:T(8,128)(2,1)S(1)}, bf16[2,128,2048]{2,1,0:T(8,128)(2,1)}, u32[]{:S(2)}, u32[]{:S(2)}) collective-permute-start(bf16[2,128,2048]{2,1,0:T(8,128)(2,1)S(1)} %get-tuple-element.222), channel_id=1, source_target_pairs={{0,4},{1,5},{2,6},{3,7},{4,0},{5,1},{6,2},{7,3},{8,12},{9,13},{10,... | collective-permute-start | bytes 3145736 | tf_op jit(solution)/shard_map/ppermute | solution.py:16
  439.1 30.1 %collective-permute-start.49 = (bf16[4,256,2048]{2,1,0:T(8,128)(2,1)}, bf16[4,256,2048]{2,1,0:T(8,128)(2,1)}, u32[]{:S(2)}, u32[]{:S(2)}) collective-permute-start(bf16[4,256,2048]{2,1,0:T(8,128)(2,1)} %get-tuple-element.229), channel_id=1, source_target_pairs={{0,1},{1,0},{2,3},{3,2},{4,5},{5,4},{6,7},{7,6},{8,9},{9,8},{10,11... | collective-permute-start | bytes 12582920 | tf_op jit(solution)/shard_map/ppermute | solution.py:16
  440.4 28.8 %all-to-all-start.3 = ((bf16[8,256,256]{2,1,0:T(8,128)(2,1)}), bf16[8,256,256]{2,1,0:T(8,128)(2,1)S(1)}, u32[]{:S(2)}, u32[]{:S(2)}) async-start(bf16[8,256,256]{2,1,0:T(8,128)(2,1)} %get-tuple-element.233), calls=%async_computation.4 | async-start | bytes 2097152 | tf_op jit(solution)/shard_map/all_to_all | solution.py:112
  444.5 129.3 %reduce-scatter.7.cloned.1.call-start = ((), (), s32[]{:S(2)}) async-start(), calls=%async_computation.12 | async-start | bytes 3932160 | tf_op jit(solution)/shard_map/reduce_scatter | solution.py:904
  444.8 57.9 %collective-permute-start.60 = (bf16[256,2048]{1,0:T(8,128)(2,1)}, bf16[256,2048]{1,0:T(8,128)(2,1)}, u32[]{:S(2)}, u32[]{:S(2)}) collective-permute-start(bf16[256,2048]{1,0:T(8,128)(2,1)} %collective-permute-done.37.refs_2_), channel_id=1, source_target_pairs={{0,1},{1,0},{2,3},{3,2},{4,5},{5,4},{6,7},{7,6},{8,9},{9,8},{10,11... | collective-permute-start | bytes 3145736 | tf_op jit(solution)/shard_map/ppermute | solution.py:16
  447.3 56.0 %collective-permute-start.61 = (bf16[256,2048]{1,0:T(8,128)(2,1)}, bf16[256,2048]{1,0:T(8,128)(2,1)}, u32[]{:S(2)}, u32[]{:S(2)}) collective-permute-start(bf16[256,2048]{1,0:T(8,128)(2,1)} %collective-permute-done.38.refs_4_), channel_id=1, source_target_pairs={{0,1},{1,0},{2,3},{3,2},{4,5},{5,4},{6,7},{7,6},{8,9},{9,8},{10,11... | collective-permute-start | bytes 3145736 | tf_op jit(solution)/shard_map/ppermute | solution.py:16
  473.6 24.1 %collective-permute-start.53 = (bf16[2,128,2048]{2,1,0:T(8,128)(2,1)}, bf16[2,128,2048]{2,1,0:T(8,128)(2,1)S(1)}, u32[]{:S(2)}, u32[]{:S(2)}) collective-permute-start(bf16[2,128,2048]{2,1,0:T(8,128)(2,1)} %get-tuple-element.239), channel_id=1, source_target_pairs={{0,2},{1,3},{2,0},{3,1},{4,6},{5,7},{6,4},{7,5},{8,10},{9,11},{10,... | collective-permute-start | bytes 3145736 | tf_op jit(solution)/shard_map/ppermute | solution.py:16
  475.2 23.7 %collective-permute-start.54 = (bf16[2,128,2048]{2,1,0:T(8,128)(2,1)S(1)}, bf16[2,128,2048]{2,1,0:T(8,128)(2,1)S(1)}, u32[]{:S(2)}, u32[]{:S(2)}) collective-permute-start(bf16[2,128,2048]{2,1,0:T(8,128)(2,1)S(1)} %get-tuple-element.240), channel_id=1, source_target_pairs={{0,4},{1,5},{2,6},{3,7},{4,0},{5,1},{6,2},{7,3},{8,12},{9,13},{10,... | collective-permute-start | bytes 3145736 | tf_op jit(solution)/shard_map/ppermute | solution.py:16
  486.3 123.5 %reduce-scatter.11.cloned.1.call-start = ((), (), s32[]{:S(2)}) async-start(), calls=%async_computation.14 | async-start | bytes 1392640 | tf_op jit(solution)/shard_map/reduce_scatter | solution.py:904
  516.8 34.3 %collective-permute-start.58 = (bf16[512,1408]{1,0:T(8,128)(2,1)}, bf16[512,1408]{1,0:T(8,128)(2,1)}, u32[]{:S(2)}, u32[]{:S(2)}) collective-permute-start(bf16[512,1408]{1,0:T(8,128)(2,1)} %reduce-scatter.9.cloned.1.call-done.refs_0_), channel_id=1, source_target_pairs={{0,2},{1,3},{2,0},{3,1},{4,6},{5,7},{6,4},{7,5},{8,10},{9,11},{10,... | collective-permute-start | bytes 4325384 | tf_op jit(solution)/shard_map/ppermute | solution.py:16
  517.3 34.0 %collective-permute-start.59 = (bf16[512,1408]{1,0:T(8,128)(2,1)}, bf16[512,1408]{1,0:T(8,128)(2,1)}, u32[]{:S(2)}, u32[]{:S(2)}) collective-permute-start(bf16[512,1408]{1,0:T(8,128)(2,1)} %reduce-scatter.9.cloned.1.call-done.refs_0_), channel_id=1, source_target_pairs={{0,4},{1,5},{2,6},{3,7},{4,0},{5,1},{6,2},{7,3},{8,12},{9,13},{10,... | collective-permute-start | bytes 4325384 | tf_op jit(solution)/shard_map/ppermute | solution.py:16
  551.3 23.6 %collective-permute-start.66 = (bf16[512,1408]{1,0:T(8,128)(2,1)}, bf16[512,1408]{1,0:T(8,128)(2,1)S(1)}, u32[]{:S(2)}, u32[]{:S(2)}) collective-permute-start(bf16[512,1408]{1,0:T(8,128)(2,1)} %collective-permute-done.59.refs_4_), channel_id=1, source_target_pairs={{0,1},{1,0},{2,3},{3,2},{4,5},{5,4},{6,7},{7,6},{8,9},{9,8},{10,11... | collective-permute-start | bytes 4325384 | tf_op jit(solution)/shard_map/ppermute | solution.py:16
  552.5 21.9 %collective-permute-start.65 = (bf16[512,1408]{1,0:T(8,128)(2,1)}, bf16[512,1408]{1,0:T(8,128)(2,1)}, u32[]{:S(2)}, u32[]{:S(2)}) collective-permute-start(bf16[512,1408]{1,0:T(8,128)(2,1)} %collective-permute-done.58.refs_2_), channel_id=1, source_target_pairs={{0,1},{1,0},{2,3},{3,2},{4,5},{5,4},{6,7},{7,6},{8,9},{9,8},{10,11... | collective-permute-start | bytes 4325384 | tf_op jit(solution)/shard_map/ppermute | solution.py:16
  609.8 57.0 %collective-permute-start.89 = (bf16[176,2048]{1,0:T(8,128)(2,1)}, bf16[176,2048]{1,0:T(8,128)(2,1)}, u32[]{:S(2)}, u32[]{:S(2)}) collective-permute-start(bf16[176,2048]{1,0:T(8,128)(2,1)} %collective-permute-done.52.refs_4_), channel_id=1, source_target_pairs={{0,1},{1,0},{2,3},{3,2},{4,5},{5,4},{6,7},{7,6},{8,9},{9,8},{10,11... | collective-permute-start | bytes 2162696 | tf_op jit(solution)/shard_map/ppermute | solution.py:16
  609.8 40.0 %collective-permute-start.90 = (bf16[176,2048]{1,0:T(8,128)(2,1)}, bf16[176,2048]{1,0:T(8,128)(2,1)}, u32[]{:S(2)}, u32[]{:S(2)}) collective-permute-start(bf16[176,2048]{1,0:T(8,128)(2,1)} %collective-permute-done.52.refs_4_), channel_id=1, source_target_pairs={{0,2},{1,3},{2,0},{3,1},{4,6},{5,7},{6,4},{7,5},{8,10},{9,11},{10,... | collective-permute-start | bytes 2162696 | tf_op jit(solution)/shard_map/ppermute | solution.py:16
  611.4 28.4 %collective-permute-start.74 = (bf16[128,2048]{1,0:T(8,128)(2,1)S(1)}, bf16[128,2048]{1,0:T(8,128)(2,1)S(1)}, u32[]{:S(2)}, u32[]{:S(2)}) collective-permute-start(bf16[128,2048]{1,0:T(8,128)(2,1)S(1)} %get-tuple-element.278), channel_id=1, source_target_pairs={{0,2},{1,3},{2,0},{3,1},{4,6},{5,7},{6,4},{7,5},{8,10},{9,11},{10,... | collective-permute-start | bytes 1572872 | tf_op jit(solution)/shard_map/ppermute | solution.py:16
  611.9 29.4 %collective-permute-start.75 = (bf16[128,2048]{1,0:T(8,128)(2,1)S(1)}, bf16[128,2048]{1,0:T(8,128)(2,1)S(1)}, u32[]{:S(2)}, u32[]{:S(2)}) collective-permute-start(bf16[128,2048]{1,0:T(8,128)(2,1)S(1)} %get-tuple-element.279), channel_id=1, source_target_pairs={{0,4},{1,5},{2,6},{3,7},{4,0},{5,1},{6,2},{7,3},{8,12},{9,13},{10,... | collective-permute-start | bytes 1572872 | tf_op jit(solution)/shard_map/ppermute | solution.py:16
  612.5 33.5 %collective-permute-start.77 = (bf16[544,256]{1,0:T(8,128)(2,1)}, bf16[544,256]{1,0:T(8,128)(2,1)S(1)}, u32[]{:S(2)}, u32[]{:S(2)}) collective-permute-start(bf16[544,256]{1,0:T(8,128)(2,1)} %reduce-scatter.11.cloned.1.call-done.refs_0_), channel_id=1, source_target_pairs={{0,1},{1,0},{2,3},{3,2},{4,5},{5,4},{6,7},{7,6},{8,9},{9,8},{10,11... | collective-permute-start | bytes 835592 | tf_op jit(solution)/shard_map/ppermute | solution.py:16
  (125 other events, 1242.5 us)
Sparse Core Ops, SparseCore 0:
  11.9 85.4 all-gather.5
  99.6 104.9 all-gather.7
  206.1 57.4 all-gather.9
  306.6 54.9 reduce-scatter.4
  366.6 100.5 reduce-scatter.8
  486.5 57.7 reduce-scatter.6
  574.4 25.7 reduce-scatter.10

commit v4 on v3

--- a/solution.py
+++ b/solution.py
@@ -1016,7 +1016,7 @@
     down = reduce_last(down_state)
     output = (hidden + total_of(down)).astype(LOW)
     gwdown_parts = gather_rest(gwdown_first, gwdown_far)
-    lanes = min(256, width)
+    lanes = min(512, width)
     gwdown = run_spread(
         place_arr,
         gwdown_parts,

time: 693 us -> 692 us (level)
  no operation moved by 1% of the time
where the time goes in v4:
time: 692 us; the launch traced here: 682 us
  waiting for transfers between devices  245 us (35%)
  Pallas kernels  207 us (30%)
  starting transfers between devices  70.8 us (10%)
  other arithmetic  43.1 us (6%)
  matrix products  43.1 us (6%)
  local copies, waits for them, and re-layouts  42.3 us (6%)
  between operations  15.9 us (2%)
  blocking collectives  14.9 us (2%)
    ppermute x92, waiting for transfers between devices, swap(): return lax.ppermute(x, 'seq', [(i, i ^ bits) for i in range(count)])  214 us
    ppermute x92, starting transfers between devices, swap(): return lax.ppermute(x, 'seq', [(i, i ^ bits) for i in range(count)])  54 us
    pallas_call x4, Pallas kernels, run_spread(): pl.pallas_call(functools.partial(spread_kernel, heights(entries), layout)...  34.5 us
    pallas_call x1, Pallas kernels, run_gate_back(): pl.pallas_call(gate_back_kernel, grid=(count // 2,), in_specs=[block(widt...  32.1 us
    pallas_call x1, Pallas kernels, run_mixer_backward(): pl.pallas_call(mixer_backward, out_shape=shapes, grid_spec=pltpu.Prefetch...  26.5 us
    pallas_call x1, Pallas kernels, run_gate(): pl.pallas_call(functools.partial(gate_kernel, sizes, heights(others)), gr...  25.6 us
    convert_element_type x9, other arithmetic, add(): return (first.astype(WIDE) + second.astype(WIDE)).astype(LOW)  23.9 us
    pallas_call x2, Pallas kernels, run_pairs(): pl.pallas_call(functools.partial(pairs_kernel, len(terms), [t[2] for t in...  23.5 us
  transfers between devices with their start and end apart: 103, of which 42 were waited for; matrix products, arithmetic and copies ran while one was open for 17% of the time, Pallas kernels for 24%

profile of v4, /device:TPU:0, one launch (start us, length us, event | category | flops | bytes accessed | tf_op | source)
XLA Modules:
  0.0 682.0 jit_solution(4594187573905610459)
XLA Ops:
  23.1 14.9 %all-gather.1 = bf16[4,31,512]{2,1,0:T(8,128)(2,1)S(1)} all-gather(bf16[1,31,512]{2,1,0:T(8,128)(2,1)S(1)} %bitcast.186), channel_id=2, replica_groups=mesh['fsdp'=4,'seq'=8] {'fsdp'}, dimensions={0}, use_global_device_ids=true | all-gather | bytes 158720 | tf_op jit(solution)/shard_map/all_gather | solution.py:845
  42.8 22.2 %collective-permute-done.3.refs_4_ = bf16[256,2048]{1,0:T(8,128)(2,1)} collective-permute-done((bf16[256,2048]{1,0:T(8,128)(2,1)S(1)}, bf16[256,2048]{1,0:T(8,128)(2,1)}, u32[]{:S(2)}, u32[]{:S(2)}) %collective-permute-start.3) | collective-permute-done | bytes 1048608 | tf_op jit(solution)/shard_map/ppermute | solution.py:16
  69.4 9.0 %collective-permute-done.4.refs_6_ = bf16[128,2048]{1,0:T(8,128)(2,1)S(1)} collective-permute-done((bf16[128,2048]{1,0:T(8,128)(2,1)S(1)}, bf16[128,2048]{1,0:T(8,128)(2,1)S(1)}, u32[]{:S(2)}, u32[]{:S(2)}) %collective-permute-start.4) | collective-permute-done | bytes 524320 | tf_op jit(solution)/shard_map/ppermute | solution.py:16
  85.8 7.4 %collective-permute-done.7.refs_16_ = bf16[128,2048]{1,0:T(8,128)(2,1)S(1)} collective-permute-done((bf16[128,2048]{1,0:T(8,128)(2,1)S(1)}, bf16[128,2048]{1,0:T(8,128)(2,1)S(1)}, u32[]{:S(2)}, u32[]{:S(2)}) %collective-permute-start.7) | collective-permute-done | bytes 524320 | tf_op jit(solution)/shard_map/ppermute | solution.py:16
  102.3 14.6 %project.1 = (bf16[8,256,768]{2,1,0:T(8,128)(2,1)}, f32[8,256,128]{2,1,0:T(8,128)}, bf16[8,256,2048]{2,1,0:T(8,128)(2,1)}) custom-call(bf16[256,2048]{1,0:T(8,128)(2,1)} %copy-done.15, bf16[256,2048]{1,0:T(8,128)(2,1)} %collective-permute-done.18.refs_1_, bf16[256,2048]{1,0:T(8,128)(2,1)} %collective-permute-done.5.refs_2_, ...), custom_call_target="tpu_custom_call" | custom-call | flops 18400000000 | bytes 56000000 | tf_op jit(solution)/shard_map/project/pallas_call | solution.py:456
  117.0 8.7 %collective-permute-done.12.refs_4_ = bf16[2048,256]{1,0:T(8,128)(2,1)S(1)} collective-permute-done((bf16[2048,256]{1,0:T(8,128)(2,1)S(1)}, bf16[2048,256]{1,0:T(8,128)(2,1)S(1)}, u32[]{:S(2)}, u32[]{:S(2)}) %collective-permute-start.12) | collective-permute-done | bytes 1048608 | tf_op jit(solution)/shard_map/ppermute | solution.py:16
  128.9 10.9 %mixer_forward.2 = (bf16[8,128,256]{2,1,0:T(8,128)(2,1)}, f32[2,2,8,128,128]{4,3,2,1,0:T(8,128)}, bf16[2,2,8,128,128]{4,3,2,1,0:T(8,128)(2,1)}, bf16[2,2,8,128,1...) custom-call(s32[1]{0:T(128)} %bitcast.place_ref, ...), custom_call_target="tpu_custom_call" | custom-call | flops 11500000256 | bytes 35000000 | tf_op jit(solution)/shard_map/mixer_forward/pallas_call | solution.py:332
  139.8 3.7 all-to-all-start
  144.6 10.9 %mixer_forward.3 = (bf16[8,128,256]{2,1,0:T(8,128)(2,1)}, f32[2,2,8,128,128]{4,3,2,1,0:T(8,128)}, bf16[2,2,8,128,128]{4,3,2,1,0:T(8,128)(2,1)}, bf16[2,2,8,128,1...) custom-call(s32[1]{0:T(128)} %bitcast.place_ref, ...), custom_call_target="tpu_custom_call", output_to_operand_aliasing={{1}: (5, {}), {2}: (6, {}), {3}: (7, {}), {4}: (8, {}), {5}... | custom-call | flops 11500000256 | bytes 35000000 | tf_op jit(solution)/shard_map/mixer_forward/pallas_call | solution.py:332
  155.5 4.2 all-to-all-start.1
  160.3 9.1 %all-to-all-done.1.refs_11_ = bf16[8,128,256]{2,1,0:T(8,128)(2,1)S(1)} async-done(((bf16[8,128,256]{2,1,0:T(8,128)(2,1)}), bf16[8,128,256]{2,1,0:T(8,128)(2,1)S(1)}, u32[]{:S(2)}, u32[]{:S(2)}) %all-to-all-start.1) | async-done | bytes 524320 | tf_op jit(solution)/shard_map/all_to_all | solution.py:112
  170.8 10.6 %branch.1 = (f32[256,2048]{1,0:T(8,128)}, bf16[256,2048]{1,0:T(8,128)(2,1)}, bf16[256,2048]{1,0:T(8,128)(2,1)}) custom-call(s32[1]{0:T(128)} %bitcast.place_ref, bf16[2048,256]{1,0:T(8,128)(2,1)} %copy-done.10, bf16[2048,256]{1,0:T(8,128)(2,1)} %collective-permute-done.9.refs_1_, bf16[2048,256]{1,0:T(8,128)(2,1)} %collective-permute-done.10.refs_2_, ...), custom_call_target="tpu_custom_call" | custom-call | flops 11500000256 | bytes 35000000 | tf_op jit(solution)/shard_map/branch/pallas_call | solution.py:632
  183.5 21.2 %collective-permute-done.26.refs_4_ = bf16[256,2048]{1,0:T(8,128)(2,1)S(1)} collective-permute-done((bf16[256,2048]{1,0:T(8,128)(2,1)}, bf16[256,2048]{1,0:T(8,128)(2,1)S(1)}, u32[]{:S(2)}, u32[]{:S(2)}) %collective-permute-start.26) | collective-permute-done | bytes 1048608 | tf_op jit(solution)/shard_map/ppermute | solution.py:16
  209.9 11.1 %collective-permute-done.28.refs_6_ = bf16[128,2048]{1,0:T(8,128)(2,1)} collective-permute-done((bf16[128,2048]{1,0:T(8,128)(2,1)S(1)}, bf16[128,2048]{1,0:T(8,128)(2,1)}, u32[]{:S(2)}, u32[]{:S(2)}) %collective-permute-start.28) | collective-permute-done | bytes 524320 | tf_op jit(solution)/shard_map/ppermute | solution.py:16
  226.6 25.6 %gate.1 = (bf16[8,256,704]{2,1,0:T(8,128)(2,1)}, bf16[8,256,704]{2,1,0:T(8,128)(2,1)}, bf16[8,256,704]{2,1,0:T(8,128)(2,1)}, bf16[8,256,2048]{2,1,0:T(8,128)(2,1)}, bf16[8,256,2048]{2,1,0:T(8,128)(2,1)}) custom-call(bf16[256,2048]{1,0:T(8,128)(2,1)} %get-tuple-element.169.refs_0_, bf16[256,2048]{1,0:T(8,128)(2,1)} %copy-done.49, ...), custom_call_target="tpu_custom_call" | custom-call | flops 28750000128 | bytes 87500000 | tf_op jit(solution)/shard_map/gate/pallas_call | solution.py:513
  252.3 11.4 %all-gather.10.cloned.1.call-done.down_ref.refs_1_ = bf16[704,2048]{1,0:T(8,128)(2,1)} async-done(((bf16[176,2048]{1,0:T(8,128)(2,1)}), bf16[704,2048]{1,0:T(8,128)(2,1)}) %all-gather.10.cloned.1.call-update) | async-done | bytes 2883600 | tf_op jit(solution)/shard_map/all_gather | solution.py:834
  263.7 32.1 %gate_back.1 = (bf16[8,256,1408]{2,1,0:T(8,128)(2,1)}, bf16[4,256,2048]{2,1,0:T(8,128)(2,1)}, bf16[4,256,2048]{2,1,0:T(8,128)(2,1)}) custom-call(bf16[8,256,2048]{2,1,0:T(8,128)(2,1)} %get-tuple-element.170.cot_ref, bf16[8,256,704]{2,1,0:T(8,128)(2,1)} %get-tuple-element.174.up_ref, bf16[8,256,704]{2,1,0:T(8,128)(2,1)} %get-tuple-element.175.gate_ref, ...), custom_call_target="tpu_custom_call" | custom-call | flops 36800000000 | bytes 112000000 | tf_op jit(solution)/shard_map/gate_back/pallas_call | solution.py:557
  295.7 10.7 %bitcast_convert_fusion.2 = bf16[704,2048]{1,0:T(8,128)(2,1)} fusion(bf16[8,256,704]{2,1,0:T(8,128)(2,1)} %get-tuple-element.198.refs_0_, bf16[8,256,2048]{2,1,0:T(8,128)(2,1)} %get-tuple-element.170.cot_ref), kind=kOutput, calls=%fused_computation.2 | convolution fusion | flops 5907021824 | bytes 14155776 | tf_op jit(solution)/shard_map/brf,brd->fd/dot_general | solution.py:910
  315.4 17.1 %bitcast_convert_fusion = bf16[2048,1408]{1,0:T(8,128)(2,1)} fusion(bf16[8,256,2048]{2,1,0:T(8,128)(2,1)S(1)} %copy-done.68, bf16[8,256,1408]{2,1,0:T(8,128)(2,1)} %get-tuple-element.184), kind=kOutput, calls=%fused_computation | convolution fusion | flops 11814043648 | bytes 19922944 | tf_op jit(solution)/shard_map/brd,brf->df/dot_general | solution.py:916
  332.6 5.9 collective-permute-done.40.refs_12_
  344.0 10.6 %down.1 = (bf16[4,256,2048]{2,1,0:T(8,128)(2,1)}, bf16[4,256,2048]{2,1,0:T(8,128)(2,1)}) custom-call(bf16[8,256,704]{2,1,0:T(8,128)(2,1)} %get-tuple-element.198.refs_0_, bf16[704,2048]{1,0:T(8,128)(2,1)} %all-gather.10.cloned.1.call-done.down_ref.refs_1_), custom_call_target="tpu_custom_call" | custom-call | flops 13799999488 | bytes 42000000 | tf_op jit(solution)/shard_map/down/pallas_call | solution.py:588
  356.6 9.8 %branch_back.1 = (f32[256,2048]{1,0:T(8,128)}, f32[1,2048]{1,0:T(1,128)}, bf16[8,256,256]{2,1,0:T(8,128)(2,1)}, bf16[8,256,256]{2,1,0:T(8,128)(2,1)}) custom-call(s32[1]{0:T(128)} %bitcast.place_ref, bf16[2048,256]{1,0:T(8,128)(2,1)} %copy-done.10, bf16[2048,256]{1,0:T(8,128)(2,1)} %collective-permute-done.9.refs_1_, ...), custom_call_target="tpu_custom_call" | custom-call | flops 11500000256 | bytes 35000000 | tf_op jit(solution)/shard_map/branch_back/pallas_call | solution.py:704
  366.5 3.8 all-to-all-start.2
  370.3 3.7 collective-permute-done.44
  376.8 4.0 add_convert_fusion.2
  380.8 4.8 all-to-all-done.2.gout_ref
  392.4 26.5 %mixer_backward.1 = (bf16[8,2,128,768]{3,2,1,0:T(8,128)(2,1)}, bf16[8,2,128,128]{3,2,1,0:T(8,128)(2,1)}, f32[2,2,3,4,128]{4,3,2,1,0:T(4,128)}, f32[2,2,1,128]{3,2,1,0:T(1,128)}) custom-call(s32[1]{0:T(128)} %bitcast.place_ref, bf16[8,2,128,768]{3,2,1,0:T(8,128)(2,1)} %bitcast.204, f32[2,3,4,128]{3,2,1,0:T(4,128)} %copy_bitcast_fusion.taps_ref, ...), custom_call_target="tpu_custom_call" | custom-call | flops 29899999232 | bytes 91000000 | tf_op jit(solution)/shard_map/mixer_backward/pallas_call | solution.py:364
  426.1 13.0 %input_back.1 = (bf16[4,256,2048]{2,1,0:T(8,128)(2,1)}, bf16[4,256,2048]{2,1,0:T(8,128)(2,1)}) custom-call(bf16[8,256,768]{2,1,0:T(8,128)(2,1)} %bitcast.179, bf16[8,256,128]{2,1,0:T(8,128)(2,1)} %bitcast.181, bf16[2048,1024]{1,0:T(8,128)(2,1)} %all-gather.6.cloned.1.call-done.refs_10_.refs_2_, bf16[128,2048]{1,0:T(8,128)(2,1)} %pad.19.refs_11_.refs_3_), custom_call_target="tpu_custom_call" | custom-call | flops 1150000000 | bytes 3500000 | tf_op jit(solution)/shard_map/input_back/pallas_call | solution.py:588
  440.4 4.0 all-to-all-start.3
  447.7 11.1 %collective-permute-done.51.refs_2_ = bf16[176,2048]{1,0:T(8,128)(2,1)} collective-permute-done((bf16[176,2048]{1,0:T(8,128)(2,1)S(1)}, bf16[176,2048]{1,0:T(8,128)(2,1)}, u32[]{:S(2)}, u32[]{:S(2)}) %collective-permute-start.51) | collective-permute-done | bytes 720928 | tf_op jit(solution)/shard_map/ppermute | solution.py:16
  459.2 4.7 convolution_bitcast_fusion
  464.0 5.2 all-to-all-done.3.cols_ref
  469.2 4.4 add_convert_fusion
  475.8 10.5 %bitcast_convert_fusion.1 = bf16[2048,768]{1,0:T(8,128)(2,1)} fusion(bf16[8,256,2048]{2,1,0:T(8,128)(2,1)} %get-tuple-element.231, bf16[8,256,768]{2,1,0:T(8,128)(2,1)S(1)} %bitcast.180), kind=kOutput, calls=%fused_computation.1 | convolution fusion | flops 6444023808 | bytes 14680064 | tf_op jit(solution)/shard_map/brd,bre->de/dot_general | solution.py:951
  490.7 7.0 %collective-permute-done.53 = bf16[2,128,2048]{2,1,0:T(8,128)(2,1)S(1)} collective-permute-done((bf16[2,128,2048]{2,1,0:T(8,128)(2,1)}, bf16[2,128,2048]{2,1,0:T(8,128)(2,1)S(1)}, u32[]{:S(2)}, u32[]{:S(2)}) %collective-permute-start.53) | collective-permute-done | bytes 1048608 | tf_op jit(solution)/shard_map/ppermute | solution.py:16
  503.3 7.7 %output_weights.1 = bf16[2048,256]{1,0:T(8,128)(2,1)} custom-call(s32[1]{0:T(128)} %bitcast.place_ref, bf16[8,256,256]{2,1,0:T(8,128)(2,1)} %copy-done.11, bf16[256,2048]{1,0:T(8,128)(2,1)} %get-tuple-element.173.refs_0_, bf16[256,2048]{1,0:T(8,128)(2,1)} %copy-done.47, bf16[256,2048]{1,0:T(8,128)(2,1)} %collective-permute-done.37.refs_2_, ...), custom_call_target="tpu_custom_call" | custom-call | flops 9200000000 | bytes 28000000 | tf_op jit(solution)/shard_map/output_weights/pallas_call | solution.py:751
  521.7 4.8 fusion.9
  528.9 22.2 %collective-permute-done.58.refs_2_ = bf16[512,1408]{1,0:T(8,128)(2,1)} collective-permute-done((bf16[512,1408]{1,0:T(8,128)(2,1)}, bf16[512,1408]{1,0:T(8,128)(2,1)}, u32[]{:S(2)}, u32[]{:S(2)}) %collective-permute-start.58) | collective-permute-done | bytes 1441824 | tf_op jit(solution)/shard_map/ppermute | solution.py:16
  556.3 14.9 %collective-permute-done.67.refs_6_ = bf16[256,1408]{1,0:T(8,128)(2,1)} collective-permute-done((bf16[256,1408]{1,0:T(8,128)(2,1)S(1)}, bf16[256,1408]{1,0:T(8,128)(2,1)}, u32[]{:S(2)}, u32[]{:S(2)}) %collective-permute-start.67) | collective-permute-done | bytes 720928 | tf_op jit(solution)/shard_map/ppermute | solution.py:16
  576.3 14.0 %spread_gate_up.1 = f32[2,512,5632]{2,1,0:T(8,128)} custom-call(s32[1]{0:T(128)} %bitcast.place_ref, bf16[512,1408]{1,0:T(8,128)(2,1)} %reduce-scatter.9.cloned.1.call-done.refs_0_, bf16[512,1408]{1,0:T(8,128)(2,1)} %collective-permute-done.57.refs_1_, bf16[512,1408]{1,0:T(8,128)(2,1)} %collective-permute-done.58.refs_2_, ...), custom_call_target="tpu_custom_call" | custom-call | flops 11500000256 | bytes 35000000 | tf_op jit(solution)/shard_map/spread_gate_up/pallas_call | solution.py:788
  590.2 3.8 collective-permute-done.64.refs_4_
  599.4 6.5 collective-permute-done.71.refs_6_
  612.5 8.4 %spread_inputs.1 = f32[3,512,2048]{2,1,0:T(8,128)} custom-call(s32[1]{0:T(128)} %bitcast.place_ref, bf16[512,768]{1,0:T(8,128)(2,1)} %reduce-scatter.7.cloned.1.call-done.refs_0_, bf16[512,768]{1,0:T(8,128)(2,1)} %copy-done.53, bf16[512,768]{1,0:T(8,128)(2,1)} %collective-permute-done.72.refs_2_, bf16[512,768]{1,0:T(8,128)(2,1)} %collective-permute-done.84.refs_3_, ...), custom_call_target="tpu_custom_call" | custom-call | flops 11500000256 | bytes 35000000 | tf_op jit(solution)/shard_map/spread_inputs/pallas_call | solution.py:788
  620.9 18.9 %collective-permute-done.74 = bf16[128,2048]{1,0:T(8,128)(2,1)S(1)} collective-permute-done((bf16[128,2048]{1,0:T(8,128)(2,1)S(1)}, bf16[128,2048]{1,0:T(8,128)(2,1)S(1)}, u32[]{:S(2)}, u32[]{:S(2)}) %collective-permute-start.74) | collective-permute-done | bytes 524320 | tf_op jit(solution)/shard_map/ppermute | solution.py:16
  641.9 4.1 fusion.12
  650.4 6.7 collective-permute-done.82.refs_6_
  662.5 4.3 spread_output.1
  666.9 7.8 %spread_down.1 = f32[1408,2048]{1,0:T(8,128)} custom-call(s32[1]{0:T(128)} %bitcast.place_ref, bf16[176,2048]{1,0:T(8,128)(2,1)} %reduce-scatter.5.cloned.1.call-done.refs_0_, bf16[176,2048]{1,0:T(8,128)(2,1)} %collective-permute-done.50.refs_1_, bf16[176,2048]{1,0:T(8,128)(2,1)} %collective-permute-done.51.refs_2_, ...), custom_call_target="tpu_custom_call" | custom-call | flops 11500000256 | bytes 35000000 | tf_op jit(solution)/shard_map/spread_down/pallas_call | solution.py:788
  (436 shorter events, 157.8 us)
Async XLA Ops:
  7.2 90.2 %all-gather.6.cloned.1.call-start = ((), (), s32[]{:S(2)}) async-start(), calls=%async_computation.8 | async-start | bytes 5242880 | tf_op jit(solution)/shard_map/all_gather | solution.py:834
  11.8 214.7 %all-gather.8.cloned.1.call-start = ((), (), s32[]{:S(2)}) async-start(), calls=%async_computation.9 | async-start | bytes 7208960 | tf_op jit(solution)/shard_map/all_gather | solution.py:834
  11.9 28.5 %collective-permute-start = (bf16[256,2048]{1,0:T(8,128)(2,1)}, bf16[256,2048]{1,0:T(8,128)(2,1)}, u32[]{:S(2)}, u32[]{:S(2)}) collective-permute-start(bf16[256,2048]{1,0:T(8,128)(2,1)} %bitcast.18.refs_10_.refs_17_), channel_id=1, source_target_pairs={{0,1},{1,0},{2,3},{3,2},{4,5},{5,4},{6,7},{7,6},{8,9},{9,8},{10,11... | collective-permute-start | bytes 3145736 | tf_op jit(solution)/shard_map/ppermute | solution.py:16
  12.4 28.0 %collective-permute-start.1 = (bf16[256,2048]{1,0:T(8,128)(2,1)}, bf16[256,2048]{1,0:T(8,128)(2,1)}, u32[]{:S(2)}, u32[]{:S(2)}) collective-permute-start(bf16[256,2048]{1,0:T(8,128)(2,1)} %bitcast.18.refs_10_.refs_17_), channel_id=1, source_target_pairs={{0,2},{1,3},{2,0},{3,1},{4,6},{5,7},{6,4},{7,5},{8,10},{9,11},{10,... | collective-permute-start | bytes 3145736 | tf_op jit(solution)/shard_map/ppermute | solution.py:16
  14.9 25.5 %collective-permute-start.2 = (bf16[256,2048]{1,0:T(8,128)(2,1)}, bf16[256,2048]{1,0:T(8,128)(2,1)}, u32[]{:S(2)}, u32[]{:S(2)}) collective-permute-start(bf16[256,2048]{1,0:T(8,128)(2,1)} %bitcast.18.refs_10_.refs_17_), channel_id=1, source_target_pairs={{0,4},{1,5},{2,6},{3,7},{4,0},{5,1},{6,2},{7,3},{8,12},{9,13},{10,... | collective-permute-start | bytes 3145736 | tf_op jit(solution)/shard_map/ppermute | solution.py:16
  40.5 24.5 %collective-permute-start.3 = (bf16[256,2048]{1,0:T(8,128)(2,1)S(1)}, bf16[256,2048]{1,0:T(8,128)(2,1)}, u32[]{:S(2)}, u32[]{:S(2)}) collective-permute-start(bf16[256,2048]{1,0:T(8,128)(2,1)S(1)} %fusion.4.refs_0_), channel_id=1, source_target_pairs={{0,4},{1,5},{2,6},{3,7},{4,0},{5,1},{6,2},{7,3},{8,12},{9,13},{10,... | collective-permute-start | bytes 3145736 | tf_op jit(solution)/shard_map/ppermute | solution.py:16
  42.0 25.4 %collective-permute-start.5 = (bf16[256,2048]{1,0:T(8,128)(2,1)S(1)}, bf16[256,2048]{1,0:T(8,128)(2,1)}, u32[]{:S(2)}, u32[]{:S(2)}) collective-permute-start(bf16[256,2048]{1,0:T(8,128)(2,1)S(1)} %fusion.4.refs_0_), channel_id=1, source_target_pairs={{0,2},{1,3},{2,0},{3,1},{4,6},{5,7},{6,4},{7,5},{8,10},{9,11},{10,... | collective-permute-start | bytes 3145736 | tf_op jit(solution)/shard_map/ppermute | solution.py:16
  98.8 44.7 %collective-permute-start.9 = (bf16[2048,256]{1,0:T(8,128)(2,1)S(1)}, bf16[2048,256]{1,0:T(8,128)(2,1)}, u32[]{:S(2)}, u32[]{:S(2)}) collective-permute-start(bf16[2048,256]{1,0:T(8,128)(2,1)S(1)} %slice.292.refs_0_), channel_id=1, source_target_pairs={{0,1},{1,0},{2,3},{3,2},{4,5},{5,4},{6,7},{7,6},{8,9},{9,8},{10,11... | collective-permute-start | bytes 3145736 | tf_op jit(solution)/shard_map/ppermute | solution.py:16
  98.9 27.8 %collective-permute-start.10 = (bf16[2048,256]{1,0:T(8,128)(2,1)S(1)}, bf16[2048,256]{1,0:T(8,128)(2,1)}, u32[]{:S(2)}, u32[]{:S(2)}) collective-permute-start(bf16[2048,256]{1,0:T(8,128)(2,1)S(1)} %slice.292.refs_0_), channel_id=1, source_target_pairs={{0,2},{1,3},{2,0},{3,1},{4,6},{5,7},{6,4},{7,5},{8,10},{9,11},{10,... | collective-permute-start | bytes 3145736 | tf_op jit(solution)/shard_map/ppermute | solution.py:16
  100.4 25.2 %collective-permute-start.12 = (bf16[2048,256]{1,0:T(8,128)(2,1)S(1)}, bf16[2048,256]{1,0:T(8,128)(2,1)S(1)}, u32[]{:S(2)}, u32[]{:S(2)}) collective-permute-start(bf16[2048,256]{1,0:T(8,128)(2,1)S(1)} %slice.292.refs_0_), channel_id=1, source_target_pairs={{0,4},{1,5},{2,6},{3,7},{4,0},{5,1},{6,2},{7,3},{8,12},{9,13},{10,... | collective-permute-start | bytes 3145736 | tf_op jit(solution)/shard_map/ppermute | solution.py:16
  143.5 25.9 %collective-permute-start.11 = (bf16[2048,256]{1,0:T(8,128)(2,1)}, bf16[2048,256]{1,0:T(8,128)(2,1)S(1)}, u32[]{:S(2)}, u32[]{:S(2)}) collective-permute-start(bf16[2048,256]{1,0:T(8,128)(2,1)} %collective-permute-done.10.refs_2_), channel_id=1, source_target_pairs={{0,1},{1,0},{2,3},{3,2},{4,5},{5,4},{6,7},{7,6},{8,9},{9,8},{10,11... | collective-permute-start | bytes 3145736 | tf_op jit(solution)/shard_map/ppermute | solution.py:16
  144.0 25.4 %collective-permute-start.13 = (bf16[2048,256]{1,0:T(8,128)(2,1)}, bf16[2048,256]{1,0:T(8,128)(2,1)}, u32[]{:S(2)}, u32[]{:S(2)}) collective-permute-start(bf16[2048,256]{1,0:T(8,128)(2,1)} %copy-done.21), channel_id=1, source_target_pairs={{0,1},{1,0},{2,3},{3,2},{4,5},{5,4},{6,7},{7,6},{8,9},{9,8},{10,11... | collective-permute-start | bytes 3145736 | tf_op jit(solution)/shard_map/ppermute | solution.py:16
  144.1 25.4 %collective-permute-start.16 = (bf16[1024,256]{1,0:T(8,128)(2,1)S(1)}, bf16[1024,256]{1,0:T(8,128)(2,1)}, u32[]{:S(2)}, u32[]{:S(2)}) collective-permute-start(bf16[1024,256]{1,0:T(8,128)(2,1)S(1)} %collective-permute-done.14.refs_6_), channel_id=1, source_target_pairs={{0,1},{1,0},{2,3},{3,2},{4,5},{5,4},{6,7},{7,6},{8,9},{9,8},{10,11... | collective-permute-start | bytes 1572872 | tf_op jit(solution)/shard_map/ppermute | solution.py:16
  144.5 24.9 %collective-permute-start.17 = (bf16[1024,256]{1,0:T(8,128)(2,1)}, bf16[1024,256]{1,0:T(8,128)(2,1)S(1)}, u32[]{:S(2)}, u32[]{:S(2)}) collective-permute-start(bf16[1024,256]{1,0:T(8,128)(2,1)} %collective-permute-done.15.refs_7_), channel_id=1, source_target_pairs={{0,1},{1,0},{2,3},{3,2},{4,5},{5,4},{6,7},{7,6},{8,9},{9,8},{10,11... | collective-permute-start | bytes 1572872 | tf_op jit(solution)/shard_map/ppermute | solution.py:16
  159.7 104.0 %all-gather.10.cloned.1.call-start = ((), (), s32[]{:S(2)}) async-start(), calls=%async_computation.10 | async-start | bytes 3604480 | tf_op jit(solution)/shard_map/all_gather | solution.py:834
  181.4 23.2 %collective-permute-start.26 = (bf16[256,2048]{1,0:T(8,128)(2,1)}, bf16[256,2048]{1,0:T(8,128)(2,1)S(1)}, u32[]{:S(2)}, u32[]{:S(2)}) collective-permute-start(bf16[256,2048]{1,0:T(8,128)(2,1)} %get-tuple-element.169.refs_0_), channel_id=1, source_target_pairs={{0,4},{1,5},{2,6},{3,7},{4,0},{5,1},{6,2},{7,3},{8,12},{9,13},{10,... | collective-permute-start | bytes 3145736 | tf_op jit(solution)/shard_map/ppermute | solution.py:16
  182.0 23.8 %collective-permute-start.24 = (bf16[256,2048]{1,0:T(8,128)(2,1)}, bf16[256,2048]{1,0:T(8,128)(2,1)S(1)}, u32[]{:S(2)}, u32[]{:S(2)}) collective-permute-start(bf16[256,2048]{1,0:T(8,128)(2,1)} %get-tuple-element.169.refs_0_), channel_id=1, source_target_pairs={{0,2},{1,3},{2,0},{3,1},{4,6},{5,7},{6,4},{7,5},{8,10},{9,11},{10,... | collective-permute-start | bytes 3145736 | tf_op jit(solution)/shard_map/ppermute | solution.py:16
  182.6 23.3 %collective-permute-start.32 = (bf16[256,2048]{1,0:T(8,128)(2,1)}, bf16[256,2048]{1,0:T(8,128)(2,1)}, u32[]{:S(2)}, u32[]{:S(2)}) collective-permute-start(bf16[256,2048]{1,0:T(8,128)(2,1)} %collective-permute-done.1.refs_12_), channel_id=1, source_target_pairs={{0,1},{1,0},{2,3},{3,2},{4,5},{5,4},{6,7},{7,6},{8,9},{9,8},{10,11... | collective-permute-start | bytes 3145736 | tf_op jit(solution)/shard_map/ppermute | solution.py:16
  182.6 23.9 %collective-permute-start.33 = (bf16[256,2048]{1,0:T(8,128)(2,1)}, bf16[256,2048]{1,0:T(8,128)(2,1)}, u32[]{:S(2)}, u32[]{:S(2)}) collective-permute-start(bf16[256,2048]{1,0:T(8,128)(2,1)} %collective-permute-done.2.refs_14_), channel_id=1, source_target_pairs={{0,1},{1,0},{2,3},{3,2},{4,5},{5,4},{6,7},{7,6},{8,9},{9,8},{10,11... | collective-permute-start | bytes 3145736 | tf_op jit(solution)/shard_map/ppermute | solution.py:16
  183.1 197.7 %reduce-scatter.5.cloned.1.call-start = ((), (), s32[]{:S(2)}) async-start(), calls=%async_computation.11 | async-start | bytes 3604480 | tf_op jit(solution)/shard_map/reduce_scatter | solution.py:904
  183.4 23.2 %collective-permute-start.34 = (bf16[128,2048]{1,0:T(8,128)(2,1)}, bf16[128,2048]{1,0:T(8,128)(2,1)S(1)}, u32[]{:S(2)}, u32[]{:S(2)}) collective-permute-start(bf16[128,2048]{1,0:T(8,128)(2,1)} %copy-done.56), channel_id=1, source_target_pairs={{0,1},{1,0},{2,3},{3,2},{4,5},{5,4},{6,7},{7,6},{8,9},{9,8},{10,11... | collective-permute-start | bytes 1572872 | tf_op jit(solution)/shard_map/ppermute | solution.py:16
  222.5 29.7 %collective-permute-start.36 = (bf16[256,2048]{1,0:T(8,128)(2,1)}, bf16[256,2048]{1,0:T(8,128)(2,1)S(1)}, u32[]{:S(2)}, u32[]{:S(2)}) collective-permute-start(bf16[256,2048]{1,0:T(8,128)(2,1)} %get-tuple-element.173.refs_0_), channel_id=1, source_target_pairs={{0,1},{1,0},{2,3},{3,2},{4,5},{5,4},{6,7},{7,6},{8,9},{9,8},{10,11... | collective-permute-start | bytes 3145736 | tf_op jit(solution)/shard_map/ppermute | solution.py:16
  223.0 29.2 %collective-permute-start.37 = (bf16[256,2048]{1,0:T(8,128)(2,1)}, bf16[256,2048]{1,0:T(8,128)(2,1)}, u32[]{:S(2)}, u32[]{:S(2)}) collective-permute-start(bf16[256,2048]{1,0:T(8,128)(2,1)} %get-tuple-element.173.refs_0_), channel_id=1, source_target_pairs={{0,2},{1,3},{2,0},{3,1},{4,6},{5,7},{6,4},{7,5},{8,10},{9,11},{10,... | collective-permute-start | bytes 3145736 | tf_op jit(solution)/shard_map/ppermute | solution.py:16
  225.2 27.1 %collective-permute-start.38 = (bf16[256,2048]{1,0:T(8,128)(2,1)}, bf16[256,2048]{1,0:T(8,128)(2,1)}, u32[]{:S(2)}, u32[]{:S(2)}) collective-permute-start(bf16[256,2048]{1,0:T(8,128)(2,1)} %get-tuple-element.173.refs_0_), channel_id=1, source_target_pairs={{0,4},{1,5},{2,6},{3,7},{4,0},{5,1},{6,2},{7,3},{8,12},{9,13},{10,... | collective-permute-start | bytes 3145736 | tf_op jit(solution)/shard_map/ppermute | solution.py:16
  306.5 210.3 %reduce-scatter.9.cloned.1.call-start = ((), (), s32[]{:S(2)}) async-start(), calls=%async_computation.13 | async-start | bytes 7208960 | tf_op jit(solution)/shard_map/reduce_scatter | solution.py:904
  312.6 25.9 %collective-permute-start.40 = (bf16[2,128,2048]{2,1,0:T(8,128)(2,1)S(1)}, bf16[2,128,2048]{2,1,0:T(8,128)(2,1)}, u32[]{:S(2)}, u32[]{:S(2)}) collective-permute-start(bf16[2,128,2048]{2,1,0:T(8,128)(2,1)S(1)} %get-tuple-element.189), channel_id=1, source_target_pairs={{0,2},{1,3},{2,0},{3,1},{4,6},{5,7},{6,4},{7,5},{8,10},{9,11},{10,... | collective-permute-start | bytes 3145736 | tf_op jit(solution)/shard_map/ppermute | solution.py:16
  314.0 25.5 %collective-permute-start.41 = (bf16[2,128,2048]{2,1,0:T(8,128)(2,1)S(1)}, bf16[2,128,2048]{2,1,0:T(8,128)(2,1)}, u32[]{:S(2)}, u32[]{:S(2)}) collective-permute-start(bf16[2,128,2048]{2,1,0:T(8,128)(2,1)S(1)} %get-tuple-element.190), channel_id=1, source_target_pairs={{0,4},{1,5},{2,6},{3,7},{4,0},{5,1},{6,2},{7,3},{8,12},{9,13},{10,... | collective-permute-start | bytes 3145736 | tf_op jit(solution)/shard_map/ppermute | solution.py:16
  387.2 38.0 %collective-permute-start.45 = (bf16[128,2048]{1,0:T(8,128)(2,1)S(1)}, bf16[128,2048]{1,0:T(8,128)(2,1)S(1)}, u32[]{:S(2)}, u32[]{:S(2)}) collective-permute-start(bf16[128,2048]{1,0:T(8,128)(2,1)S(1)} %slice.319), channel_id=1, source_target_pairs={{0,2},{1,3},{2,0},{3,1},{4,6},{5,7},{6,4},{7,5},{8,10},{9,11},{10,... | collective-permute-start | bytes 1572872 | tf_op jit(solution)/shard_map/ppermute | solution.py:16
  388.8 36.3 %collective-permute-start.46 = (bf16[128,2048]{1,0:T(8,128)(2,1)S(1)}, bf16[128,2048]{1,0:T(8,128)(2,1)S(1)}, u32[]{:S(2)}, u32[]{:S(2)}) collective-permute-start(bf16[128,2048]{1,0:T(8,128)(2,1)S(1)} %slice.320), channel_id=1, source_target_pairs={{0,4},{1,5},{2,6},{3,7},{4,0},{5,1},{6,2},{7,3},{8,12},{9,13},{10,... | collective-permute-start | bytes 1572872 | tf_op jit(solution)/shard_map/ppermute | solution.py:16
  389.6 32.9 %collective-permute-start.47 = (bf16[2,128,2048]{2,1,0:T(8,128)(2,1)S(1)}, bf16[2,128,2048]{2,1,0:T(8,128)(2,1)S(1)}, u32[]{:S(2)}, u32[]{:S(2)}) collective-permute-start(bf16[2,128,2048]{2,1,0:T(8,128)(2,1)S(1)} %copy-done.16), channel_id=1, source_target_pairs={{0,2},{1,3},{2,0},{3,1},{4,6},{5,7},{6,4},{7,5},{8,10},{9,11},{10,... | collective-permute-start | bytes 3145736 | tf_op jit(solution)/shard_map/ppermute | solution.py:16
  391.0 34.2 %collective-permute-start.48 = (bf16[2,128,2048]{2,1,0:T(8,128)(2,1)S(1)}, bf16[2,128,2048]{2,1,0:T(8,128)(2,1)}, u32[]{:S(2)}, u32[]{:S(2)}) collective-permute-start(bf16[2,128,2048]{2,1,0:T(8,128)(2,1)S(1)} %get-tuple-element.222), channel_id=1, source_target_pairs={{0,4},{1,5},{2,6},{3,7},{4,0},{5,1},{6,2},{7,3},{8,12},{9,13},{10,... | collective-permute-start | bytes 3145736 | tf_op jit(solution)/shard_map/ppermute | solution.py:16
  439.1 30.1 %collective-permute-start.49 = (bf16[4,256,2048]{2,1,0:T(8,128)(2,1)}, bf16[4,256,2048]{2,1,0:T(8,128)(2,1)}, u32[]{:S(2)}, u32[]{:S(2)}) collective-permute-start(bf16[4,256,2048]{2,1,0:T(8,128)(2,1)} %get-tuple-element.229), channel_id=1, source_target_pairs={{0,1},{1,0},{2,3},{3,2},{4,5},{5,4},{6,7},{7,6},{8,9},{9,8},{10,11... | collective-permute-start | bytes 12582920 | tf_op jit(solution)/shard_map/ppermute | solution.py:16
  440.4 28.8 %all-to-all-start.3 = ((bf16[8,256,256]{2,1,0:T(8,128)(2,1)}), bf16[8,256,256]{2,1,0:T(8,128)(2,1)S(1)}, u32[]{:S(2)}, u32[]{:S(2)}) async-start(bf16[8,256,256]{2,1,0:T(8,128)(2,1)} %get-tuple-element.233), calls=%async_computation.4 | async-start | bytes 2097152 | tf_op jit(solution)/shard_map/all_to_all | solution.py:112
  444.5 129.3 %reduce-scatter.7.cloned.1.call-start = ((), (), s32[]{:S(2)}) async-start(), calls=%async_computation.12 | async-start | bytes 3932160 | tf_op jit(solution)/shard_map/reduce_scatter | solution.py:904
  444.8 57.9 %collective-permute-start.60 = (bf16[256,2048]{1,0:T(8,128)(2,1)}, bf16[256,2048]{1,0:T(8,128)(2,1)}, u32[]{:S(2)}, u32[]{:S(2)}) collective-permute-start(bf16[256,2048]{1,0:T(8,128)(2,1)} %collective-permute-done.37.refs_2_), channel_id=1, source_target_pairs={{0,1},{1,0},{2,3},{3,2},{4,5},{5,4},{6,7},{7,6},{8,9},{9,8},{10,11... | collective-permute-start | bytes 3145736 | tf_op jit(solution)/shard_map/ppermute | solution.py:16
  447.3 56.0 %collective-permute-start.61 = (bf16[256,2048]{1,0:T(8,128)(2,1)}, bf16[256,2048]{1,0:T(8,128)(2,1)}, u32[]{:S(2)}, u32[]{:S(2)}) collective-permute-start(bf16[256,2048]{1,0:T(8,128)(2,1)} %collective-permute-done.38.refs_4_), channel_id=1, source_target_pairs={{0,1},{1,0},{2,3},{3,2},{4,5},{5,4},{6,7},{7,6},{8,9},{9,8},{10,11... | collective-permute-start | bytes 3145736 | tf_op jit(solution)/shard_map/ppermute | solution.py:16
  473.6 24.1 %collective-permute-start.53 = (bf16[2,128,2048]{2,1,0:T(8,128)(2,1)}, bf16[2,128,2048]{2,1,0:T(8,128)(2,1)S(1)}, u32[]{:S(2)}, u32[]{:S(2)}) collective-permute-start(bf16[2,128,2048]{2,1,0:T(8,128)(2,1)} %get-tuple-element.239), channel_id=1, source_target_pairs={{0,2},{1,3},{2,0},{3,1},{4,6},{5,7},{6,4},{7,5},{8,10},{9,11},{10,... | collective-permute-start | bytes 3145736 | tf_op jit(solution)/shard_map/ppermute | solution.py:16
  475.2 23.7 %collective-permute-start.54 = (bf16[2,128,2048]{2,1,0:T(8,128)(2,1)S(1)}, bf16[2,128,2048]{2,1,0:T(8,128)(2,1)S(1)}, u32[]{:S(2)}, u32[]{:S(2)}) collective-permute-start(bf16[2,128,2048]{2,1,0:T(8,128)(2,1)S(1)} %get-tuple-element.240), channel_id=1, source_target_pairs={{0,4},{1,5},{2,6},{3,7},{4,0},{5,1},{6,2},{7,3},{8,12},{9,13},{10,... | collective-permute-start | bytes 3145736 | tf_op jit(solution)/shard_map/ppermute | solution.py:16
  486.3 123.5 %reduce-scatter.11.cloned.1.call-start = ((), (), s32[]{:S(2)}) async-start(), calls=%async_computation.14 | async-start | bytes 1392640 | tf_op jit(solution)/shard_map/reduce_scatter | solution.py:904
  516.8 34.3 %collective-permute-start.58 = (bf16[512,1408]{1,0:T(8,128)(2,1)}, bf16[512,1408]{1,0:T(8,128)(2,1)}, u32[]{:S(2)}, u32[]{:S(2)}) collective-permute-start(bf16[512,1408]{1,0:T(8,128)(2,1)} %reduce-scatter.9.cloned.1.call-done.refs_0_), channel_id=1, source_target_pairs={{0,2},{1,3},{2,0},{3,1},{4,6},{5,7},{6,4},{7,5},{8,10},{9,11},{10,... | collective-permute-start | bytes 4325384 | tf_op jit(solution)/shard_map/ppermute | solution.py:16
  517.3 34.0 %collective-permute-start.59 = (bf16[512,1408]{1,0:T(8,128)(2,1)}, bf16[512,1408]{1,0:T(8,128)(2,1)}, u32[]{:S(2)}, u32[]{:S(2)}) collective-permute-start(bf16[512,1408]{1,0:T(8,128)(2,1)} %reduce-scatter.9.cloned.1.call-done.refs_0_), channel_id=1, source_target_pairs={{0,4},{1,5},{2,6},{3,7},{4,0},{5,1},{6,2},{7,3},{8,12},{9,13},{10,... | collective-permute-start | bytes 4325384 | tf_op jit(solution)/shard_map/ppermute | solution.py:16
  551.3 23.6 %collective-permute-start.66 = (bf16[512,1408]{1,0:T(8,128)(2,1)}, bf16[512,1408]{1,0:T(8,128)(2,1)S(1)}, u32[]{:S(2)}, u32[]{:S(2)}) collective-permute-start(bf16[512,1408]{1,0:T(8,128)(2,1)} %collective-permute-done.59.refs_4_), channel_id=1, source_target_pairs={{0,1},{1,0},{2,3},{3,2},{4,5},{5,4},{6,7},{7,6},{8,9},{9,8},{10,11... | collective-permute-start | bytes 4325384 | tf_op jit(solution)/shard_map/ppermute | solution.py:16
  552.5 21.9 %collective-permute-start.65 = (bf16[512,1408]{1,0:T(8,128)(2,1)}, bf16[512,1408]{1,0:T(8,128)(2,1)}, u32[]{:S(2)}, u32[]{:S(2)}) collective-permute-start(bf16[512,1408]{1,0:T(8,128)(2,1)} %collective-permute-done.58.refs_2_), channel_id=1, source_target_pairs={{0,1},{1,0},{2,3},{3,2},{4,5},{5,4},{6,7},{7,6},{8,9},{9,8},{10,11... | collective-permute-start | bytes 4325384 | tf_op jit(solution)/shard_map/ppermute | solution.py:16
  609.8 57.0 %collective-permute-start.89 = (bf16[176,2048]{1,0:T(8,128)(2,1)}, bf16[176,2048]{1,0:T(8,128)(2,1)}, u32[]{:S(2)}, u32[]{:S(2)}) collective-permute-start(bf16[176,2048]{1,0:T(8,128)(2,1)} %collective-permute-done.52.refs_4_), channel_id=1, source_target_pairs={{0,1},{1,0},{2,3},{3,2},{4,5},{5,4},{6,7},{7,6},{8,9},{9,8},{10,11... | collective-permute-start | bytes 2162696 | tf_op jit(solution)/shard_map/ppermute | solution.py:16
  609.8 40.0 %collective-permute-start.90 = (bf16[176,2048]{1,0:T(8,128)(2,1)}, bf16[176,2048]{1,0:T(8,128)(2,1)}, u32[]{:S(2)}, u32[]{:S(2)}) collective-permute-start(bf16[176,2048]{1,0:T(8,128)(2,1)} %collective-permute-done.52.refs_4_), channel_id=1, source_target_pairs={{0,2},{1,3},{2,0},{3,1},{4,6},{5,7},{6,4},{7,5},{8,10},{9,11},{10,... | collective-permute-start | bytes 2162696 | tf_op jit(solution)/shard_map/ppermute | solution.py:16
  611.4 28.4 %collective-permute-start.74 = (bf16[128,2048]{1,0:T(8,128)(2,1)S(1)}, bf16[128,2048]{1,0:T(8,128)(2,1)S(1)}, u32[]{:S(2)}, u32[]{:S(2)}) collective-permute-start(bf16[128,2048]{1,0:T(8,128)(2,1)S(1)} %get-tuple-element.278), channel_id=1, source_target_pairs={{0,2},{1,3},{2,0},{3,1},{4,6},{5,7},{6,4},{7,5},{8,10},{9,11},{10,... | collective-permute-start | bytes 1572872 | tf_op jit(solution)/shard_map/ppermute | solution.py:16
  611.9 29.4 %collective-permute-start.75 = (bf16[128,2048]{1,0:T(8,128)(2,1)S(1)}, bf16[128,2048]{1,0:T(8,128)(2,1)S(1)}, u32[]{:S(2)}, u32[]{:S(2)}) collective-permute-start(bf16[128,2048]{1,0:T(8,128)(2,1)S(1)} %get-tuple-element.279), channel_id=1, source_target_pairs={{0,4},{1,5},{2,6},{3,7},{4,0},{5,1},{6,2},{7,3},{8,12},{9,13},{10,... | collective-permute-start | bytes 1572872 | tf_op jit(solution)/shard_map/ppermute | solution.py:16
  612.5 33.5 %collective-permute-start.77 = (bf16[544,256]{1,0:T(8,128)(2,1)}, bf16[544,256]{1,0:T(8,128)(2,1)S(1)}, u32[]{:S(2)}, u32[]{:S(2)}) collective-permute-start(bf16[544,256]{1,0:T(8,128)(2,1)} %reduce-scatter.11.cloned.1.call-done.refs_0_), channel_id=1, source_target_pairs={{0,1},{1,0},{2,3},{3,2},{4,5},{5,4},{6,7},{7,6},{8,9},{9,8},{10,11... | collective-permute-start | bytes 835592 | tf_op jit(solution)/shard_map/ppermute | solution.py:16
  (125 other events, 1241.2 us)
Sparse Core Ops, SparseCore 0:
  11.9 85.4 all-gather.5
  99.6 104.9 all-gather.7
  206.1 57.4 all-gather.9
  306.6 54.9 reduce-scatter.4
  366.6 100.5 reduce-scatter.8
  486.5 57.7 reduce-scatter.6
  574.4 25.7 reduce-scatter.10
